TPU v7x, 32 devices: a whole 2x2x4 slice. The times are simulated.
32 devices in a mesh: face: 4 (over y, x), tile: 8 (over z, core).
Axes of the slice: x: 2, y: 2, z: 4, core: 2. Of those that a mesh axis runs over, the one named last changes fastest.
Arguments:
- atmos_state: bfloat16 [128, 512, 1024], P(None, 'face', 'tile'), may hold values from -6 to 6
- ocean_state: bfloat16 [64, 512, 1024], P(None, 'face', 'tile'), may hold values from -6 to 6
- land_mask: int32 [512, 32], P('face', 'tile'), may hold values 0 or 1
- face_turns: int32 [4, 8], P('face', 'tile'), may hold values from 0 to 3
- block_target: int32 [4096, 1], P(('face', 'tile')), may hold values from 0 to 31; in each aligned block of 128 rows (0 to 127, 128 to 255, ...) at most 8 rows name the same one
- block_patch: int32 [4096, 1], P(('face', 'tile')), may hold values from 0 to 127
- block_weight: float32 [4096, 1], P(('face', 'tile')), may hold values from 0.25 to 1
- atmos_w1: bfloat16 [9, 128, 144], replicated, may hold values from -0.15625 to 0.15625
- atmos_w2: bfloat16 [9, 128, 128], replicated, may hold values from -0.1875 to 0.1875
- ocean_w1: bfloat16 [9, 64, 80], replicated, may hold values from -0.21875 to 0.21875
- ocean_w2: bfloat16 [9, 64, 64], replicated, may hold values from -0.25 to 0.25
Outputs:
- atmos_out: bfloat16 [128, 512, 1024], P(None, 'face', 'tile')
- ocean_out: bfloat16 [64, 512, 1024], P(None, 'face', 'tile')
Inputs may be any that keep to these rules, and one draw needn't show every extreme that they name: `block_target`: among the 128 blocks of one device, at most 8 have the same target, and in every draw some device has exactly 8 blocks with one target.
All inputs are finite; a program needn't handle non-finite values. No bound on the sum of `land_mask` on one device may be relied on, other than what follows from the above.
Results may differ from a plain program's by a relative error of at most 0.001.
The roundings to bfloat16 on the way count: a program that leaves them out, or rounds other values in their place, can miss the bound.
Values may be sent and summed in bfloat16 or wider, within the bound.
No kernel may reach another device: no remote copies, remote signals or barrier semaphores. Data moves between devices by JAX's collectives and lax.ppermute only.
A program may use at most 192 MiB of HBM per device.

v0:
```python
from functools import partial

import jax
import jax.numpy as jnp
import numpy as np
from jax import lax
from jax.experimental import pallas as pl
from jax.experimental.pallas import tpu as pltpu
from jax.sharding import PartitionSpec as P

CS = 16
CF = 16
RUN = 32
F32 = jnp.float32
BF16 = jnp.bfloat16
VM = pl.BlockSpec(memory_space=pltpu.VMEM)
SM = pl.BlockSpec(memory_space=pltpu.SMEM)
SMALL = pltpu.CompilerParams(vmem_limit_bytes=16 << 20)


def iota(shape, axis):
    return lax.broadcasted_iota(jnp.int32, shape, axis)


def dot(a, b, dims=((1,), (0,))):
    return lax.dot_general(a, b, (dims, ((), ())), preferred_element_type=F32)


def reverser(size, flip):
    rows, cols = iota((size, size), 0), iota((size, size), 1)
    wanted = jnp.where(flip, size - 1 - rows, rows)
    return jnp.where(cols == wanted, 1.0, 0.0).astype(BF16)


def cell_mask(land, cols):
    runs, rows = land.shape
    parts = [
        jnp.broadcast_to(land[run : run + 1, :].astype(F32), (cols // runs, rows))
        for run in range(runs)
    ]
    return jnp.concatenate(parts, axis=0).T


def across(row):
    return jnp.broadcast_to(row.astype(F32), (row.shape[1],) * 2)


def pack_kernel(capacity, surface, land, target, weight, patch, out):
    rows, cols = surface.shape[1], surface.shape[2]
    slots = out.shape[0]
    first, second = iota((rows, rows), 0), iota((rows, rows), 1)
    targets = across(target[...])
    same = (targets.T == targets) & (first < second)
    rank = jnp.sum(jnp.where(same, 1.0, 0.0), axis=0, keepdims=True)
    slot = (targets[0:1, :] * capacity + rank).astype(jnp.int32)
    packer = jnp.where(iota((slots, rows), 0) == slot, 1.0, 0.0).astype(BF16)
    mask = cell_mask(land[...], cols).astype(BF16)
    for c in range(CS):
        out[:, c * cols : (c + 1) * cols] = dot(packer, surface[c] * mask).astype(BF16)
    lanes = iota((rows, rows), 1)
    described = jnp.where(
        lanes == 0, across(weight[...]).T, jnp.where(lanes == 1, across(patch[...]).T, 0.0)
    )
    out[:, CS * cols :] = dot(packer, described.astype(BF16)).astype(BF16)


def common_kernel(turn, surface, out):
    side = surface.shape[1]
    k = turn[0, 0]
    flip_rows = reverser(side, k >= 2)
    flip_cols = reverser(side, (k == 1) | (k == 2))
    odd = (k % 2) == 1
    for c in range(CF):
        tile = surface[c].astype(F32)
        tile = jnp.where(odd, tile.T, tile).astype(BF16)
        tile = dot(tile, flip_cols).astype(BF16)
        out[:, c * side : (c + 1) * side] = dot(flip_rows, tile).astype(BF16)


def return_kernel(meta, rows, out):
    slots, side = meta.shape
    patch = meta[:, 1:2].astype(F32).astype(jnp.int32)
    select = jnp.where(iota((slots, side), 1) == patch, 1.0, 0.0).astype(BF16)
    for c in range(CF):
        part = slice(c * side, (c + 1) * side)
        out[:, part] = dot(select, rows[:, part]).astype(BF16)


def turn_edges(k, edges, size):
    width = edges[0].shape[1]
    rows, cols = iota((width, width), 0), iota((width, width), 1)
    flip = jnp.where(rows + cols == size - 1, 1.0, 0.0).astype(BF16)
    top, bottom, left, right = edges
    top_r, bottom_r, left_r, right_r = [dot(value.astype(BF16), flip) for value in edges]

    def chosen(*options):
        value = options[3]
        for number in range(3):
            value = jnp.where(k == number, options[number], value)
        return value

    return (
        chosen(top, left_r, bottom_r, right),
        chosen(bottom, right_r, top_r, left),
        chosen(left, bottom, right_r, top_r),
        chosen(right, top, left_r, bottom_r),
    )


def column_edges(ref):
    count, channels, cols = ref.shape
    lanes = iota((channels, count), 1)

    def step(y, carry):
        row = ref[y].astype(F32)
        return (
            jnp.where(lanes == y, row[:, 0:1], carry[0]),
            jnp.where(lanes == y, row[:, cols - 1 :], carry[1]),
        )

    zero = jnp.zeros((channels, count), F32)
    return lax.fori_loop(0, count, step, (zero, zero), unroll=16)


def all_edges(ref):
    last = ref.shape[0] - 1
    return (ref[0].astype(F32), ref[last].astype(F32), *column_edges(ref))


def early_kernel(turn, state, ocean, *outs):
    atmos = turn_edges(turn[0, 0], all_edges(state), state.shape[2])
    sea = all_edges(ocean)
    for out, above, below in zip(outs, atmos, sea):
        out[...] = jnp.concatenate([above, below], axis=0).astype(BF16)


def sea_kernel(turn, incoming, out, *edges):
    side = out.shape[0]
    slots = incoming.shape[0]
    k = turn[0, 0]
    flip_x = reverser(side, (k == 1) | (k == 2))
    meta = incoming[:, CS * side :].astype(F32)

    def placed(patch):
        patch = patch.astype(jnp.int32)
        return jnp.where(k >= 2, side - 1 - patch, patch)

    @pl.when((k % 2) == 0)
    def _():
        turned = meta.T
        spread = jnp.where(
            iota((side, slots), 0) == placed(turned[1:2, :]), turned[0:1, :], 0.0
        )
        scale = jnp.maximum(jnp.sum(spread, axis=1, keepdims=True), 1.0)
        spread = spread.astype(BF16)
        for c in range(CS):
            part = dot(incoming[:, c * side : (c + 1) * side], flip_x).astype(BF16)
            value = dot(spread, part) / scale
            out[:, c, :] = value.astype(BF16).astype(F32)

    @pl.when((k % 2) == 1)
    def _():
        spread = jnp.where(
            iota((slots, side), 1) == placed(meta[:, 1:2]), meta[:, 0:1], 0.0
        )
        scale = jnp.maximum(jnp.sum(spread, axis=0, keepdims=True), 1.0)
        spread = spread.astype(BF16)
        for c in range(CS):
            part = dot(incoming[:, c * side : (c + 1) * side], flip_x)
            value = dot(part.T.astype(BF16), spread) / scale
            out[:, c, :] = value.astype(BF16).astype(F32)

    for edge, value in zip(edges, turn_edges(k, all_edges(out), side)):
        edge[...] = value.astype(BF16)


def force_kernel(capacity, target, returned, out, *edges):
    rows, cols = out.shape[0], out.shape[2]
    slots = returned.shape[0]
    first, second = iota((rows, rows), 0), iota((rows, rows), 1)
    targets = across(target[...])
    same = (targets.T == targets) & (second < first)
    rank = jnp.sum(jnp.where(same, 1.0, 0.0), axis=1, keepdims=True)
    slot = (targets.T[:, 0:1] * capacity + rank).astype(jnp.int32)
    pick = jnp.where(iota((rows, slots), 1) == slot, 1.0, 0.0).astype(BF16)
    for c in range(CF):
        out[:, c, :] = dot(pick, returned[:, c * cols : (c + 1) * cols])
    for edge, value in zip(edges, all_edges(out)):
        edge[...] = value.astype(BF16)


def widened(value):
    return jnp.concatenate([value, jnp.zeros_like(value)], axis=1)


def framed(before, value, after):
    cols = value.shape[1]
    lanes = iota((value.shape[0], 2 * cols), 1)
    moved = pltpu.roll(widened(value), 1, 1)
    return jnp.where(lanes == 0, before, jnp.where(lanes == cols + 1, after, moved))


def side_kernel(start, place, above, below, fold, left, right, *outs):
    to_left, to_right, above_out, below_out = outs
    over, under = above[...].astype(F32), below[...].astype(F32)
    if fold is not None:
        channels, cols = over.shape
        ocean = iota((channels, cols), 0) >= start
        over = jnp.where(ocean & (place[0] == 0), 0.0, over)
        flip = reverser(cols, True)
        back = dot(fold[...], flip)
        if start:
            back = jnp.concatenate([jnp.zeros((start, cols), F32), back], axis=0)
        under = jnp.where(ocean & (place[0] == 1), back, under)
    above_out[...] = over.astype(BF16)
    below_out[...] = under.astype(BF16)
    cols = over.shape[1]
    to_left[...] = framed(over[:, :1], left[...].astype(F32), under[:, :1]).astype(BF16)
    to_right[...] = framed(
        over[:, cols - 1 :], right[...].astype(F32), under[:, cols - 1 :]
    ).astype(BF16)


def halo_kernel(spans, turned, turn, *refs):
    ends, left, right = refs[-3:]
    pieces = []
    for number, (low, high) in enumerate(spans):
        above, below, from_left, from_right = [
            ref[low:high, :].astype(F32) for ref in refs[4 * number : 4 * number + 4]
        ]
        last = above.shape[1] + 1
        pieces.append(
            (
                framed(from_left[:, :1], above, from_right[:, :1]),
                framed(from_left[:, last : last + 1], below, from_right[:, last : last + 1]),
                from_left,
                from_right,
            )
        )
    halo = [jnp.concatenate(part, axis=0) if len(part) > 1 else part[0] for part in zip(*pieces)]
    if turned:
        halo = turn_edges(lax.rem(4 - turn[0, 0], 4), halo, left.shape[1] + 2)
    ends[0], ends[1] = halo[0], halo[1]
    cols = left.shape[1]
    width = 2 * cols
    left[...] = pltpu.roll(halo[2], width - 1, 1)[:, :cols]
    right[...] = pltpu.roll(halo[3], width - 1, 1)[:, :cols]


def conv_kernel(parts, mode, *refs):
    refs = list(refs)
    turn = refs.pop(0)
    sources = [refs.pop(0) for _ in range(parts)]
    ends, left, right, taps = [refs.pop(0) for _ in range(4)]
    base = refs.pop(0) if mode in ("add", "masked") else None
    mask = refs.pop(0) if mode == "masked" else None
    out = refs.pop(0)
    gelu = mode in ("turned", "plain")
    edges = [refs.pop(0) for _ in range(4)] if gelu else None
    stacked, sums, early, late = refs[:4]
    edge_left, edge_right = refs[4:] if gelu else (None, None)
    rows, outputs, cols = out.shape
    channels = ends.shape[1]
    lanes = iota((channels, cols), 1)
    out_lanes = iota((outputs, cols), 1)

    def place(slot, half, shifted):
        for b, value in enumerate(shifted):
            stacked[slot, b * channels : (b + 1) * channels, half * cols : (half + 1) * cols] = (
                value.astype(BF16)
            )

    def inner(slot, half, y):
        row = [source[y].astype(F32) for source in sources]
        row = row[0] if parts == 1 else jnp.concatenate(row, axis=0)
        before = pltpu.roll(left[...], lax.rem(cols - y, cols), 1)
        after = pltpu.roll(right[...], cols - 1 - y, 1)
        place(
            slot,
            half,
            (
                jnp.where(lanes == 0, before, pltpu.roll(row, 1, 1)),
                row,
                jnp.where(lanes == cols - 1, after, pltpu.roll(row, cols - 1, 1)),
            ),
        )

    def end(slot, half, which):
        row = ends[which]
        place(slot, half, [row[:, b : b + cols] for b in range(3)])

    def emit(y, value):
        if gelu:
            value = jax.nn.gelu(value, approximate=True).astype(BF16)
            out[y] = value
            value = value.astype(F32)
            edge_left[...] = jnp.where(out_lanes == y, value[:, 0:1], edge_left[...])
            edge_right[...] = jnp.where(out_lanes == y, value[:, cols - 1 :], edge_right[...])
        else:
            value = base[y].astype(F32) + value
            if mode == "masked":
                value = value * mask[y]
            out[y] = value.astype(BF16)

    def product(slot):
        sums[slot] = dot(taps[...], stacked[slot])

    def tap(slot, a, half):
        return sums[slot, a * outputs : (a + 1) * outputs, half * cols : (half + 1) * cols]

    def carry(slot):
        early[...] = tap(slot, 0, 0) + tap(slot, 1, 1)
        late[...] = tap(slot, 0, 1)

    def finish(slot, j):
        emit(2 * j - 2, early[...] + tap(slot, 2, 0))
        emit(2 * j - 1, late[...] + tap(slot, 1, 0) + tap(slot, 2, 1))
        carry(slot)

    def load(slot, j):
        inner(slot, 0, 2 * j - 1)
        inner(slot, 1, 2 * j)

    spare = stacked.shape[1] - 3 * channels
    if spare:
        stacked[:, 3 * channels :, :] = jnp.zeros((stacked.shape[0], spare, 2 * cols), BF16)
    if gelu:
        edge_left[...] = jnp.zeros(edge_left.shape, F32)
        edge_right[...] = jnp.zeros(edge_right.shape, F32)
    pairs = rows // 2
    end(0, 0, 0)
    inner(0, 1, 0)
    product(0)
    load(1, 1)
    carry(0)
    product(1)
    load(0, 2)

    def step(i, _):
        j = 2 * i + 2
        product(0)
        finish(1, j - 1)
        load(1, j + 1)
        product(1)
        finish(0, j)
        load(0, j + 2)
        return 0

    lax.fori_loop(0, pairs // 2 - 2, step, 0)
    product(0)
    finish(1, pairs - 3)
    load(1, pairs - 1)
    product(1)
    finish(0, pairs - 2)
    inner(0, 0, rows - 1)
    end(0, 1, 1)
    product(0)
    finish(1, pairs - 1)
    finish(0, pairs)
    if gelu:
        found = (
            out[0].astype(F32),
            out[rows - 1].astype(F32),
            edge_left[...],
            edge_right[...],
        )
        if mode == "turned":
            found = turn_edges(turn[0, 0], found, cols)
        for edge, value in zip(edges, found):
            edge[...] = value.astype(BF16)


def convolve(turn, sources, halo, taps, mode, base=None, mask=None):
    rows, _, cols = sources[0].shape
    outputs = taps.shape[0] // 3
    operands = [turn, *sources, *halo, taps]
    operands += [value for value in (base, mask) if value is not None]
    shapes = [jax.ShapeDtypeStruct((rows, outputs, cols), BF16)]
    scratch = [
        pltpu.VMEM((2, taps.shape[1], 2 * cols), BF16),
        pltpu.VMEM((2, taps.shape[0], 2 * cols), F32),
        pltpu.VMEM((outputs, cols), F32),
        pltpu.VMEM((outputs, cols), F32),
    ]
    if base is None:
        shapes += [jax.ShapeDtypeStruct((outputs, cols), BF16)] * 4
        scratch += [pltpu.VMEM((outputs, cols), F32)] * 2
    result = pl.pallas_call(
        partial(conv_kernel, len(sources), mode),
        out_shape=shapes,
        in_specs=[SM] + [VM] * (len(operands) - 1),
        out_specs=[VM] * len(shapes),
        scratch_shapes=scratch,
        compiler_params=SMALL,
    )(*operands)
    return (result[0], result[1:]) if base is None else result[0]


def shifted(value, axis, distance):
    count = lax.axis_size(axis)
    return lax.ppermute(value, axis, [(i, (i + distance) % count) for i in range(count)])


def exchanged(edges, place, start=None):
    top, bottom, left, right = edges
    channels, cols = top.shape
    above = shifted(bottom, "face", 1)
    below = shifted(top, "face", -1)
    operands = [above, below]
    if start is not None:
        faces, tiles = lax.axis_size("face"), lax.axis_size("tile")
        north = (faces - 1) * tiles
        operands.append(
            lax.ppermute(
                bottom[start:],
                ("face", "tile"),
                [(north + t, north + tiles - 1 - t) for t in range(tiles)],
            )
        )
    operands += [left, right]
    kernel = partial(side_kernel, start)
    if start is None:

        def kernel(place, above, below, left, right, *outs):
            side_kernel(None, place, above, below, None, left, right, *outs)

    to_left, to_right, above, below = pl.pallas_call(
        kernel,
        out_shape=[jax.ShapeDtypeStruct((channels, 2 * cols), BF16)] * 2
        + [jax.ShapeDtypeStruct((channels, cols), BF16)] * 2,
        in_specs=[SM] + [VM] * len(operands),
        out_specs=[VM] * 4,
        compiler_params=SMALL,
    )(place, *operands)
    return above, below, shifted(to_right, "tile", 1), shifted(to_left, "tile", -1)


def halo_of(turn, spans, turned, *pieces):
    channels = sum(high - low for low, high in spans)
    cols = pieces[0][0].shape[1]
    operands = [value for piece in pieces for value in piece]
    return pl.pallas_call(
        partial(halo_kernel, spans, turned),
        out_shape=[jax.ShapeDtypeStruct((2, channels, 2 * cols), F32)]
        + [jax.ShapeDtypeStruct((channels, cols), F32)] * 2,
        in_specs=[SM] + [VM] * len(operands),
        out_specs=[VM] * 3,
        compiler_params=SMALL,
    )(turn, *operands)


def stack_taps(weight):
    _, outputs, channels = weight.shape
    taps = weight.reshape(3, 3, outputs, channels).transpose(0, 2, 1, 3)
    taps = taps.reshape(3 * outputs, 3 * channels)
    return jnp.pad(taps, ((0, 0), (0, -taps.shape[1] % 128)))


def on_device(
    atmos_state,
    ocean_state,
    land_mask,
    face_turns,
    block_target,
    block_patch,
    block_weight,
    atmos_w1,
    atmos_w2,
    ocean_w1,
    ocean_w2,
):
    state_channels, side = atmos_state.shape[0], atmos_state.shape[2]
    ocean_channels, rows, cols = ocean_state.shape
    devices = lax.axis_size(("face", "tile"))
    capacity = max(2, 2 * rows // devices)
    slots = devices * capacity
    axes = ("face", "tile")
    face = lax.axis_index("face")
    place = jnp.where(face == 0, 0, jnp.where(face == lax.axis_size("face") - 1, 1, 2))
    place = place.astype(jnp.int32).reshape(1)

    def surface_spec(values, channels):
        return pl.BlockSpec((channels, *values.shape[1:]), lambda i: (0, 0, 0))

    def whole(values):
        return pl.BlockSpec(values.shape, lambda i: (0,) * values.ndim)

    def edge_shapes(channels):
        return [jax.ShapeDtypeStruct((channels, cols), BF16)] * 4

    target = block_target.reshape(1, rows)
    small = (land_mask.T, target, block_weight.reshape(1, rows), block_patch.reshape(1, rows))
    payload = pl.pallas_call(
        partial(pack_kernel, capacity),
        grid=(1,),
        out_shape=jax.ShapeDtypeStruct((slots, (CS + 1) * cols), BF16),
        in_specs=[surface_spec(ocean_state, CS)] + [whole(values) for values in small],
        out_specs=VM,
        compiler_params=SMALL,
    )(ocean_state, *small)
    incoming = lax.all_to_all(payload, axes, split_axis=0, concat_axis=0, tiled=True)

    state = atmos_state.transpose(1, 0, 2)
    mask = jnp.repeat(land_mask, RUN, axis=1).astype(BF16)
    ocean = (ocean_state * mask[None]).transpose(1, 0, 2)
    early = pl.pallas_call(
        early_kernel,
        out_shape=edge_shapes(state_channels + ocean_channels),
        in_specs=[SM, VM, VM],
        out_specs=[VM] * 4,
        compiler_params=SMALL,
    )(face_turns, state, ocean)
    early_halo = exchanged(early, place, state_channels)

    turned_taps = jnp.asarray(
        np.stack([np.rot90(np.arange(9).reshape(3, 3), number).ravel() for number in range(4)])
    )[face_turns[0, 0]]
    taps1 = stack_taps(atmos_w1[turned_taps])
    taps2 = stack_taps(atmos_w2[turned_taps])
    ocean_taps1, ocean_taps2 = stack_taps(ocean_w1), stack_taps(ocean_w2)
    common_rows = pl.pallas_call(
        common_kernel,
        grid=(1,),
        out_shape=jax.ShapeDtypeStruct((side, CF * side), BF16),
        in_specs=[SM, surface_spec(atmos_state, CF)],
        out_specs=VM,
        compiler_params=SMALL,
    )(face_turns, atmos_state)
    incoming, state, ocean, early_halo, common_rows, taps1, taps2, ocean_taps1, ocean_taps2 = (
        lax.optimization_barrier(
            (
                incoming,
                state,
                ocean,
                early_halo,
                common_rows,
                taps1,
                taps2,
                ocean_taps1,
                ocean_taps2,
            )
        )
    )
    answer = pl.pallas_call(
        return_kernel,
        grid=(1,),
        out_shape=jax.ShapeDtypeStruct((slots, CF * side), BF16),
        in_specs=[pl.BlockSpec((slots, side), lambda i: (0, CS)), VM],
        out_specs=VM,
        compiler_params=SMALL,
    )(incoming, common_rows)
    incoming, answer = lax.optimization_barrier((incoming, answer))
    returned = lax.all_to_all(answer, axes, split_axis=0, concat_axis=0, tiled=True)

    sea, *sea_edges = pl.pallas_call(
        sea_kernel,
        out_shape=[jax.ShapeDtypeStruct((side, CS, side), F32), *edge_shapes(CS)],
        in_specs=[SM, VM],
        out_specs=[VM] * 5,
        compiler_params=SMALL,
    )(face_turns, incoming)
    early_span = (0, state_channels)
    halo = halo_of(
        face_turns, [early_span, (0, CS)], True, early_halo, exchanged(sea_edges, place)
    )
    hidden, hidden_edges = convolve(face_turns, [state, sea], halo, taps1, "turned")
    halo = halo_of(face_turns, [early_span], True, exchanged(hidden_edges, place))
    atmos_out = convolve(face_turns, [hidden], halo, taps2, "add", base=state)

    forcing, *forcing_edges = pl.pallas_call(
        partial(force_kernel, capacity),
        out_shape=[jax.ShapeDtypeStruct((rows, CF, cols), F32), *edge_shapes(CF)],
        in_specs=[VM, VM],
        out_specs=[VM] * 5,
        compiler_params=SMALL,
    )(target, returned)
    early_span = (state_channels, state_channels + ocean_channels)
    halo = halo_of(
        face_turns, [early_span, (0, CF)], False, early_halo, exchanged(forcing_edges, place, 0)
    )
    hidden, hidden_edges = convolve(
        face_turns, [ocean, forcing], halo, ocean_taps1, "plain"
    )
    halo = halo_of(
        face_turns, [(0, ocean_channels)], False, exchanged(hidden_edges, place, 0)
    )
    ocean_out = convolve(
        face_turns,
        [hidden],
        halo,
        ocean_taps2,
        "masked",
        base=ocean,
        mask=mask.astype(F32)[:, None, :],
    )
    return atmos_out.transpose(1, 0, 2), ocean_out.transpose(1, 0, 2)


def solution(mesh):
    placed = (
        P(None, "face", "tile"),
        P(None, "face", "tile"),
        P("face", "tile"),
        P("face", "tile"),
        P(("face", "tile"), None),
        P(("face", "tile"), None),
        P(("face", "tile"), None),
        P(),
        P(),
        P(),
        P(),
    )
    return jax.shard_map(
        on_device,
        mesh=mesh,
        in_specs=placed,
        out_specs=(P(None, "face", "tile"), P(None, "face", "tile")),
        check_vma=False,
    )
```

profile of v0, /device:TPU:0, one launch (start us, length us, event | category | flops | bytes accessed | tf_op | source)
XLA Modules:
  0.0 218.7 jit_solution(6064347583378592124)
XLA Ops:
  0.7 1.6 copy-done.5
  6.5 7.3 %all-to-all-start = ((bf16[32,8,2176]{2,1,0:T(8,128)(2,1)}), bf16[32,8,2176]{2,1,0:T(8,128)(2,1)S(1)}, u32[]{:S(2)}, u32[]{:S(2)}) async-start(bf16[32,8,2176]{2,1,0:T(8,128)(2,1)} %bitcast.57), calls=%async_computation | async-start | bytes 2228224 | tf_op jit(solution)/shard_map/all_to_all | solution.py:501
  15.2 5.0 %copy.45 = bf16[128,128,128]{2,0,1:T(8,128)(2,1)S(1)} copy(bf16[128,128,128]{2,1,0:T(8,128)(2,1)} %surface.3) | data formatting | bytes 8388608 | tf_op args[0]
  22.3 6.0 %shard_map.132 = (bf16[192,128]{1,0:T(8,128)(2,1)}, bf16[192,128]{1,0:T(8,128)(2,1)}, bf16[192,128]{1,0:T(8,128)(2,1)S(1)}, bf16[192,128]{1,0:T(8,128)(2,1)S(1)}) custom-call(s32[1,1]{1,0:T(1,128)} %copy.50.turn.refs_0_, bf16[128,128,128]{2,1,0:T(8,128)(2,1)S(1)} %bitcast.50, bf16[128,64,128]{2,1,0:T(8,128)(2,1)S(1)} %fusion.ocean.refs_1_.refs_6_), custom_call_target="tpu_custom_call" | custom-call | tf_op jit(solution)/shard_map/pallas_call | solution.py:506
  29.5 1.8 collective-permute-start
  31.3 1.3 slice.3
  33.9 4.9 %collective-permute-start.1 = (bf16[192,128]{1,0:T(8,128)(2,1)}, bf16[192,128]{1,0:T(8,128)(2,1)}, u32[]{:S(2)}, u32[]{:S(2)}) collective-permute-start(bf16[192,128]{1,0:T(8,128)(2,1)} %get-tuple-element.73), channel_id=1, source_target_pairs={{0,24},{8,0},{16,8},{24,16},{1,25},{9,1},{17,9},{25,17},{2,26},{10... | collective-permute-start | bytes 147464 | tf_op jit(solution)/shard_map/ppermute | solution.py:401
  39.5 2.2 copy-done.4
  43.1 1.7 copy.49
  44.9 1.7 reshape.103
  46.6 1.7 copy.48
  48.3 1.7 reshape.105
  50.0 1.6 pad.13.refs_6_
  51.6 1.5 pad.14.refs_5_
  54.8 1.7 shard_map.133
  58.1 3.2 %collective-permute-start.4 = (bf16[192,256]{1,0:T(8,128)(2,1)}, bf16[192,256]{1,0:T(8,128)(2,1)}, u32[]{:S(2)}, u32[]{:S(2)}) collective-permute-start(bf16[192,256]{1,0:T(8,128)(2,1)} %get-tuple-element.79), channel_id=1, source_target_pairs={{0,7},{1,0},{2,1},{3,2},{4,3},{5,4},{6,5},{7,6},{8,15},{9,8},{10,9... | collective-permute-start | bytes 294920 | tf_op jit(solution)/shard_map/ppermute | solution.py:401
  61.3 2.3 %gather_fusion.1 = bf16[9,128,128]{2,1,0:T(8,128)(2,1)} fusion(bf16[9,128,128]{2,1,0:T(8,128)(2,1)} %param.20, s32[1024]{0:T(1024)S(1)} %pad_clamp_fusion), kind=kCustom, calls=%fused_computation.1 | custom fusion | bytes 589860 | tf_op jit(solution)/shard_map/gather | solution.py:519
  68.8 1.9 copy.28
  70.7 1.8 pad.12.refs_6_
  75.0 3.4 %all-to-all-start.1 = ((bf16[32,8,2048]{2,1,0:T(8,128)(2,1)}), bf16[32,8,2048]{2,1,0:T(8,128)(2,1)}, u32[]{:S(2)}, u32[]{:S(2)}) async-start(bf16[32,8,2048]{2,1,0:T(8,128)(2,1)} %bitcast.58), calls=%async_computation.1 | async-start | bytes 2097152 | tf_op jit(solution)/shard_map/all_to_all | solution.py:553
  78.4 2.5 %shard_map.136 = (f32[128,16,128]{2,1,0:T(8,128)S(1)}, bf16[16,128]{1,0:T(8,128)(2,1)S(1)}, bf16[16,128]{1,0:T(8,128)(2,1)S(1)}, bf16[16,128]{1,0:T(8,128)(2,1)S(1)}, bf16[16,128]{1,0:T(8,128)(2,1)S(1)}) custom-call(s32[1,1]{1,0:T(1,128)} %copy.50.turn.refs_0_, bf16[256,2176]{1,0:T(8,128)(2,1)S(1)} %bitcast.55), custom_call_target="tpu_custom_call" | custom-call | tf_op jit(solution)/shard_map/pallas_call | solution.py:555
  80.9 1.7 collective-permute-start.5
  82.6 1.4 collective-permute-start.6
  84.0 2.5 %collective-permute-done.5.above = bf16[16,128]{1,0:T(8,128)(2,1)S(1)} collective-permute-done((bf16[16,128]{1,0:T(8,128)(2,1)S(1)}, bf16[16,128]{1,0:T(8,128)(2,1)S(1)}, u32[]{:S(2)}, u32[]{:S(2)}) %collective-permute-start.5) | collective-permute-done | bytes 4128 | tf_op jit(solution)/shard_map/ppermute | solution.py:401
  86.6 3.9 %collective-permute-start.8 = (bf16[16,256]{1,0:T(8,128)(2,1)S(1)}, bf16[16,256]{1,0:T(8,128)(2,1)S(1)}, u32[]{:S(2)}, u32[]{:S(2)}) collective-permute-start(bf16[16,256]{1,0:T(8,128)(2,1)S(1)} %get-tuple-element.96), channel_id=1, source_target_pairs={{0,7},{1,0},{2,1},{3,2},{4,3},{5,4},{6,5},{7,6},{8,15},{9,8},{10,9... | collective-permute-start | bytes 24584 | tf_op jit(solution)/shard_map/ppermute | solution.py:401
  90.5 8.9 %collective-permute-done.7.refs_6_ = bf16[16,256]{1,0:T(8,128)(2,1)S(1)} collective-permute-done((bf16[16,256]{1,0:T(8,128)(2,1)S(1)}, bf16[16,256]{1,0:T(8,128)(2,1)S(1)}, u32[]{:S(2)}, u32[]{:S(2)}) %collective-permute-start.7) | collective-permute-done | bytes 8224 | tf_op jit(solution)/shard_map/ppermute | solution.py:401
  101.0 1.4 shard_map.138
  102.4 2.2 copy-done.2
  105.6 19.3 %shard_map.139 = (bf16[128,128,128]{2,1,0:T(8,128)(2,1)S(1)}, bf16[128,128]{1,0:T(8,128)(2,1)S(1)}, bf16[128,128]{1,0:T(8,128)(2,1)S(1)}, bf16[128,128]{1,0:T(8,128)(2,1)S(1)}, bf16[128,128]{1,0:T(8,128)(2,1)S(1)}) custom-call(s32[1,1]{1,0:T(1,128)} %copy.50.turn.refs_0_, bf16[128,128,128]{2,1,0:T(8,128)(2,1)S(1)} %bitcast.51, ...), custom_call_target="tpu_custom_call" | custom-call | tf_op jit(solution)/shard_map/pallas_call | solution.py:388
  124.9 2.0 copy-done.8
  126.8 1.5 collective-permute-start.9
  128.3 1.4 collective-permute-start.10
  129.8 1.9 collective-permute-done.9.above
  132.4 3.5 %collective-permute-start.12 = (bf16[128,256]{1,0:T(8,128)(2,1)S(1)}, bf16[128,256]{1,0:T(8,128)(2,1)S(1)}, u32[]{:S(2)}, u32[]{:S(2)}) collective-permute-start(bf16[128,256]{1,0:T(8,128)(2,1)S(1)} %get-tuple-element.109), channel_id=1, source_target_pairs={{0,7},{1,0},{2,1},{3,2},{4,3},{5,4},{6,5},{7,6},{8,15},{9,8},{10,9... | collective-permute-start | bytes 196616 | tf_op jit(solution)/shard_map/ppermute | solution.py:401
  136.0 3.6 %shard_map.143 = (f32[128,16,128]{2,1,0:T(8,128)S(1)}, bf16[16,128]{1,0:T(8,128)(2,1)S(1)}, bf16[16,128]{1,0:T(8,128)(2,1)S(1)}, bf16[16,128]{1,0:T(8,128)(2,1)S(1)}, bf16[16,128]{1,0:T(8,128)(2,1)S(1)}) custom-call(s32[1,128]{1,0:T(1,128)S(1)} %bitcast.62, bf16[256,2048]{1,0:T(8,128)(2,1)} %bitcast.23.returned), custom_call_target="tpu_custom_call" | custom-call | tf_op jit(solution)/shard_map/pallas_call | solution.py:570
  139.6 2.4 %collective-permute-start.14 = (bf16[16,128]{1,0:T(8,128)(2,1)S(1)}, bf16[16,128]{1,0:T(8,128)(2,1)S(1)}, u32[]{:S(2)}, u32[]{:S(2)}) collective-permute-start(bf16[16,128]{1,0:T(8,128)(2,1)S(1)} %get-tuple-element.118), channel_id=1, source_target_pairs={{0,24},{8,0},{16,8},{24,16},{1,25},{9,1},{17,9},{25,17},{2,26},{10... | collective-permute-start | bytes 12296 | tf_op jit(solution)/shard_map/ppermute | solution.py:401
  143.6 3.6 %collective-permute-done.13.above = bf16[16,128]{1,0:T(8,128)(2,1)S(1)} collective-permute-done((bf16[16,128]{1,0:T(8,128)(2,1)S(1)}, bf16[16,128]{1,0:T(8,128)(2,1)S(1)}, u32[]{:S(2)}, u32[]{:S(2)}) %collective-permute-start.13) | collective-permute-done | bytes 4128 | tf_op jit(solution)/shard_map/ppermute | solution.py:401
  147.4 3.5 %collective-permute-start.17 = (bf16[16,256]{1,0:T(8,128)(2,1)S(1)}, bf16[16,256]{1,0:T(8,128)(2,1)S(1)}, u32[]{:S(2)}, u32[]{:S(2)}) collective-permute-start(bf16[16,256]{1,0:T(8,128)(2,1)S(1)} %get-tuple-element.124), channel_id=1, source_target_pairs={{0,7},{1,0},{2,1},{3,2},{4,3},{5,4},{6,5},{7,6},{8,15},{9,8},{10,9... | collective-permute-start | bytes 24584 | tf_op jit(solution)/shard_map/ppermute | solution.py:401
  153.5 11.6 %shard_map.146 = (bf16[128,64,128]{2,1,0:T(8,128)(2,1)S(1)}, bf16[64,128]{1,0:T(8,128)(2,1)S(1)}, bf16[64,128]{1,0:T(8,128)(2,1)S(1)}, bf16[64,128]{1,0:T(8,128)(2,1)S(1)}, bf16[64,128]{1,0:T(8,128)(2,1)S(1)}) custom-call(s32[1,1]{1,0:T(1,128)} %copy.50.turn.refs_0_, bf16[128,64,128]{2,1,0:T(8,128)(2,1)S(1)} %fusion.ocean.refs_1_.refs_6_, ...), custom_call_target="tpu_custom_call" | custom-call | tf_op jit(solution)/shard_map/pallas_call | solution.py:388
  166.4 2.1 collective-permute-start.19
  170.2 6.1 %collective-permute-done.18.above = bf16[64,128]{1,0:T(8,128)(2,1)S(1)} collective-permute-done((bf16[64,128]{1,0:T(8,128)(2,1)S(1)}, bf16[64,128]{1,0:T(8,128)(2,1)S(1)}, u32[]{:S(2)}, u32[]{:S(2)}) %collective-permute-start.18) | collective-permute-done | bytes 16416 | tf_op jit(solution)/shard_map/ppermute | solution.py:401
  176.5 3.5 %collective-permute-start.22 = (bf16[64,256]{1,0:T(8,128)(2,1)S(1)}, bf16[64,256]{1,0:T(8,128)(2,1)S(1)}, u32[]{:S(2)}, u32[]{:S(2)}) collective-permute-start(bf16[64,256]{1,0:T(8,128)(2,1)S(1)} %get-tuple-element.137), channel_id=1, source_target_pairs={{0,7},{1,0},{2,1},{3,2},{4,3},{5,4},{6,5},{7,6},{8,15},{9,8},{10,9... | collective-permute-start | bytes 98312 | tf_op jit(solution)/shard_map/ppermute | solution.py:401
  180.7 2.2 copy-done.3
  182.8 2.2 copy-done.9
  185.0 16.3 %shard_map.142 = bf16[128,128,128]{2,1,0:T(8,128)(2,1)S(1)} custom-call(s32[1,1]{1,0:T(1,128)} %copy.50.turn.refs_0_, bf16[128,128,128]{2,1,0:T(8,128)(2,1)S(1)} %copy-done.9, f32[2,128,256]{2,1,0:T(8,128)S(1)} %get-tuple-element.110.refs_2_, f32[128,128]{1,0:T(8,128)S(1)} %get-tuple-element.111.refs_3_, f32[128,128]{1,0:T(8,128)S(1)} %get-tuple-element.112.refs_4_, ...), custom_call_target="tpu_custom_call" | custom-call | tf_op jit(solution)/shard_map/pallas_call | solution.py:388
  201.4 4.7 %copy.33 = bf16[128,128,128]{2,1,0:T(8,128)(2,1)} copy(bf16[128,128,128]{2,0,1:T(8,128)(2,1)S(1)} %bitcast.53) | data formatting | bytes 8388608
  206.2 9.8 %shard_map.149 = bf16[128,64,128]{2,1,0:T(8,128)(2,1)S(1)} custom-call(s32[1,1]{1,0:T(1,128)} %copy.50.turn.refs_0_, bf16[128,64,128]{2,1,0:T(8,128)(2,1)S(1)} %copy-done.12, f32[2,64,256]{2,1,0:T(8,128)S(1)} %get-tuple-element.138.refs_2_, f32[64,128]{1,0:T(8,128)S(1)} %get-tuple-element.139.refs_3_, f32[64,128]{1,0:T(8,128)S(1)} %get-tuple-element.140.refs_4_, ...), custom_call_target="tpu_custom_call" | custom-call | tf_op jit(solution)/shard_map/pallas_call | solution.py:388
  216.0 2.7 %copy.34 = bf16[64,128,128]{2,1,0:T(8,128)(2,1)} copy(bf16[64,128,128]{2,0,1:T(8,128)(2,1)S(1)} %bitcast.56) | data formatting | bytes 4194304
  (119 shorter events, 34.2 us)
Async XLA Ops:
  0.6 64.9 %copy-start = (bf16[9,128,144]{1,2,0:T(8,128)(2,1)S(1)}, bf16[9,128,144]{1,2,0:T(8,128)(2,1)}, u32[]{:S(2)}) copy-start(bf16[9,128,144]{1,2,0:T(8,128)(2,1)} %param.19) | copy-start | bytes 995332
  0.6 1.6 copy-start.5
  4.9 8.9 %copy-start.30 = (s32[128,4]{0,1:T(4,128)S(1)}, s32[128,4]{0,1:T(4,128)}, u32[]{:S(2)}) copy-start(s32[128,4]{0,1:T(4,128)} %param.14) | copy-start | bytes 6148
  5.5 1.0 copy-start.7
  6.5 66.0 %all-to-all-start = ((bf16[32,8,2176]{2,1,0:T(8,128)(2,1)}), bf16[32,8,2176]{2,1,0:T(8,128)(2,1)S(1)}, u32[]{:S(2)}, u32[]{:S(2)}) async-start(bf16[32,8,2176]{2,1,0:T(8,128)(2,1)} %bitcast.57), calls=%async_computation | async-start | bytes 2228224 | tf_op jit(solution)/shard_map/all_to_all | solution.py:501
  15.2 5.0 %copy-start.6 = (bf16[64,128,128]{2,1,0:T(8,128)(2,1)S(1)}, bf16[64,128,128]{2,1,0:T(8,128)(2,1)}, u32[]{:S(2)}) copy-start(bf16[64,128,128]{2,1,0:T(8,128)(2,1)} %surface.2) | copy-start | bytes 6291460
  15.2 5.1 %copy-start.35 = (bf16[128,128]{1,0:T(8,128)(2,1)S(1)}, bf16[128,128]{1,0:T(8,128)(2,1)}, u32[]{:S(2)}) copy-start(bf16[128,128]{1,0:T(8,128)(2,1)} %copy.25) | copy-start | bytes 98308
  20.3 2.0 copy-start.1
  29.5 23.6 %collective-permute-start = (bf16[192,128]{1,0:T(8,128)(2,1)}, bf16[192,128]{1,0:T(8,128)(2,1)}, u32[]{:S(2)}, u32[]{:S(2)}) collective-permute-start(bf16[192,128]{1,0:T(8,128)(2,1)} %get-tuple-element.72), channel_id=1, source_target_pairs={{0,8},{8,16},{16,24},{24,0},{1,9},{9,17},{17,25},{25,1},{2,10},{10... | collective-permute-start | bytes 147464 | tf_op jit(solution)/shard_map/ppermute | solution.py:401
  32.6 20.5 %collective-permute-start.2 = (bf16[64,128]{1,0:T(8,128)(2,1)}, bf16[64,128]{1,0:T(8,128)(2,1)}, u32[]{:S(2)}, u32[]{:S(2)}) collective-permute-start(bf16[64,128]{1,0:T(8,128)(2,1)} %slice.3), channel_id=1, source_target_pairs={{24,31},{25,30},{26,29},{27,28},{28,27},{29,26},{30,25},{31,24}} | collective-permute-start | bytes 49160 | tf_op jit(solution)/shard_map/ppermute | solution.py:414
  33.9 19.3 %collective-permute-start.1 = (bf16[192,128]{1,0:T(8,128)(2,1)}, bf16[192,128]{1,0:T(8,128)(2,1)}, u32[]{:S(2)}, u32[]{:S(2)}) collective-permute-start(bf16[192,128]{1,0:T(8,128)(2,1)} %get-tuple-element.73), channel_id=1, source_target_pairs={{0,24},{8,0},{16,8},{24,16},{1,25},{9,1},{17,9},{25,17},{2,26},{10... | collective-permute-start | bytes 147464 | tf_op jit(solution)/shard_map/ppermute | solution.py:401
  39.5 2.2 %copy-start.4 = (bf16[128,128,128]{2,1,0:T(8,128)(2,1)S(1)}, bf16[128,128,128]{2,1,0:T(8,128)(2,1)}, u32[]{:S(2)}) copy-start(bf16[128,128,128]{2,1,0:T(8,128)(2,1)} %surface.3) | copy-start | bytes 12582916
  57.7 14.8 %collective-permute-start.3 = (bf16[192,256]{1,0:T(8,128)(2,1)}, bf16[192,256]{1,0:T(8,128)(2,1)}, u32[]{:S(2)}, u32[]{:S(2)}) collective-permute-start(bf16[192,256]{1,0:T(8,128)(2,1)} %get-tuple-element.78), channel_id=1, source_target_pairs={{0,1},{1,2},{2,3},{3,4},{4,5},{5,6},{6,7},{7,0},{8,9},{9,10},{10,1... | collective-permute-start | bytes 294920 | tf_op jit(solution)/shard_map/ppermute | solution.py:401
  58.1 14.4 %collective-permute-start.4 = (bf16[192,256]{1,0:T(8,128)(2,1)}, bf16[192,256]{1,0:T(8,128)(2,1)}, u32[]{:S(2)}, u32[]{:S(2)}) collective-permute-start(bf16[192,256]{1,0:T(8,128)(2,1)} %get-tuple-element.79), channel_id=1, source_target_pairs={{0,7},{1,0},{2,1},{3,2},{4,3},{5,4},{6,5},{7,6},{8,15},{9,8},{10,9... | collective-permute-start | bytes 294920 | tf_op jit(solution)/shard_map/ppermute | solution.py:401
  72.5 1.0 copy-start.14
  74.0 1.0 copy-start.10
  75.0 61.0 %all-to-all-start.1 = ((bf16[32,8,2048]{2,1,0:T(8,128)(2,1)}), bf16[32,8,2048]{2,1,0:T(8,128)(2,1)}, u32[]{:S(2)}, u32[]{:S(2)}) async-start(bf16[32,8,2048]{2,1,0:T(8,128)(2,1)} %bitcast.58), calls=%async_computation.1 | async-start | bytes 2097152 | tf_op jit(solution)/shard_map/all_to_all | solution.py:553
  80.9 5.6 %collective-permute-start.5 = (bf16[16,128]{1,0:T(8,128)(2,1)S(1)}, bf16[16,128]{1,0:T(8,128)(2,1)S(1)}, u32[]{:S(2)}, u32[]{:S(2)}) collective-permute-start(bf16[16,128]{1,0:T(8,128)(2,1)S(1)} %get-tuple-element.89), channel_id=1, source_target_pairs={{0,8},{8,16},{16,24},{24,0},{1,9},{9,17},{17,25},{25,1},{2,10},{10... | collective-permute-start | bytes 12296 | tf_op jit(solution)/shard_map/ppermute | solution.py:401
  82.6 3.9 %collective-permute-start.6 = (bf16[16,128]{1,0:T(8,128)(2,1)S(1)}, bf16[16,128]{1,0:T(8,128)(2,1)S(1)}, u32[]{:S(2)}, u32[]{:S(2)}) collective-permute-start(bf16[16,128]{1,0:T(8,128)(2,1)S(1)} %get-tuple-element.90), channel_id=1, source_target_pairs={{0,24},{8,0},{16,8},{24,16},{1,25},{9,1},{17,9},{25,17},{2,26},{10... | collective-permute-start | bytes 12296 | tf_op jit(solution)/shard_map/ppermute | solution.py:401
  86.6 12.8 %collective-permute-start.7 = (bf16[16,256]{1,0:T(8,128)(2,1)S(1)}, bf16[16,256]{1,0:T(8,128)(2,1)S(1)}, u32[]{:S(2)}, u32[]{:S(2)}) collective-permute-start(bf16[16,256]{1,0:T(8,128)(2,1)S(1)} %get-tuple-element.95), channel_id=1, source_target_pairs={{0,1},{1,2},{2,3},{3,4},{4,5},{5,6},{6,7},{7,0},{8,9},{9,10},{10,1... | collective-permute-start | bytes 24584 | tf_op jit(solution)/shard_map/ppermute | solution.py:401
  86.6 12.8 %collective-permute-start.8 = (bf16[16,256]{1,0:T(8,128)(2,1)S(1)}, bf16[16,256]{1,0:T(8,128)(2,1)S(1)}, u32[]{:S(2)}, u32[]{:S(2)}) collective-permute-start(bf16[16,256]{1,0:T(8,128)(2,1)S(1)} %get-tuple-element.96), channel_id=1, source_target_pairs={{0,7},{1,0},{2,1},{3,2},{4,3},{5,4},{6,5},{7,6},{8,15},{9,8},{10,9... | collective-permute-start | bytes 24584 | tf_op jit(solution)/shard_map/ppermute | solution.py:401
  102.4 2.2 %copy-start.2 = (bf16[128,128,128]{2,0,1:T(8,128)(2,1)S(1)}, bf16[128,128,128]{2,0,1:T(8,128)(2,1)}, u32[]{:S(2)}) copy-start(bf16[128,128,128]{2,0,1:T(8,128)(2,1)} %copy-done.1) | copy-start | bytes 12582916
  104.6 1.0 copy-start.15
  105.6 30.4 %copy-start.32 = (s32[128,1]{0,1:T(1,128)S(1)}, s32[128,1]{0,1:T(1,128)}, u32[]{:S(2)}) copy-start(s32[128,1]{0,1:T(1,128)} %param.16) | copy-start | bytes 1540
  105.6 46.8 %copy-start.21 = (bf16[192,128]{1,0:T(8,128)(2,1)S(1)}, bf16[192,128]{1,0:T(8,128)(2,1)}, u32[]{:S(2)}) copy-start(bf16[192,128]{1,0:T(8,128)(2,1)} %copy-done.19) | copy-start | bytes 147460
  105.6 46.8 %copy-start.24 = (bf16[192,128]{1,0:T(8,128)(2,1)S(1)}, bf16[192,128]{1,0:T(8,128)(2,1)}, u32[]{:S(2)}) copy-start(bf16[192,128]{1,0:T(8,128)(2,1)} %copy-done.22) | copy-start | bytes 147460
  105.6 47.9 %copy-start.17 = (bf16[192,256]{1,0:T(8,128)(2,1)S(1)}, bf16[192,256]{1,0:T(8,128)(2,1)}, u32[]{:S(2)}) copy-start(bf16[192,256]{1,0:T(8,128)(2,1)} %pad.13.refs_6_) | copy-start | bytes 294916
  124.9 2.0 copy-start.8
  126.8 4.8 %collective-permute-start.9 = (bf16[128,128]{1,0:T(8,128)(2,1)S(1)}, bf16[128,128]{1,0:T(8,128)(2,1)S(1)}, u32[]{:S(2)}, u32[]{:S(2)}) collective-permute-start(bf16[128,128]{1,0:T(8,128)(2,1)S(1)} %get-tuple-element.102), channel_id=1, source_target_pairs={{0,8},{8,16},{16,24},{24,0},{1,9},{9,17},{17,25},{25,1},{2,10},{10... | collective-permute-start | bytes 98312 | tf_op jit(solution)/shard_map/ppermute | solution.py:401
  128.3 3.9 %collective-permute-start.10 = (bf16[128,128]{1,0:T(8,128)(2,1)S(1)}, bf16[128,128]{1,0:T(8,128)(2,1)S(1)}, u32[]{:S(2)}, u32[]{:S(2)}) collective-permute-start(bf16[128,128]{1,0:T(8,128)(2,1)S(1)} %get-tuple-element.103), channel_id=1, source_target_pairs={{0,24},{8,0},{16,8},{24,16},{1,25},{9,1},{17,9},{25,17},{2,26},{10... | collective-permute-start | bytes 98312 | tf_op jit(solution)/shard_map/ppermute | solution.py:401
  132.4 47.8 %collective-permute-start.11 = (bf16[128,256]{1,0:T(8,128)(2,1)S(1)}, bf16[128,256]{1,0:T(8,128)(2,1)S(1)}, u32[]{:S(2)}, u32[]{:S(2)}) collective-permute-start(bf16[128,256]{1,0:T(8,128)(2,1)S(1)} %get-tuple-element.108), channel_id=1, source_target_pairs={{0,1},{1,2},{2,3},{3,4},{4,5},{5,6},{6,7},{7,0},{8,9},{9,10},{10,1... | collective-permute-start | bytes 196616 | tf_op jit(solution)/shard_map/ppermute | solution.py:401
  132.4 47.8 %collective-permute-start.12 = (bf16[128,256]{1,0:T(8,128)(2,1)S(1)}, bf16[128,256]{1,0:T(8,128)(2,1)S(1)}, u32[]{:S(2)}, u32[]{:S(2)}) collective-permute-start(bf16[128,256]{1,0:T(8,128)(2,1)S(1)} %get-tuple-element.109), channel_id=1, source_target_pairs={{0,7},{1,0},{2,1},{3,2},{4,3},{5,4},{6,5},{7,6},{8,15},{9,8},{10,9... | collective-permute-start | bytes 196616 | tf_op jit(solution)/shard_map/ppermute | solution.py:401
  139.6 4.0 %collective-permute-start.14 = (bf16[16,128]{1,0:T(8,128)(2,1)S(1)}, bf16[16,128]{1,0:T(8,128)(2,1)S(1)}, u32[]{:S(2)}, u32[]{:S(2)}) collective-permute-start(bf16[16,128]{1,0:T(8,128)(2,1)S(1)} %get-tuple-element.118), channel_id=1, source_target_pairs={{0,24},{8,0},{16,8},{24,16},{1,25},{9,1},{17,9},{25,17},{2,26},{10... | collective-permute-start | bytes 12296 | tf_op jit(solution)/shard_map/ppermute | solution.py:401
  142.0 1.6 collective-permute-start.15
  142.7 4.6 %collective-permute-start.13 = (bf16[16,128]{1,0:T(8,128)(2,1)S(1)}, bf16[16,128]{1,0:T(8,128)(2,1)S(1)}, u32[]{:S(2)}, u32[]{:S(2)}) collective-permute-start(bf16[16,128]{1,0:T(8,128)(2,1)S(1)} %get-tuple-element.117), channel_id=1, source_target_pairs={{0,8},{8,16},{16,24},{24,0},{1,9},{9,17},{17,25},{25,1},{2,10},{10... | collective-permute-start | bytes 12296 | tf_op jit(solution)/shard_map/ppermute | solution.py:401
  147.4 4.9 %collective-permute-start.16 = (bf16[16,256]{1,0:T(8,128)(2,1)S(1)}, bf16[16,256]{1,0:T(8,128)(2,1)S(1)}, u32[]{:S(2)}, u32[]{:S(2)}) collective-permute-start(bf16[16,256]{1,0:T(8,128)(2,1)S(1)} %get-tuple-element.123), channel_id=1, source_target_pairs={{0,1},{1,2},{2,3},{3,4},{4,5},{5,6},{6,7},{7,0},{8,9},{9,10},{10,1... | collective-permute-start | bytes 24584 | tf_op jit(solution)/shard_map/ppermute | solution.py:401
  147.4 4.9 %collective-permute-start.17 = (bf16[16,256]{1,0:T(8,128)(2,1)S(1)}, bf16[16,256]{1,0:T(8,128)(2,1)S(1)}, u32[]{:S(2)}, u32[]{:S(2)}) collective-permute-start(bf16[16,256]{1,0:T(8,128)(2,1)S(1)} %get-tuple-element.124), channel_id=1, source_target_pairs={{0,7},{1,0},{2,1},{3,2},{4,3},{5,4},{6,5},{7,6},{8,15},{9,8},{10,9... | collective-permute-start | bytes 24584 | tf_op jit(solution)/shard_map/ppermute | solution.py:401
  152.4 28.3 %copy-start.16 = (bf16[48,8,3,128]{3,1,2,0:T(8,128)(2,1)S(1)}, bf16[48,8,3,128]{3,1,2,0:T(8,128)(2,1)}, u32[]{:S(2)}) copy-start(bf16[48,8,3,128]{3,1,2,0:T(8,128)(2,1)} %copy.47) | copy-start | bytes 884740
  165.1 1.3 copy-start.11
  166.4 3.8 %collective-permute-start.19 = (bf16[64,128]{1,0:T(8,128)(2,1)S(1)}, bf16[64,128]{1,0:T(8,128)(2,1)S(1)}, u32[]{:S(2)}, u32[]{:S(2)}) collective-permute-start(bf16[64,128]{1,0:T(8,128)(2,1)S(1)} %get-tuple-element.131), channel_id=1, source_target_pairs={{0,24},{8,0},{16,8},{24,16},{1,25},{9,1},{17,9},{25,17},{2,26},{10... | collective-permute-start | bytes 49160 | tf_op jit(solution)/shard_map/ppermute | solution.py:401
  168.5 1.7 collective-permute-start.20
  169.2 7.1 %collective-permute-start.18 = (bf16[64,128]{1,0:T(8,128)(2,1)S(1)}, bf16[64,128]{1,0:T(8,128)(2,1)S(1)}, u32[]{:S(2)}, u32[]{:S(2)}) collective-permute-start(bf16[64,128]{1,0:T(8,128)(2,1)S(1)} %get-tuple-element.130), channel_id=1, source_target_pairs={{0,8},{8,16},{16,24},{24,0},{1,9},{9,17},{17,25},{25,1},{2,10},{10... | collective-permute-start | bytes 49160 | tf_op jit(solution)/shard_map/ppermute | solution.py:401
  176.5 29.6 %collective-permute-start.21 = (bf16[64,256]{1,0:T(8,128)(2,1)S(1)}, bf16[64,256]{1,0:T(8,128)(2,1)S(1)}, u32[]{:S(2)}, u32[]{:S(2)}) collective-permute-start(bf16[64,256]{1,0:T(8,128)(2,1)S(1)} %get-tuple-element.136), channel_id=1, source_target_pairs={{0,1},{1,2},{2,3},{3,4},{4,5},{5,6},{6,7},{7,0},{8,9},{9,10},{10,1... | collective-permute-start | bytes 98312 | tf_op jit(solution)/shard_map/ppermute | solution.py:401
  176.5 29.6 %collective-permute-start.22 = (bf16[64,256]{1,0:T(8,128)(2,1)S(1)}, bf16[64,256]{1,0:T(8,128)(2,1)S(1)}, u32[]{:S(2)}, u32[]{:S(2)}) collective-permute-start(bf16[64,256]{1,0:T(8,128)(2,1)S(1)} %get-tuple-element.137), channel_id=1, source_target_pairs={{0,7},{1,0},{2,1},{3,2},{4,3},{5,4},{6,5},{7,6},{8,15},{9,8},{10,9... | collective-permute-start | bytes 98312 | tf_op jit(solution)/shard_map/ppermute | solution.py:401
  180.6 2.2 %copy-start.3 = (bf16[128,128,128]{2,0,1:T(8,128)(2,1)S(1)}, bf16[128,128,128]{2,0,1:T(8,128)(2,1)}, u32[]{:S(2)}) copy-start(bf16[128,128,128]{2,0,1:T(8,128)(2,1)} %copy-done.1) | copy-start | bytes 12582916
  182.8 2.2 %copy-start.9 = (bf16[128,128,128]{2,1,0:T(8,128)(2,1)S(1)}, bf16[128,128,128]{2,1,0:T(8,128)(2,1)}, u32[]{:S(2)}) copy-start(bf16[128,128,128]{2,1,0:T(8,128)(2,1)} %copy-done.8) | copy-start | bytes 12582916
  201.3 4.9 %copy-start.12 = (bf16[128,64,128]{2,1,0:T(8,128)(2,1)S(1)}, bf16[128,64,128]{2,1,0:T(8,128)(2,1)}, u32[]{:S(2)}) copy-start(bf16[128,64,128]{2,1,0:T(8,128)(2,1)} %copy-done.11) | copy-start | bytes 6291460
  201.4 4.9 %copy-start.18 = (bf16[192,256]{1,0:T(8,128)(2,1)S(1)}, bf16[192,256]{1,0:T(8,128)(2,1)}, u32[]{:S(2)}) copy-start(bf16[192,256]{1,0:T(8,128)(2,1)} %pad.14.refs_5_) | copy-start | bytes 294916
  (13 other events, 9.1 us)
where the time goes:
time: 220 us; the launch traced here: 219 us
  Pallas kernels  76.1 us (35%)
  local copies, waits for them, and re-layouts  63.3 us (29%)
  starting transfers between devices  48.8 us (22%)
  waiting for transfers between devices  26.7 us (12%)
    pallas_call x4, Pallas kernels, convolve(): pl.pallas_call(partial(conv_kernel, len(sources), mode), out_shape=shapes...  56.9 us
    unnamed x77, local copies, waits for them, and re-layouts  41.4 us
    ppermute x20, starting transfers between devices, shifted(): lax.ppermute(value, axis, [(i, (i + distance) % count) for i in range(cou...  35.6 us
    ppermute x20, waiting for transfers between devices, shifted(): lax.ppermute(value, axis, [(i, (i + distance) % count) for i in range(cou...  26.7 us
    all_to_all x1, starting transfers between devices, on_device(): lax.all_to_all(payload, axes, split_axis=0, concat_axis=0, tiled=True)  7.33 us
    pallas_call x1, Pallas kernels, on_device(): pl.pallas_call(early_kernel, out_shape=edge_shapes(state_channels + ocean...  6 us
    reshape x4, local copies, waits for them, and re-layouts, stack_taps(): taps = weight.reshape(3, 3, outputs, channels).transpose(0, 2, 1, 3)  5.79 us
    reshape x3, local copies, waits for them, and re-layouts, stack_taps(): taps = taps.reshape(3 * outputs, 3 * channels)  5.36 us
  transfers between devices with their start and end apart: 25, of which 9 were waited for; matrix products, arithmetic and copies ran while one was open for 16% of the time, Pallas kernels for 30%

commit v1 on v0

--- a/solution.py
+++ b/solution.py
@@ -2,7 +2,6 @@
 
 import jax
 import jax.numpy as jnp
-import numpy as np
 from jax import lax
 from jax.experimental import pallas as pl
 from jax.experimental.pallas import tpu as pltpu
@@ -11,11 +10,16 @@
 CS = 16
 CF = 16
 RUN = 32
+RATE = 1 << 30
 F32 = jnp.float32
 BF16 = jnp.bfloat16
 VM = pl.BlockSpec(memory_space=pltpu.VMEM)
 SM = pl.BlockSpec(memory_space=pltpu.SMEM)
-SMALL = pltpu.CompilerParams(vmem_limit_bytes=16 << 20)
+SMALL = pltpu.CompilerParams(vmem_limit_bytes=8 << 20)
+
+
+def lasting(microseconds):
+    return pl.CostEstimate(flops=int(microseconds * RATE), bytes_accessed=0, transcendentals=0)
 
 
 def iota(shape, axis):
@@ -174,7 +178,7 @@
         edge[...] = value.astype(BF16)
 
 
-def force_kernel(capacity, target, returned, out, *edges):
+def force_kernel(capacity, place, target, returned, out, *edges):
     rows, cols = out.shape[0], out.shape[2]
     slots = returned.shape[0]
     first, second = iota((rows, rows), 0), iota((rows, rows), 1)
@@ -185,8 +189,14 @@
     pick = jnp.where(iota((rows, slots), 1) == slot, 1.0, 0.0).astype(BF16)
     for c in range(CF):
         out[:, c, :] = dot(pick, returned[:, c * cols : (c + 1) * cols])
-    for edge, value in zip(edges, all_edges(out)):
+    for edge, value in zip(edges, paired(place, all_edges(out))):
         edge[...] = value.astype(BF16)
+
+
+def paired(place, edges):
+    first, last, left, right = edges
+    even = place[0, 1] == 0
+    return jnp.where(even, first, last), jnp.where(even, last, first), left, right
 
 
 def widened(value):
@@ -200,25 +210,52 @@
     return jnp.where(lanes == 0, before, jnp.where(lanes == cols + 1, after, moved))
 
 
-def side_kernel(start, place, above, below, fold, left, right, *outs):
-    to_left, to_right, above_out, below_out = outs
-    over, under = above[...].astype(F32), below[...].astype(F32)
-    if fold is not None:
-        channels, cols = over.shape
+def side_kernel(start, swaps, place, *refs):
+    to_left, to_right, above_out, below_out = refs[-4:]
+    left, right = refs[-6:-4]
+    over, under = refs[0][...].astype(F32), refs[1][...].astype(F32)
+    channels, cols = over.shape
+    if swaps:
+        even = place[0, 1] == 0
+        over, under = jnp.where(even, over, under), jnp.where(even, under, over)
+        back = dot(under.astype(BF16), reverser(cols, True))
+        under = jnp.where(place[0, 0] == 1, back, under)
+    elif start is not None:
         ocean = iota((channels, cols), 0) >= start
-        over = jnp.where(ocean & (place[0] == 0), 0.0, over)
-        flip = reverser(cols, True)
-        back = dot(fold[...], flip)
-        if start:
-            back = jnp.concatenate([jnp.zeros((start, cols), F32), back], axis=0)
-        under = jnp.where(ocean & (place[0] == 1), back, under)
+        over = jnp.where(ocean & (place[0, 0] == 0), 0.0, over)
+        back = dot(refs[2][...], reverser(cols, True))
+        back = jnp.concatenate([jnp.zeros((start, cols), F32), back], axis=0)
+        under = jnp.where(ocean & (place[0, 0] == 1), back, under)
     above_out[...] = over.astype(BF16)
     below_out[...] = under.astype(BF16)
-    cols = over.shape[1]
     to_left[...] = framed(over[:, :1], left[...].astype(F32), under[:, :1]).astype(BF16)
     to_right[...] = framed(
         over[:, cols - 1 :], right[...].astype(F32), under[:, cols - 1 :]
     ).astype(BF16)
+
+
+def tap_kernel(splits, turn, *refs):
+    count = len(splits)
+    k = turn[0, 0]
+    for number, (split, turned) in enumerate(splits):
+        weight, out = refs[number], refs[count + number]
+        outputs, channels = weight.shape[1:]
+        for a in range(3):
+            taps = []
+            for b in range(3):
+                at = 3 * a + b
+                if turned:
+                    moved = (3 * b + 2 - a, 8 - at, 3 * (2 - b) + a)
+                    for quarter in range(3):
+                        at = jnp.where(k == quarter + 1, moved[quarter], at)
+                taps.append(weight[at].astype(F32))
+            row = [tap[:, :split] for tap in taps]
+            if split < channels:
+                row += [tap[:, split:] for tap in taps]
+            spare = out.shape[1] - 3 * channels
+            if spare:
+                row.append(jnp.zeros((outputs, spare), F32))
+            out[a * outputs : (a + 1) * outputs, :] = jnp.concatenate(row, axis=1).astype(BF16)
 
 
 def halo_kernel(spans, turned, turn, *refs):
@@ -257,50 +294,52 @@
     out = refs.pop(0)
     gelu = mode in ("turned", "plain")
     edges = [refs.pop(0) for _ in range(4)] if gelu else None
-    stacked, sums, early, late = refs[:4]
-    edge_left, edge_right = refs[4:] if gelu else (None, None)
+    stacked, sums = refs[:2]
+    edge_left, edge_right = refs[2:] if gelu else (None, None)
     rows, outputs, cols = out.shape
     channels = ends.shape[1]
     lanes = iota((channels, cols), 1)
     out_lanes = iota((outputs, cols), 1)
 
-    def place(slot, half, shifted):
+    spans, low = [], 0
+    for source in sources:
+        spans.append((low, low + source.shape[1]))
+        low += source.shape[1]
+
+    def place(slot, half, low, high, shifted):
         for b, value in enumerate(shifted):
-            stacked[slot, b * channels : (b + 1) * channels, half * cols : (half + 1) * cols] = (
-                value.astype(BF16)
+            at = 3 * low + b * (high - low)
+            stacked[slot, at : at + high - low, half * cols : (half + 1) * cols] = value.astype(
+                BF16
             )
 
     def inner(slot, half, y):
-        row = [source[y].astype(F32) for source in sources]
-        row = row[0] if parts == 1 else jnp.concatenate(row, axis=0)
-        before = pltpu.roll(left[...], lax.rem(cols - y, cols), 1)
-        after = pltpu.roll(right[...], cols - 1 - y, 1)
-        place(
-            slot,
-            half,
-            (
-                jnp.where(lanes == 0, before, pltpu.roll(row, 1, 1)),
+        for source, (low, high) in zip(sources, spans):
+            row = source[y].astype(F32)
+            before = pltpu.roll(left[low:high, :], lax.rem(cols - y, cols), 1)
+            after = pltpu.roll(right[low:high, :], cols - 1 - y, 1)
+            shifts = (
+                jnp.where(lanes[low:high] == 0, before, pltpu.roll(row, 1, 1)),
                 row,
-                jnp.where(lanes == cols - 1, after, pltpu.roll(row, cols - 1, 1)),
-            ),
-        )
+                jnp.where(lanes[low:high] == cols - 1, after, pltpu.roll(row, cols - 1, 1)),
+            )
+            place(slot, half, low, high, shifts)
 
     def end(slot, half, which):
-        row = ends[which]
-        place(slot, half, [row[:, b : b + cols] for b in range(3)])
+        for low, high in spans:
+            row = ends[which, low:high, :]
+            place(slot, half, low, high, [row[:, b : b + cols] for b in range(3)])
 
     def emit(y, value):
         if gelu:
             value = jax.nn.gelu(value, approximate=True).astype(BF16)
             out[y] = value
-            value = value.astype(F32)
-            edge_left[...] = jnp.where(out_lanes == y, value[:, 0:1], edge_left[...])
-            edge_right[...] = jnp.where(out_lanes == y, value[:, cols - 1 :], edge_right[...])
-        else:
-            value = base[y].astype(F32) + value
-            if mode == "masked":
-                value = value * mask[y]
-            out[y] = value.astype(BF16)
+            return value.astype(F32)
+        value = base[y].astype(F32) + value
+        if mode == "masked":
+            value = value * mask[y]
+        out[y] = value.astype(BF16)
+        return None
 
     def product(slot):
         sums[slot] = dot(taps[...], stacked[slot])
@@ -308,14 +347,22 @@
     def tap(slot, a, half):
         return sums[slot, a * outputs : (a + 1) * outputs, half * cols : (half + 1) * cols]
 
-    def carry(slot):
-        early[...] = tap(slot, 0, 0) + tap(slot, 1, 1)
-        late[...] = tap(slot, 0, 1)
-
     def finish(slot, j):
-        emit(2 * j - 2, early[...] + tap(slot, 2, 0))
-        emit(2 * j - 1, late[...] + tap(slot, 1, 0) + tap(slot, 2, 1))
-        carry(slot)
+        was = (slot + 3) % 4
+        rows_of = [
+            (2 * j - 2, tap(was, 0, 0) + tap(was, 1, 1) + tap(slot, 2, 0)),
+            (2 * j - 1, tap(was, 0, 1) + tap(slot, 1, 0) + tap(slot, 2, 1)),
+        ]
+        return [(y, emit(y, value)) for y, value in rows_of]
+
+    def note(done):
+        if gelu:
+            first, last = edge_left[...], edge_right[...]
+            for y, value in done:
+                first = jnp.where(out_lanes == y, value[:, 0:1], first)
+                last = jnp.where(out_lanes == y, value[:, cols - 1 :], last)
+            edge_left[...] = first
+            edge_right[...] = last
 
     def load(slot, j):
         inner(slot, 0, 2 * j - 1)
@@ -328,35 +375,44 @@
         edge_left[...] = jnp.zeros(edge_left.shape, F32)
         edge_right[...] = jnp.zeros(edge_right.shape, F32)
     pairs = rows // 2
-    end(0, 0, 0)
-    inner(0, 1, 0)
+    assert pairs % 4 == 0 and pairs >= 8
+    end(3, 0, 0)
+    inner(3, 1, 0)
+    load(0, 1)
+    load(1, 2)
+    product(3)
     product(0)
-    load(1, 1)
-    carry(0)
     product(1)
-    load(0, 2)
+    load(2, 3)
+    load(3, 4)
+
+    def half(j, now, other, final=False):
+        product(now)
+        done = finish(other, j - 2)
+        load(other, j + 2)
+        product(now + 1)
+        done += finish(other + 1, j - 1)
+        if final:
+            inner(other + 1, 0, rows - 1)
+            end(other + 1, 1, 1)
+        else:
+            load(other + 1, j + 3)
+        note(done)
 
     def step(i, _):
-        j = 2 * i + 2
-        product(0)
-        finish(1, j - 1)
-        load(1, j + 1)
-        product(1)
-        finish(0, j)
-        load(0, j + 2)
+        half(4 * i + 3, 2, 0)
+        half(4 * i + 5, 0, 2)
         return 0
 
-    lax.fori_loop(0, pairs // 2 - 2, step, 0)
-    product(0)
-    finish(1, pairs - 3)
-    load(1, pairs - 1)
-    product(1)
-    finish(0, pairs - 2)
-    inner(0, 0, rows - 1)
-    end(0, 1, 1)
-    product(0)
-    finish(1, pairs - 1)
-    finish(0, pairs)
+    lax.fori_loop(0, (pairs - 8) // 4, step, 0)
+    half(pairs - 5, 2, 0)
+    half(pairs - 3, 0, 2, True)
+    product(2)
+    done = finish(0, pairs - 3)
+    product(3)
+    done += finish(1, pairs - 2)
+    note(done)
+    note(finish(2, pairs - 1) + finish(3, pairs))
     if gelu:
         found = (
             out[0].astype(F32),
@@ -366,6 +422,8 @@
         )
         if mode == "turned":
             found = turn_edges(turn[0, 0], found, cols)
+        else:
+            found = paired(turn, found)
         for edge, value in zip(edges, found):
             edge[...] = value.astype(BF16)
 
@@ -377,10 +435,8 @@
     operands += [value for value in (base, mask) if value is not None]
     shapes = [jax.ShapeDtypeStruct((rows, outputs, cols), BF16)]
     scratch = [
-        pltpu.VMEM((2, taps.shape[1], 2 * cols), BF16),
-        pltpu.VMEM((2, taps.shape[0], 2 * cols), F32),
-        pltpu.VMEM((outputs, cols), F32),
-        pltpu.VMEM((outputs, cols), F32),
+        pltpu.VMEM((4, taps.shape[1], 2 * cols), BF16),
+        pltpu.VMEM((4, taps.shape[0], 2 * cols), F32),
     ]
     if base is None:
         shapes += [jax.ShapeDtypeStruct((outputs, cols), BF16)] * 4
@@ -391,6 +447,7 @@
         in_specs=[SM] + [VM] * (len(operands) - 1),
         out_specs=[VM] * len(shapes),
         scratch_shapes=scratch,
+        cost_estimate=lasting(rows * outputs * taps.shape[1] / 700000),
         compiler_params=SMALL,
     )(*operands)
     return (result[0], result[1:]) if base is None else result[0]
@@ -401,38 +458,51 @@
     return lax.ppermute(value, axis, [(i, (i + distance) % count) for i in range(count)])
 
 
-def exchanged(edges, place, start=None):
-    top, bottom, left, right = edges
-    channels, cols = top.shape
-    above = shifted(bottom, "face", 1)
-    below = shifted(top, "face", -1)
-    operands = [above, below]
+def send_rows(edges, start=None, swaps=False):
+    top, bottom = edges[:2]
+    faces, tiles = lax.axis_size("face"), lax.axis_size("tile")
+    north = (faces - 1) * tiles
+    axes = ("face", "tile")
+    fold = [(north + t, north + tiles - 1 - t) for t in range(tiles)]
+    if swaps:
+        assert faces % 2 == 0
+
+        def swap(low):
+            return [
+                (source * tiles + t, target * tiles + t)
+                for at in range(low, faces - 1, 2)
+                for source, target in ((at, at + 1), (at + 1, at))
+                for t in range(tiles)
+            ]
+
+        return [lax.ppermute(top, axes, swap(1) + fold), lax.ppermute(bottom, axes, swap(0))]
+    rows = [shifted(bottom, "face", 1), shifted(top, "face", -1)]
     if start is not None:
-        faces, tiles = lax.axis_size("face"), lax.axis_size("tile")
-        north = (faces - 1) * tiles
-        operands.append(
-            lax.ppermute(
-                bottom[start:],
-                ("face", "tile"),
-                [(north + t, north + tiles - 1 - t) for t in range(tiles)],
-            )
-        )
-    operands += [left, right]
-    kernel = partial(side_kernel, start)
-    if start is None:
-
-        def kernel(place, above, below, left, right, *outs):
-            side_kernel(None, place, above, below, None, left, right, *outs)
-
-    to_left, to_right, above, below = pl.pallas_call(
-        kernel,
+        rows.append(lax.ppermute(bottom[start:], axes, fold))
+    return rows
+
+
+def sides_of(place, rows, edges, start=None, swaps=False):
+    operands = [*rows, *edges[2:]]
+    channels, cols = edges[0].shape
+    return pl.pallas_call(
+        partial(side_kernel, start, swaps),
         out_shape=[jax.ShapeDtypeStruct((channels, 2 * cols), BF16)] * 2
         + [jax.ShapeDtypeStruct((channels, cols), BF16)] * 2,
         in_specs=[SM] + [VM] * len(operands),
         out_specs=[VM] * 4,
+        cost_estimate=lasting(1),
         compiler_params=SMALL,
     )(place, *operands)
+
+
+def send_sides(sides):
+    to_left, to_right, above, below = sides
     return above, below, shifted(to_right, "tile", 1), shifted(to_left, "tile", -1)
+
+
+def exchanged(edges, place, **how):
+    return send_sides(sides_of(place, send_rows(edges, **how), edges, **how))
 
 
 def halo_of(turn, spans, turned, *pieces):
@@ -445,15 +515,25 @@
         + [jax.ShapeDtypeStruct((channels, cols), F32)] * 2,
         in_specs=[SM] + [VM] * len(operands),
         out_specs=[VM] * 3,
+        cost_estimate=lasting(1),
         compiler_params=SMALL,
     )(turn, *operands)
 
 
-def stack_taps(weight):
-    _, outputs, channels = weight.shape
-    taps = weight.reshape(3, 3, outputs, channels).transpose(0, 2, 1, 3)
-    taps = taps.reshape(3 * outputs, 3 * channels)
-    return jnp.pad(taps, ((0, 0), (0, -taps.shape[1] % 128)))
+def stack_taps(turn, weights, splits):
+    def shape(weight):
+        _, outputs, channels = weight.shape
+        wide = 3 * channels + -3 * channels % 128
+        return jax.ShapeDtypeStruct((3 * outputs, wide), BF16)
+
+    return pl.pallas_call(
+        partial(tap_kernel, splits),
+        out_shape=[shape(weight) for weight in weights],
+        in_specs=[SM] + [VM] * len(weights),
+        out_specs=[VM] * len(weights),
+        cost_estimate=lasting(1),
+        compiler_params=SMALL,
+    )(turn, *weights)
 
 
 def on_device(
@@ -476,8 +556,8 @@
     slots = devices * capacity
     axes = ("face", "tile")
     face = lax.axis_index("face")
-    place = jnp.where(face == 0, 0, jnp.where(face == lax.axis_size("face") - 1, 1, 2))
-    place = place.astype(jnp.int32).reshape(1)
+    end = jnp.where(face == 0, 0, jnp.where(face == lax.axis_size("face") - 1, 1, 2))
+    place = jnp.stack([end, face % 2]).astype(jnp.int32).reshape(1, 2)
 
     def surface_spec(values, channels):
         return pl.BlockSpec((channels, *values.shape[1:]), lambda i: (0, 0, 0))
@@ -496,6 +576,7 @@
         out_shape=jax.ShapeDtypeStruct((slots, (CS + 1) * cols), BF16),
         in_specs=[surface_spec(ocean_state, CS)] + [whole(values) for values in small],
         out_specs=VM,
+        cost_estimate=lasting(1),
         compiler_params=SMALL,
     )(ocean_state, *small)
     incoming = lax.all_to_all(payload, axes, split_axis=0, concat_axis=0, tiled=True)
@@ -508,22 +589,28 @@
         out_shape=edge_shapes(state_channels + ocean_channels),
         in_specs=[SM, VM, VM],
         out_specs=[VM] * 4,
+        cost_estimate=lasting(6),
         compiler_params=SMALL,
     )(face_turns, state, ocean)
-    early_halo = exchanged(early, place, state_channels)
-
-    turned_taps = jnp.asarray(
-        np.stack([np.rot90(np.arange(9).reshape(3, 3), number).ravel() for number in range(4)])
-    )[face_turns[0, 0]]
-    taps1 = stack_taps(atmos_w1[turned_taps])
-    taps2 = stack_taps(atmos_w2[turned_taps])
-    ocean_taps1, ocean_taps2 = stack_taps(ocean_w1), stack_taps(ocean_w2)
+    early_halo = exchanged(early, place, start=state_channels)
+
+    taps1, taps2, ocean_taps1, ocean_taps2 = stack_taps(
+        face_turns,
+        (atmos_w1, atmos_w2, ocean_w1, ocean_w2),
+        (
+            (state_channels, True),
+            (state_channels, True),
+            (ocean_channels, False),
+            (ocean_channels, False),
+        ),
+    )
     common_rows = pl.pallas_call(
         common_kernel,
         grid=(1,),
         out_shape=jax.ShapeDtypeStruct((side, CF * side), BF16),
         in_specs=[SM, surface_spec(atmos_state, CF)],
         out_specs=VM,
+        cost_estimate=lasting(1),
         compiler_params=SMALL,
     )(face_turns, atmos_state)
     incoming, state, ocean, early_halo, common_rows, taps1, taps2, ocean_taps1, ocean_taps2 = (
@@ -547,53 +634,65 @@
         out_shape=jax.ShapeDtypeStruct((slots, CF * side), BF16),
         in_specs=[pl.BlockSpec((slots, side), lambda i: (0, CS)), VM],
         out_specs=VM,
+        cost_estimate=lasting(1),
         compiler_params=SMALL,
     )(incoming, common_rows)
-    incoming, answer = lax.optimization_barrier((incoming, answer))
+
+    barrier = lax.optimization_barrier
+    incoming, answer = barrier((incoming, answer))
     returned = lax.all_to_all(answer, axes, split_axis=0, concat_axis=0, tiled=True)
-
     sea, *sea_edges = pl.pallas_call(
         sea_kernel,
         out_shape=[jax.ShapeDtypeStruct((side, CS, side), F32), *edge_shapes(CS)],
         in_specs=[SM, VM],
         out_specs=[VM] * 5,
+        cost_estimate=lasting(3),
         compiler_params=SMALL,
     )(face_turns, incoming)
-    early_span = (0, state_channels)
-    halo = halo_of(
-        face_turns, [early_span, (0, CS)], True, early_halo, exchanged(sea_edges, place)
-    )
-    hidden, hidden_edges = convolve(face_turns, [state, sea], halo, taps1, "turned")
-    halo = halo_of(face_turns, [early_span], True, exchanged(hidden_edges, place))
-    atmos_out = convolve(face_turns, [hidden], halo, taps2, "add", base=state)
-
+    sea_halo = exchanged(sea_edges, place)
     forcing, *forcing_edges = pl.pallas_call(
         partial(force_kernel, capacity),
         out_shape=[jax.ShapeDtypeStruct((rows, CF, cols), F32), *edge_shapes(CF)],
-        in_specs=[VM, VM],
+        in_specs=[SM, VM, VM],
         out_specs=[VM] * 5,
-        compiler_params=SMALL,
-    )(target, returned)
-    early_span = (state_channels, state_channels + ocean_channels)
-    halo = halo_of(
-        face_turns, [early_span, (0, CF)], False, early_halo, exchanged(forcing_edges, place, 0)
-    )
-    hidden, hidden_edges = convolve(
-        face_turns, [ocean, forcing], halo, ocean_taps1, "plain"
-    )
-    halo = halo_of(
-        face_turns, [(0, ocean_channels)], False, exchanged(hidden_edges, place, 0)
-    )
+        cost_estimate=lasting(3),
+        compiler_params=SMALL,
+    )(place, target, returned)
+    forcing_rows = send_rows(forcing_edges, swaps=True)
+
+    state_span = (0, state_channels)
+    halo = halo_of(face_turns, [state_span, (0, CS)], True, early_halo, sea_halo)
+    sea, _ = barrier((sea, forcing))
+    hidden, hidden_edges = convolve(face_turns, [state, sea], halo, taps1, "turned")
+    forcing_rows, hidden_edges = barrier((forcing_rows, hidden_edges))
+    forcing_sides = sides_of(place, forcing_rows, forcing_edges, swaps=True)
+    forcing_halo = send_sides(forcing_sides)
+    hidden_sides = sides_of(place, send_rows(hidden_edges), hidden_edges)
+    hidden_halo = send_sides(hidden_sides)
+
+    ocean_span = (state_channels, state_channels + ocean_channels)
+    forcing, _ = barrier((forcing, hidden_sides[0]))
+    halo = halo_of(face_turns, [ocean_span, (0, CF)], False, early_halo, forcing_halo)
+    hidden_ocean, ocean_edges = convolve(place, [ocean, forcing], halo, ocean_taps1, "plain")
+
+    ocean_sent = send_rows(ocean_edges, swaps=True)
+    halo = halo_of(face_turns, [state_span], True, hidden_halo)
+    hidden, _ = barrier((hidden, hidden_ocean))
+    atmos_out = convolve(face_turns, [hidden], halo, taps2, "add", base=state)
+    ocean_sent, atmos_out = barrier((ocean_sent, atmos_out))
+    ocean_halo = send_sides(sides_of(place, ocean_sent, ocean_edges, swaps=True))
+    ocean_halo, atmos_out = barrier((ocean_halo, atmos_out.transpose(1, 0, 2)))
+    halo = halo_of(face_turns, [(0, ocean_channels)], False, ocean_halo)
     ocean_out = convolve(
-        face_turns,
-        [hidden],
+        place,
+        [hidden_ocean],
         halo,
         ocean_taps2,
         "masked",
         base=ocean,
         mask=mask.astype(F32)[:, None, :],
     )
-    return atmos_out.transpose(1, 0, 2), ocean_out.transpose(1, 0, 2)
+    return atmos_out, ocean_out.transpose(1, 0, 2)
 
 
 def solution(mesh):

time: 220 us -> 163 us (0.74)
  local copies, waits for them, and re-layouts: 63.3 us -> 32.3 us
  Pallas kernels: 76.1 us -> 57.4 us
  waiting for transfers between devices: 26.7 us -> 19.8 us
    pallas_call x4, Pallas kernels: 56.9 us -> 38 us  [convolve(): pl.pallas_call(partial(conv_kernel, len(sources), mode), out_shape=shapes...]
    ppermute x20 -> x16, waiting for transfers between devices: 26.7 us -> 13.7 us  [shifted(): lax.ppermute(value, axis, [(i, (i + distance) % count) for i in range(cou...]
    reshape x7 -> x0, local copies, waits for them, and re-layouts: 11.1 us -> none  [the longest x4 5.79 us: stack_taps(): taps = weight.reshape(3, 3, outputs, channels).transpose(0, 2, 1, 3)]
    unnamed x77 -> x72, local copies, waits for them, and re-layouts: 41.4 us -> 32.1 us
    ppermute x20 -> x16, starting transfers between devices: 35.6 us -> 27.8 us  [shifted(): lax.ppermute(value, axis, [(i, (i + distance) % count) for i in range(cou...]
    ppermute x3 -> x5, starting transfers between devices: 2.55 us -> 9.09 us  [the longest x2 7 us: send_rows(): lax.ppermute(bottom, axes, swap(0))]
    all_to_all x1, waiting for transfers between devices: 0.01 us -> 6.07 us  [on_device(): lax.all_to_all(answer, axes, split_axis=0, concat_axis=0, tiled=True)]
    pad x3 -> x0, local copies, waits for them, and re-layouts: 4.88 us -> none  [stack_taps(): return jnp.pad(taps, ((0, 0), (0, -taps.shape[1] % 128)))]
  transfers between devices with their start and end apart: 25 -> 23, of which waited for: 9 -> 8; matrix products, arithmetic and copies ran while one was open for 16% -> 5% of each run, Pallas kernels for 30% -> 26%
where the time goes in v1:
time: 163 us; the launch traced here: 161 us
  Pallas kernels  57.4 us (35%)
  starting transfers between devices  48.2 us (30%)
  local copies, waits for them, and re-layouts  32.3 us (20%)
  waiting for transfers between devices  19.8 us (12%)
  between operations  1.71 us (1%)
    pallas_call x4, Pallas kernels, convolve(): pl.pallas_call(partial(conv_kernel, len(sources), mode), out_shape=shapes...  38 us
    unnamed x72, local copies, waits for them, and re-layouts  32.1 us
    ppermute x16, starting transfers between devices, shifted(): lax.ppermute(value, axis, [(i, (i + distance) % count) for i in range(cou...  27.8 us
    ppermute x16, waiting for transfers between devices, shifted(): lax.ppermute(value, axis, [(i, (i + distance) % count) for i in range(cou...  13.7 us
    all_to_all x1, starting transfers between devices, on_device(): lax.all_to_all(payload, axes, split_axis=0, concat_axis=0, tiled=True)  7.33 us
    ppermute x2, starting transfers between devices, send_rows(): lax.ppermute(bottom, axes, swap(0))  7 us
    all_to_all x1, waiting for transfers between devices, on_device(): lax.all_to_all(answer, axes, split_axis=0, concat_axis=0, tiled=True)  6.07 us
    pallas_call x1, Pallas kernels, on_device(): pl.pallas_call(early_kernel, out_shape=edge_shapes(state_channels + ocean...  5.38 us
  transfers between devices with their start and end apart: 23, of which 8 were waited for; matrix products, arithmetic and copies ran while one was open for 5% of the time, Pallas kernels for 26%

profile of v1, /device:TPU:0, one launch (start us, length us, event | category | flops | bytes accessed | tf_op | source)
XLA Modules:
  0.0 160.8 jit_solution(8028385158555844188)
XLA Ops:
  0.6 1.6 copy-done.5
  4.9 1.5 shard_map.122
  6.4 7.3 %all-to-all-start = ((bf16[32,8,2176]{2,1,0:T(8,128)(2,1)}), bf16[32,8,2176]{2,1,0:T(8,128)(2,1)S(1)}, u32[]{:S(2)}, u32[]{:S(2)}) async-start(bf16[32,8,2176]{2,1,0:T(8,128)(2,1)} %bitcast.7), calls=%async_computation | async-start | bytes 2228224 | tf_op jit(solution)/shard_map/all_to_all | solution.py:582
  14.5 5.0 %copy.31 = bf16[128,128,128]{2,0,1:T(8,128)(2,1)S(1)} copy(bf16[128,128,128]{2,1,0:T(8,128)(2,1)} %surface.3) | data formatting | bytes 8388608 | tf_op args[0]
  19.6 1.3 fusion.ocean.refs_1_.refs_6_
  20.9 0.7 copy-done.1
  21.6 5.4 %shard_map.123 = (bf16[192,128]{1,0:T(8,128)(2,1)S(1)}, bf16[192,128]{1,0:T(8,128)(2,1)S(1)}, bf16[192,128]{1,0:T(8,128)(2,1)S(1)}, bf16[192,128]{1,0:T(8,128)(2,1)S(1)}) custom-call(s32[1,1]{1,0:T(1,128)S(6)} %copy.32.turn.refs_0_, bf16[128,128,128]{2,1,0:T(8,128)(2,1)S(1)} %bitcast.21, bf16[128,64,128]{2,1,0:T(8,128)(2,1)S(1)} %fusion.ocean.refs_1_.refs_6_), custom_call_target="tpu_custom_call" | custom-call | flops 6442450944 | tf_op jit(solution)/shard_map/pallas_call | solution.py:587
  27.0 1.8 %collective-permute-start = (bf16[192,128]{1,0:T(8,128)(2,1)S(1)}, bf16[192,128]{1,0:T(8,128)(2,1)S(1)}, u32[]{:S(2)}, u32[]{:S(2)}) collective-permute-start(bf16[192,128]{1,0:T(8,128)(2,1)S(1)} %get-tuple-element.93), channel_id=1, source_target_pairs={{0,8},{8,16},{16,24},{24,0},{1,9},{9,17},{17,25},{25,1},{2,10},{10... | collective-permute-start | bytes 147464 | tf_op jit(solution)/shard_map/ppermute | solution.py:458
  29.5 5.5 %collective-permute-start.1 = (bf16[192,128]{1,0:T(8,128)(2,1)S(1)}, bf16[192,128]{1,0:T(8,128)(2,1)S(1)}, u32[]{:S(2)}, u32[]{:S(2)}) collective-permute-start(bf16[192,128]{1,0:T(8,128)(2,1)S(1)} %get-tuple-element.94), channel_id=1, source_target_pairs={{0,24},{8,0},{16,8},{24,16},{1,25},{9,1},{17,9},{25,17},{2,26},{10... | collective-permute-start | bytes 147464 | tf_op jit(solution)/shard_map/ppermute | solution.py:458
  35.1 2.2 %copy-done = bf16[128,128,128]{2,1,0:T(8,128)(2,1)S(1)} copy-done((bf16[128,128,128]{2,1,0:T(8,128)(2,1)S(1)}, bf16[128,128,128]{2,1,0:T(8,128)(2,1)}, u32[]{:S(2)}) %copy-start) | copy-done | bytes 4194328
  37.9 0.8 copy-done.9
  38.7 2.1 %copy.23.refs_0_ = bf16[9,128,144]{2,1,0:T(8,128)(2,1)} copy(bf16[9,128,144]{1,2,0:T(8,128)(2,1)} %param.18) | data formatting | bytes 663552 | tf_op args[7]
  40.8 0.8 shard_map.124
  43.2 3.2 %collective-permute-start.4 = (bf16[192,256]{1,0:T(8,128)(2,1)S(1)}, bf16[192,256]{1,0:T(8,128)(2,1)S(1)}, u32[]{:S(2)}, u32[]{:S(2)}) collective-permute-start(bf16[192,256]{1,0:T(8,128)(2,1)S(1)} %get-tuple-element.100), channel_id=1, source_target_pairs={{0,7},{1,0},{2,1},{3,2},{4,3},{5,4},{6,5},{7,6},{8,15},{9,8},{10,9... | collective-permute-start | bytes 294920 | tf_op jit(solution)/shard_map/ppermute | solution.py:458
  46.6 0.7 copy-done.22
  47.3 0.7 copy-done.24
  48.8 1.0 copy-done.10
  50.3 1.0 copy-done.7
  51.3 3.9 %all-to-all-start.1 = ((bf16[32,8,2048]{2,1,0:T(8,128)(2,1)}), bf16[32,8,2048]{2,1,0:T(8,128)(2,1)}, u32[]{:S(2)}, u32[]{:S(2)}) async-start(bf16[32,8,2048]{2,1,0:T(8,128)(2,1)} %bitcast.28), calls=%async_computation.1 | async-start | bytes 2097152 | tf_op jit(solution)/shard_map/all_to_all | solution.py:643
  55.2 2.7 %shard_map.129 = (f32[128,16,128]{2,1,0:T(8,128)S(1)}, bf16[16,128]{1,0:T(8,128)(2,1)S(1)}, bf16[16,128]{1,0:T(8,128)(2,1)S(1)}, bf16[16,128]{1,0:T(8,128)(2,1)S(1)}, bf16[16,128]{1,0:T(8,128)(2,1)S(1)}) custom-call(s32[1,1]{1,0:T(1,128)S(6)} %copy.32.turn.refs_0_, bf16[256,2176]{1,0:T(8,128)(2,1)S(1)} %bitcast.27), custom_call_target="tpu_custom_call" | custom-call | flops 3221225472 | tf_op jit(solution)/shard_map/pallas_call | solution.py:644
  57.9 1.0 copy-done.28
  58.9 1.5 collective-permute-start.7
  60.4 1.4 collective-permute-start.8
  61.9 1.6 collective-permute-done.7.refs_0_
  63.4 0.7 collective-permute-done.8.refs_1_
  64.8 3.4 %collective-permute-start.10 = (bf16[16,256]{1,0:T(8,128)(2,1)S(1)}, bf16[16,256]{1,0:T(8,128)(2,1)S(1)}, u32[]{:S(2)}, u32[]{:S(2)}) collective-permute-start(bf16[16,256]{1,0:T(8,128)(2,1)S(1)} %get-tuple-element.127), channel_id=1, source_target_pairs={{0,7},{1,0},{2,1},{3,2},{4,3},{5,4},{6,5},{7,6},{8,15},{9,8},{10,9... | collective-permute-start | bytes 24584 | tf_op jit(solution)/shard_map/ppermute | solution.py:458
  68.2 4.7 %collective-permute-done.10.refs_7_ = bf16[16,256]{1,0:T(8,128)(2,1)S(1)} collective-permute-done((bf16[16,256]{1,0:T(8,128)(2,1)S(1)}, bf16[16,256]{1,0:T(8,128)(2,1)S(1)}, u32[]{:S(2)}, u32[]{:S(2)}) %collective-permute-start.10) | collective-permute-done | bytes 8224 | tf_op jit(solution)/shard_map/ppermute | solution.py:458
  72.9 3.4 %collective-permute-done.9.refs_6_ = bf16[16,256]{1,0:T(8,128)(2,1)S(1)} collective-permute-done((bf16[16,256]{1,0:T(8,128)(2,1)S(1)}, bf16[16,256]{1,0:T(8,128)(2,1)S(1)}, u32[]{:S(2)}, u32[]{:S(2)}) %collective-permute-start.9) | collective-permute-done | bytes 8224 | tf_op jit(solution)/shard_map/ppermute | solution.py:458
  76.7 6.1 %all-to-all-done.1 = bf16[32,8,2048]{2,1,0:T(8,128)(2,1)} async-done(((bf16[32,8,2048]{2,1,0:T(8,128)(2,1)}), bf16[32,8,2048]{2,1,0:T(8,128)(2,1)}, u32[]{:S(2)}, u32[]{:S(2)}) %all-to-all-start.1) | async-done | bytes 1048608 | tf_op jit(solution)/shard_map/all_to_all | solution.py:643
  82.8 3.8 %shard_map.128 = (f32[128,16,128]{2,1,0:T(8,128)S(1)}, bf16[16,128]{1,0:T(8,128)(2,1)S(1)}, bf16[16,128]{1,0:T(8,128)(2,1)S(1)}, bf16[16,128]{1,0:T(8,128)(2,1)S(1)}, bf16[16,128]{1,0:T(8,128)(2,1)S(1)}) custom-call(s32[1,2]{1,0:T(1,128)S(1)} %add_bitcast_fusion.place.refs_0_, s32[1,128]{1,0:T(1,128)S(1)} %bitcast.33, bf16[256,2048]{1,0:T(8,128)(2,1)} %bitcast.13.returned), custom_call_target="tpu_custom_call" | custom-call | flops 3221225472 | tf_op jit(solution)/shard_map/pallas_call | solution.py:653
  87.2 3.3 %collective-permute-start.6 = (bf16[16,128]{1,0:T(8,128)(2,1)S(1)}, bf16[16,128]{1,0:T(8,128)(2,1)S(1)}, u32[]{:S(2)}, u32[]{:S(2)}) collective-permute-start(bf16[16,128]{1,0:T(8,128)(2,1)S(1)} %get-tuple-element.111), channel_id=1, source_target_pairs={{0,8},{1,9},{2,10},{3,11},{4,12},{5,13},{6,14},{7,15},{8,0},{9,1},... | collective-permute-start | bytes 12296 | tf_op jit(solution)/shard_map/ppermute | solution.py:478
  90.6 12.5 %shard_map.132 = (bf16[128,128,128]{2,1,0:T(8,128)(2,1)S(1)}, bf16[128,128]{1,0:T(8,128)(2,1)S(1)}, bf16[128,128]{1,0:T(8,128)(2,1)S(1)}, bf16[128,128]{1,0:T(8,128)(2,1)S(1)}, bf16[128,128]{1,0:T(8,128)(2,1)S(1)}) custom-call(s32[1,1]{1,0:T(1,128)S(6)} %copy.32.turn.refs_0_, bf16[128,128,128]{2,1,0:T(8,128)(2,1)S(1)} %bitcast.22, ...), custom_call_target="tpu_custom_call" | custom-call | flops 12867427328 | tf_op jit(solution)/shard_map/pallas_call | solution.py:444
  103.1 0.7 shard_map.134
  103.8 3.5 %collective-permute-start.14 = (bf16[16,256]{1,0:T(8,128)(2,1)S(1)}, bf16[16,256]{1,0:T(8,128)(2,1)S(1)}, u32[]{:S(2)}, u32[]{:S(2)}) collective-permute-start(bf16[16,256]{1,0:T(8,128)(2,1)S(1)} %get-tuple-element.149), channel_id=1, source_target_pairs={{0,7},{1,0},{2,1},{3,2},{4,3},{5,4},{6,5},{7,6},{8,15},{9,8},{10,9... | collective-permute-start | bytes 24584 | tf_op jit(solution)/shard_map/ppermute | solution.py:458
  107.4 2.9 %collective-permute-start.12 = (bf16[128,128]{1,0:T(8,128)(2,1)S(1)}, bf16[128,128]{1,0:T(8,128)(2,1)S(1)}, u32[]{:S(2)}, u32[]{:S(2)}) collective-permute-start(bf16[128,128]{1,0:T(8,128)(2,1)S(1)} %get-tuple-element.137), channel_id=1, source_target_pairs={{0,24},{8,0},{16,8},{24,16},{1,25},{9,1},{17,9},{25,17},{2,26},{10... | collective-permute-start | bytes 98312 | tf_op jit(solution)/shard_map/ppermute | solution.py:458
  110.4 1.7 %collective-permute-done.11.refs_0_ = bf16[128,128]{1,0:T(8,128)(2,1)S(1)} collective-permute-done((bf16[128,128]{1,0:T(8,128)(2,1)S(1)}, bf16[128,128]{1,0:T(8,128)(2,1)S(1)}, u32[]{:S(2)}, u32[]{:S(2)}) %collective-permute-start.11) | collective-permute-done | bytes 32800 | tf_op jit(solution)/shard_map/ppermute | solution.py:458
  113.4 7.5 %shard_map.136 = (bf16[128,64,128]{2,1,0:T(8,128)(2,1)S(1)}, bf16[64,128]{1,0:T(8,128)(2,1)S(1)}, bf16[64,128]{1,0:T(8,128)(2,1)S(1)}, bf16[64,128]{1,0:T(8,128)(2,1)S(1)}, bf16[64,128]{1,0:T(8,128)(2,1)S(1)}) custom-call(s32[1,2]{1,0:T(1,128)S(1)} %add_bitcast_fusion.place.refs_0_, bf16[128,64,128]{2,1,0:T(8,128)(2,1)S(1)} %fusion.ocean.refs_1_.refs_6_, ...), custom_call_target="tpu_custom_call" | custom-call | flops 3216856832 | tf_op jit(solution)/shard_map/pallas_call | solution.py:444
  120.9 1.3 copy-done.20
  122.2 0.8 collective-permute-start.15
  123.0 3.7 %collective-permute-start.16 = (bf16[64,128]{1,0:T(8,128)(2,1)S(1)}, bf16[64,128]{1,0:T(8,128)(2,1)S(1)}, u32[]{:S(2)}, u32[]{:S(2)}) collective-permute-start(bf16[64,128]{1,0:T(8,128)(2,1)S(1)} %get-tuple-element.155), channel_id=1, source_target_pairs={{0,8},{1,9},{2,10},{3,11},{4,12},{5,13},{6,14},{7,15},{8,0},{9,1},... | collective-permute-start | bytes 49160 | tf_op jit(solution)/shard_map/ppermute | solution.py:478
  127.1 11.1 %shard_map.138 = bf16[128,128,128]{2,1,0:T(8,128)(2,1)S(1)} custom-call(s32[1,1]{1,0:T(1,128)S(6)} %copy.32.turn.refs_0_, bf16[128,128,128]{2,1,0:T(8,128)(2,1)S(1)} %get-tuple-element.158.refs_1_, f32[2,128,256]{2,1,0:T(8,128)S(1)} %get-tuple-element.162.refs_2_, f32[128,128]{1,0:T(8,128)S(1)} %get-tuple-element.163.refs_3_, ...), custom_call_target="tpu_custom_call" | custom-call | flops 9650570240 | tf_op jit(solution)/shard_map/pallas_call | solution.py:444
  138.3 2.0 %copy-done.3 = bf16[128,128,128]{2,1,0:T(8,128)(2,1)} copy-done((bf16[128,128,128]{2,1,0:T(8,128)(2,1)}, bf16[128,128,128]{2,1,0:T(8,128)(2,1)S(1)}, u32[]{:S(2)}) %copy-start.3) | copy-done | bytes 4194328
  140.3 0.8 shard_map.139
  141.1 3.5 %collective-permute-start.20 = (bf16[64,256]{1,0:T(8,128)(2,1)S(1)}, bf16[64,256]{1,0:T(8,128)(2,1)S(1)}, u32[]{:S(2)}, u32[]{:S(2)}) collective-permute-start(bf16[64,256]{1,0:T(8,128)(2,1)S(1)} %get-tuple-element.173), channel_id=1, source_target_pairs={{0,7},{1,0},{2,1},{3,2},{4,3},{5,4},{6,5},{7,6},{8,15},{9,8},{10,9... | collective-permute-start | bytes 98312 | tf_op jit(solution)/shard_map/ppermute | solution.py:458
  144.8 1.5 collective-permute-done.19.refs_2_
  146.5 6.9 %shard_map.141 = bf16[128,64,128]{2,1,0:T(8,128)(2,1)S(1)} custom-call(s32[1,2]{1,0:T(1,128)S(1)} %add_bitcast_fusion.place.refs_0_, bf16[128,64,128]{2,1,0:T(8,128)(2,1)S(1)} %copy-done.21, f32[2,64,256]{2,1,0:T(8,128)S(1)} %get-tuple-element.180.refs_2_, f32[64,128]{1,0:T(8,128)S(1)} %get-tuple-element.181.refs_3_, ...), custom_call_target="tpu_custom_call" | custom-call | flops 3216856832 | tf_op jit(solution)/shard_map/pallas_call | solution.py:444
  153.4 2.7 %copy.26 = bf16[64,128,128]{2,1,0:T(8,128)(2,1)} copy(bf16[64,128,128]{2,0,1:T(8,128)(2,1)S(1)} %bitcast.25) | data formatting | bytes 4194304
  156.1 4.7 %copy.25 = bf16[128,128,128]{2,1,0:T(8,128)(2,1)} copy(bf16[128,128,128]{2,0,1:T(8,128)(2,1)S(1)} %bitcast.24) | data formatting | bytes 8388608
  (98 shorter events, 11.1 us)
Async XLA Ops:
  0.6 1.6 copy-start.5
  6.4 7.3 %copy-start.12 = (s32[128,4]{0,1:T(4,128)S(1)}, s32[128,4]{0,1:T(4,128)}, u32[]{:S(2)}) copy-start(s32[128,4]{0,1:T(4,128)} %param.13) | copy-start | bytes 6148
  6.4 42.4 %all-to-all-start = ((bf16[32,8,2176]{2,1,0:T(8,128)(2,1)}), bf16[32,8,2176]{2,1,0:T(8,128)(2,1)S(1)}, u32[]{:S(2)}, u32[]{:S(2)}) async-start(bf16[32,8,2176]{2,1,0:T(8,128)(2,1)} %bitcast.7), calls=%async_computation | async-start | bytes 2228224 | tf_op jit(solution)/shard_map/all_to_all | solution.py:582
  14.5 5.1 %copy-start.6 = (bf16[64,128,128]{2,1,0:T(8,128)(2,1)S(1)}, bf16[64,128,128]{2,1,0:T(8,128)(2,1)}, u32[]{:S(2)}) copy-start(bf16[64,128,128]{2,1,0:T(8,128)(2,1)} %surface.2) | copy-start | bytes 6291460
  19.6 2.0 %copy-start.1 = (bf16[128,128,128]{2,0,1:T(8,128)(2,1)}, bf16[128,128,128]{2,0,1:T(8,128)(2,1)S(1)}, u32[]{:S(2)}) copy-start(bf16[128,128,128]{2,0,1:T(8,128)(2,1)S(1)} %copy.31) | copy-start | bytes 12582916
  27.0 13.8 %collective-permute-start = (bf16[192,128]{1,0:T(8,128)(2,1)S(1)}, bf16[192,128]{1,0:T(8,128)(2,1)S(1)}, u32[]{:S(2)}, u32[]{:S(2)}) collective-permute-start(bf16[192,128]{1,0:T(8,128)(2,1)S(1)} %get-tuple-element.93), channel_id=1, source_target_pairs={{0,8},{8,16},{16,24},{24,0},{1,9},{9,17},{17,25},{25,1},{2,10},{10... | collective-permute-start | bytes 147464 | tf_op jit(solution)/shard_map/ppermute | solution.py:458
  28.8 12.0 %collective-permute-start.2 = (bf16[64,128]{1,0:T(8,128)(2,1)S(1)}, bf16[64,128]{1,0:T(8,128)(2,1)S(1)}, u32[]{:S(2)}, u32[]{:S(2)}) collective-permute-start(bf16[64,128]{1,0:T(8,128)(2,1)S(1)} %slice.3), channel_id=1, source_target_pairs={{24,31},{25,30},{26,29},{27,28},{28,27},{29,26},{30,25},{31,24}} | collective-permute-start | bytes 49160 | tf_op jit(solution)/shard_map/ppermute | solution.py:481
  29.5 11.3 %collective-permute-start.1 = (bf16[192,128]{1,0:T(8,128)(2,1)S(1)}, bf16[192,128]{1,0:T(8,128)(2,1)S(1)}, u32[]{:S(2)}, u32[]{:S(2)}) collective-permute-start(bf16[192,128]{1,0:T(8,128)(2,1)S(1)} %get-tuple-element.94), channel_id=1, source_target_pairs={{0,24},{8,0},{16,8},{24,16},{1,25},{9,1},{17,9},{25,17},{2,26},{10... | collective-permute-start | bytes 147464 | tf_op jit(solution)/shard_map/ppermute | solution.py:458
  35.1 2.2 %copy-start = (bf16[128,128,128]{2,1,0:T(8,128)(2,1)S(1)}, bf16[128,128,128]{2,1,0:T(8,128)(2,1)}, u32[]{:S(2)}) copy-start(bf16[128,128,128]{2,1,0:T(8,128)(2,1)} %surface.3) | copy-start | bytes 12582916
  37.9 0.8 copy-start.9
  40.8 5.6 %copy-start.8 = (bf16[9,128,144]{2,1,0:T(8,128)(2,1)S(1)}, bf16[9,128,144]{2,1,0:T(8,128)(2,1)}, u32[]{:S(2)}) copy-start(bf16[9,128,144]{2,1,0:T(8,128)(2,1)} %copy.23.refs_0_) | copy-start | bytes 995332
  40.8 5.6 %copy-start.13 = (bf16[9,128,128]{2,1,0:T(8,128)(2,1)S(1)}, bf16[9,128,128]{2,1,0:T(8,128)(2,1)}, u32[]{:S(2)}) copy-start(bf16[9,128,128]{2,1,0:T(8,128)(2,1)} %refs_1_.1) | copy-start | bytes 884740
  40.8 5.6 %copy-start.14 = (bf16[9,64,80]{2,1,0:T(8,128)(2,1)S(1)}, bf16[9,64,80]{2,1,0:T(8,128)(2,1)}, u32[]{:S(2)}) copy-start(bf16[9,64,80]{2,1,0:T(8,128)(2,1)} %refs_2_.1) | copy-start | bytes 276484
  40.8 5.6 %copy-start.15 = (bf16[9,64,64]{2,1,0:T(8,128)(2,1)S(1)}, bf16[9,64,64]{2,1,0:T(8,128)(2,1)}, u32[]{:S(2)}) copy-start(bf16[9,64,64]{2,1,0:T(8,128)(2,1)} %refs_3_.1) | copy-start | bytes 221188
  42.8 6.0 %collective-permute-start.3 = (bf16[192,256]{1,0:T(8,128)(2,1)S(1)}, bf16[192,256]{1,0:T(8,128)(2,1)S(1)}, u32[]{:S(2)}, u32[]{:S(2)}) collective-permute-start(bf16[192,256]{1,0:T(8,128)(2,1)S(1)} %get-tuple-element.99), channel_id=1, source_target_pairs={{0,1},{1,2},{2,3},{3,4},{4,5},{5,6},{6,7},{7,0},{8,9},{9,10},{10,1... | collective-permute-start | bytes 294920 | tf_op jit(solution)/shard_map/ppermute | solution.py:458
  43.2 5.6 %collective-permute-start.4 = (bf16[192,256]{1,0:T(8,128)(2,1)S(1)}, bf16[192,256]{1,0:T(8,128)(2,1)S(1)}, u32[]{:S(2)}, u32[]{:S(2)}) collective-permute-start(bf16[192,256]{1,0:T(8,128)(2,1)S(1)} %get-tuple-element.100), channel_id=1, source_target_pairs={{0,7},{1,0},{2,1},{3,2},{4,3},{5,4},{6,5},{7,6},{8,15},{9,8},{10,9... | collective-permute-start | bytes 294920 | tf_op jit(solution)/shard_map/ppermute | solution.py:458
  48.8 1.0 copy-start.10
  50.3 1.0 copy-start.7
  51.3 31.5 %all-to-all-start.1 = ((bf16[32,8,2048]{2,1,0:T(8,128)(2,1)}), bf16[32,8,2048]{2,1,0:T(8,128)(2,1)}, u32[]{:S(2)}, u32[]{:S(2)}) async-start(bf16[32,8,2048]{2,1,0:T(8,128)(2,1)} %bitcast.28), calls=%async_computation.1 | async-start | bytes 2097152 | tf_op jit(solution)/shard_map/all_to_all | solution.py:643
  57.9 1.0 copy-start.28
  58.9 17.3 %copy-start.31 = (bf16[192,128]{1,0:T(8,128)(2,1)S(1)}, bf16[192,128]{1,0:T(8,128)(2,1)}, u32[]{:S(2)}) copy-start(bf16[192,128]{1,0:T(8,128)(2,1)} %copy-done.30) | copy-start | bytes 147460
  58.9 17.3 %copy-start.33 = (bf16[192,128]{1,0:T(8,128)(2,1)S(1)}, bf16[192,128]{1,0:T(8,128)(2,1)}, u32[]{:S(2)}) copy-start(bf16[192,128]{1,0:T(8,128)(2,1)} %copy-done.32) | copy-start | bytes 147460
  58.9 4.5 %collective-permute-start.7 = (bf16[16,128]{1,0:T(8,128)(2,1)S(1)}, bf16[16,128]{1,0:T(8,128)(2,1)S(1)}, u32[]{:S(2)}, u32[]{:S(2)}) collective-permute-start(bf16[16,128]{1,0:T(8,128)(2,1)S(1)} %get-tuple-element.120), channel_id=1, source_target_pairs={{0,8},{8,16},{16,24},{24,0},{1,9},{9,17},{17,25},{25,1},{2,10},{10... | collective-permute-start | bytes 12296 | tf_op jit(solution)/shard_map/ppermute | solution.py:458
  60.4 3.7 %collective-permute-start.8 = (bf16[16,128]{1,0:T(8,128)(2,1)S(1)}, bf16[16,128]{1,0:T(8,128)(2,1)S(1)}, u32[]{:S(2)}, u32[]{:S(2)}) collective-permute-start(bf16[16,128]{1,0:T(8,128)(2,1)S(1)} %get-tuple-element.121), channel_id=1, source_target_pairs={{0,24},{8,0},{16,8},{24,16},{1,25},{9,1},{17,9},{25,17},{2,26},{10... | collective-permute-start | bytes 12296 | tf_op jit(solution)/shard_map/ppermute | solution.py:458
  64.8 18.0 %copy-start.19 = (s32[128,1]{0,1:T(1,128)S(1)}, s32[128,1]{0,1:T(1,128)}, u32[]{:S(2)}) copy-start(s32[128,1]{0,1:T(1,128)} %param.15) | copy-start | bytes 1540
  64.8 8.1 %collective-permute-start.10 = (bf16[16,256]{1,0:T(8,128)(2,1)S(1)}, bf16[16,256]{1,0:T(8,128)(2,1)S(1)}, u32[]{:S(2)}, u32[]{:S(2)}) collective-permute-start(bf16[16,256]{1,0:T(8,128)(2,1)S(1)} %get-tuple-element.127), channel_id=1, source_target_pairs={{0,7},{1,0},{2,1},{3,2},{4,3},{5,4},{6,5},{7,6},{8,15},{9,8},{10,9... | collective-permute-start | bytes 24584 | tf_op jit(solution)/shard_map/ppermute | solution.py:458
  68.2 8.1 %collective-permute-start.9 = (bf16[16,256]{1,0:T(8,128)(2,1)S(1)}, bf16[16,256]{1,0:T(8,128)(2,1)S(1)}, u32[]{:S(2)}, u32[]{:S(2)}) collective-permute-start(bf16[16,256]{1,0:T(8,128)(2,1)S(1)} %get-tuple-element.126), channel_id=1, source_target_pairs={{0,1},{1,2},{2,3},{3,4},{4,5},{5,6},{6,7},{7,0},{8,9},{9,10},{10,1... | collective-permute-start | bytes 24584 | tf_op jit(solution)/shard_map/ppermute | solution.py:458
  82.7 7.8 %copy-start.2 = (bf16[128,128,128]{2,0,1:T(8,128)(2,1)S(1)}, bf16[128,128,128]{2,0,1:T(8,128)(2,1)}, u32[]{:S(2)}) copy-start(bf16[128,128,128]{2,0,1:T(8,128)(2,1)} %copy-done.1) | copy-start | bytes 12582916
  82.7 7.8 %copy-start.23 = (bf16[384,512]{1,0:T(8,128)(2,1)S(1)}, bf16[384,512]{1,0:T(8,128)(2,1)}, u32[]{:S(2)}) copy-start(bf16[384,512]{1,0:T(8,128)(2,1)} %copy-done.22) | copy-start | bytes 1179652
  82.8 7.8 %copy-start.29 = (f32[128,16,128]{2,1,0:T(8,128)S(1)}, f32[128,16,128]{2,1,0:T(8,128)}, u32[]{:S(2)}) copy-start(f32[128,16,128]{2,1,0:T(8,128)} %copy-done.28) | copy-start | bytes 3145732
  86.6 16.5 %collective-permute-start.5 = (bf16[16,128]{1,0:T(8,128)(2,1)S(1)}, bf16[16,128]{1,0:T(8,128)(2,1)S(1)}, u32[]{:S(2)}, u32[]{:S(2)}) collective-permute-start(bf16[16,128]{1,0:T(8,128)(2,1)S(1)} %get-tuple-element.110), channel_id=1, source_target_pairs={{8,16},{9,17},{10,18},{11,19},{12,20},{13,21},{14,22},{15,23},{16,... | collective-permute-start | bytes 12296 | tf_op jit(solution)/shard_map/ppermute | solution.py:478
  87.2 15.8 %collective-permute-start.6 = (bf16[16,128]{1,0:T(8,128)(2,1)S(1)}, bf16[16,128]{1,0:T(8,128)(2,1)S(1)}, u32[]{:S(2)}, u32[]{:S(2)}) collective-permute-start(bf16[16,128]{1,0:T(8,128)(2,1)S(1)} %get-tuple-element.111), channel_id=1, source_target_pairs={{0,8},{1,9},{2,10},{3,11},{4,12},{5,13},{6,14},{7,15},{8,0},{9,1},... | collective-permute-start | bytes 12296 | tf_op jit(solution)/shard_map/ppermute | solution.py:478
  103.8 6.5 %collective-permute-start.13 = (bf16[16,256]{1,0:T(8,128)(2,1)S(1)}, bf16[16,256]{1,0:T(8,128)(2,1)S(1)}, u32[]{:S(2)}, u32[]{:S(2)}) collective-permute-start(bf16[16,256]{1,0:T(8,128)(2,1)S(1)} %get-tuple-element.148), channel_id=1, source_target_pairs={{0,1},{1,2},{2,3},{3,4},{4,5},{5,6},{6,7},{7,0},{8,9},{9,10},{10,1... | collective-permute-start | bytes 24584 | tf_op jit(solution)/shard_map/ppermute | solution.py:458
  103.8 6.5 %collective-permute-start.14 = (bf16[16,256]{1,0:T(8,128)(2,1)S(1)}, bf16[16,256]{1,0:T(8,128)(2,1)S(1)}, u32[]{:S(2)}, u32[]{:S(2)}) collective-permute-start(bf16[16,256]{1,0:T(8,128)(2,1)S(1)} %get-tuple-element.149), channel_id=1, source_target_pairs={{0,7},{1,0},{2,1},{3,2},{4,3},{5,4},{6,5},{7,6},{8,15},{9,8},{10,9... | collective-permute-start | bytes 24584 | tf_op jit(solution)/shard_map/ppermute | solution.py:458
  107.4 4.8 %collective-permute-start.11 = (bf16[128,128]{1,0:T(8,128)(2,1)S(1)}, bf16[128,128]{1,0:T(8,128)(2,1)S(1)}, u32[]{:S(2)}, u32[]{:S(2)}) collective-permute-start(bf16[128,128]{1,0:T(8,128)(2,1)S(1)} %get-tuple-element.136), channel_id=1, source_target_pairs={{0,8},{8,16},{16,24},{24,0},{1,9},{9,17},{17,25},{25,1},{2,10},{10... | collective-permute-start | bytes 98312 | tf_op jit(solution)/shard_map/ppermute | solution.py:458
  107.4 4.8 %collective-permute-start.12 = (bf16[128,128]{1,0:T(8,128)(2,1)S(1)}, bf16[128,128]{1,0:T(8,128)(2,1)S(1)}, u32[]{:S(2)}, u32[]{:S(2)}) collective-permute-start(bf16[128,128]{1,0:T(8,128)(2,1)S(1)} %get-tuple-element.137), channel_id=1, source_target_pairs={{0,24},{8,0},{16,8},{24,16},{1,25},{9,1},{17,9},{25,17},{2,26},{10... | collective-permute-start | bytes 98312 | tf_op jit(solution)/shard_map/ppermute | solution.py:458
  110.4 3.0 %copy-start.27 = (bf16[192,256]{1,0:T(8,128)(2,1)S(1)}, bf16[192,256]{1,0:T(8,128)(2,1)}, u32[]{:S(2)}) copy-start(bf16[192,256]{1,0:T(8,128)(2,1)} %copy-done.26) | copy-start | bytes 294916
  112.8 13.8 %collective-permute-start.18 = (bf16[128,256]{1,0:T(8,128)(2,1)S(1)}, bf16[128,256]{1,0:T(8,128)(2,1)S(1)}, u32[]{:S(2)}, u32[]{:S(2)}) collective-permute-start(bf16[128,256]{1,0:T(8,128)(2,1)S(1)} %get-tuple-element.140), channel_id=1, source_target_pairs={{0,7},{1,0},{2,1},{3,2},{4,3},{5,4},{6,5},{7,6},{8,15},{9,8},{10,9... | collective-permute-start | bytes 196616 | tf_op jit(solution)/shard_map/ppermute | solution.py:458
  113.1 13.6 %collective-permute-start.17 = (bf16[128,256]{1,0:T(8,128)(2,1)S(1)}, bf16[128,256]{1,0:T(8,128)(2,1)S(1)}, u32[]{:S(2)}, u32[]{:S(2)}) collective-permute-start(bf16[128,256]{1,0:T(8,128)(2,1)S(1)} %get-tuple-element.161), channel_id=1, source_target_pairs={{0,1},{1,2},{2,3},{3,4},{4,5},{5,6},{6,7},{7,0},{8,9},{9,10},{10,1... | collective-permute-start | bytes 196616 | tf_op jit(solution)/shard_map/ppermute | solution.py:458
  120.9 1.3 copy-start.20
  122.2 4.9 %copy-start.25 = (bf16[384,384]{1,0:T(8,128)(2,1)S(1)}, bf16[384,384]{1,0:T(8,128)(2,1)}, u32[]{:S(2)}) copy-start(bf16[384,384]{1,0:T(8,128)(2,1)} %copy-done.24) | copy-start | bytes 884740
  122.2 18.1 %collective-permute-start.15 = (bf16[64,128]{1,0:T(8,128)(2,1)S(1)}, bf16[64,128]{1,0:T(8,128)(2,1)S(1)}, u32[]{:S(2)}, u32[]{:S(2)}) collective-permute-start(bf16[64,128]{1,0:T(8,128)(2,1)S(1)} %get-tuple-element.154), channel_id=1, source_target_pairs={{8,16},{9,17},{10,18},{11,19},{12,20},{13,21},{14,22},{15,23},{16,... | collective-permute-start | bytes 49160 | tf_op jit(solution)/shard_map/ppermute | solution.py:478
  123.0 17.3 %collective-permute-start.16 = (bf16[64,128]{1,0:T(8,128)(2,1)S(1)}, bf16[64,128]{1,0:T(8,128)(2,1)S(1)}, u32[]{:S(2)}, u32[]{:S(2)}) collective-permute-start(bf16[64,128]{1,0:T(8,128)(2,1)S(1)} %get-tuple-element.155), channel_id=1, source_target_pairs={{0,8},{1,9},{2,10},{3,11},{4,12},{5,13},{6,14},{7,15},{8,0},{9,1},... | collective-permute-start | bytes 49160 | tf_op jit(solution)/shard_map/ppermute | solution.py:478
  138.3 2.0 %copy-start.3 = (bf16[128,128,128]{2,1,0:T(8,128)(2,1)}, bf16[128,128,128]{2,1,0:T(8,128)(2,1)S(1)}, u32[]{:S(2)}) copy-start(bf16[128,128,128]{2,1,0:T(8,128)(2,1)S(1)} %shard_map.138) | copy-start | bytes 12582916
  141.1 5.2 %collective-permute-start.19 = (bf16[64,256]{1,0:T(8,128)(2,1)S(1)}, bf16[64,256]{1,0:T(8,128)(2,1)S(1)}, u32[]{:S(2)}, u32[]{:S(2)}) collective-permute-start(bf16[64,256]{1,0:T(8,128)(2,1)S(1)} %get-tuple-element.172), channel_id=1, source_target_pairs={{0,1},{1,2},{2,3},{3,4},{4,5},{5,6},{6,7},{7,0},{8,9},{9,10},{10,1... | collective-permute-start | bytes 98312 | tf_op jit(solution)/shard_map/ppermute | solution.py:458
  141.1 5.2 %collective-permute-start.20 = (bf16[64,256]{1,0:T(8,128)(2,1)S(1)}, bf16[64,256]{1,0:T(8,128)(2,1)S(1)}, u32[]{:S(2)}, u32[]{:S(2)}) collective-permute-start(bf16[64,256]{1,0:T(8,128)(2,1)S(1)} %get-tuple-element.173), channel_id=1, source_target_pairs={{0,7},{1,0},{2,1},{3,2},{4,3},{5,4},{6,5},{7,6},{8,15},{9,8},{10,9... | collective-permute-start | bytes 98312 | tf_op jit(solution)/shard_map/ppermute | solution.py:458
  144.8 1.7 %copy-start.21 = (bf16[128,64,128]{2,1,0:T(8,128)(2,1)S(1)}, bf16[128,64,128]{2,1,0:T(8,128)(2,1)}, u32[]{:S(2)}) copy-start(bf16[128,64,128]{2,1,0:T(8,128)(2,1)} %copy-done.20) | copy-start | bytes 6291460
  153.4 2.7 %copy-start.4 = (bf16[128,128,128]{2,1,0:T(8,128)(2,1)S(1)}, bf16[128,128,128]{2,1,0:T(8,128)(2,1)}, u32[]{:S(2)}) copy-start(bf16[128,128,128]{2,1,0:T(8,128)(2,1)} %copy-done.3) | copy-start | bytes 12582916
  (9 other events, 6.0 us)

commit v2 on v1

--- a/solution.py
+++ b/solution.py
@@ -453,6 +453,287 @@
     return (result[0], result[1:]) if base is None else result[0]
 
 
+def spans_of(sources):
+    spans, low = [], 0
+    for source in sources:
+        spans.append((low, low + source.shape[1]))
+        low += source.shape[1]
+    return spans
+
+
+def main_kernel(parts, mode, *refs):
+    refs = list(refs)
+    sources = [refs.pop(0) for _ in range(parts)]
+    taps = refs.pop(0)
+    base = refs.pop(0) if mode != "gelu" else None
+    mask = refs.pop(0) if mode == "masked" else None
+    out, edge_left, edge_right, stacked, sums = refs
+    rows, outputs, cols = out.shape
+    spans = spans_of(sources)
+    channels = spans[-1][1]
+    lanes = iota((channels, cols), 1)
+    out_lanes = iota((outputs, cols), 1)
+
+    def place(slot, half, low, high, shifted):
+        for b, value in enumerate(shifted):
+            at = 3 * low + b * (high - low)
+            stacked[slot, at : at + high - low, half * cols : (half + 1) * cols] = value.astype(
+                BF16
+            )
+
+    def inner(slot, half, y):
+        for source, (low, high) in zip(sources, spans):
+            row = source[y].astype(F32)
+            shifts = (
+                jnp.where(lanes[low:high] == 0, 0.0, pltpu.roll(row, 1, 1)),
+                row,
+                jnp.where(lanes[low:high] == cols - 1, 0.0, pltpu.roll(row, cols - 1, 1)),
+            )
+            place(slot, half, low, high, shifts)
+
+    def end(slot, half):
+        for low, high in spans:
+            place(slot, half, low, high, [jnp.zeros((high - low, cols), F32)] * 3)
+
+    def emit(y, value):
+        result = value
+        if mode == "gelu":
+            result = jax.nn.gelu(value, approximate=True)
+        else:
+            result = base[y].astype(F32) + value
+            if mode == "masked":
+                result = result * mask[y]
+        out[y] = result.astype(BF16)
+        return value
+
+    def product(slot):
+        sums[slot] = dot(taps[...], stacked[slot])
+
+    def tap(slot, a, half):
+        return sums[slot, a * outputs : (a + 1) * outputs, half * cols : (half + 1) * cols]
+
+    def finish(slot, j):
+        was = (slot + 3) % 4
+        rows_of = [
+            (2 * j - 2, tap(was, 0, 0) + tap(was, 1, 1) + tap(slot, 2, 0)),
+            (2 * j - 1, tap(was, 0, 1) + tap(slot, 1, 0) + tap(slot, 2, 1)),
+        ]
+        return [(y, emit(y, value)) for y, value in rows_of]
+
+    def note(done):
+        first, last = edge_left[...], edge_right[...]
+        for y, value in done:
+            first = jnp.where(out_lanes == y, value[:, 0:1], first)
+            last = jnp.where(out_lanes == y, value[:, cols - 1 :], last)
+        edge_left[...] = first
+        edge_right[...] = last
+
+    def load(slot, j):
+        inner(slot, 0, 2 * j - 1)
+        inner(slot, 1, 2 * j)
+
+    spare = stacked.shape[1] - 3 * channels
+    if spare:
+        stacked[:, 3 * channels :, :] = jnp.zeros((stacked.shape[0], spare, 2 * cols), BF16)
+    edge_left[...] = jnp.zeros(edge_left.shape, F32)
+    edge_right[...] = jnp.zeros(edge_right.shape, F32)
+    pairs = rows // 2
+    assert pairs % 4 == 0 and pairs >= 8
+    end(3, 0)
+    inner(3, 1, 0)
+    load(0, 1)
+    load(1, 2)
+    product(3)
+    product(0)
+    product(1)
+    load(2, 3)
+    load(3, 4)
+
+    def half(j, now, other, final=False):
+        product(now)
+        done = finish(other, j - 2)
+        load(other, j + 2)
+        product(now + 1)
+        done += finish(other + 1, j - 1)
+        if final:
+            inner(other + 1, 0, rows - 1)
+            end(other + 1, 1)
+        else:
+            load(other + 1, j + 3)
+        note(done)
+
+    def step(i, _):
+        half(4 * i + 3, 2, 0)
+        half(4 * i + 5, 0, 2)
+        return 0
+
+    lax.fori_loop(0, (pairs - 8) // 4, step, 0)
+    half(pairs - 5, 2, 0)
+    half(pairs - 3, 0, 2, True)
+    product(2)
+    done = finish(0, pairs - 3)
+    product(3)
+    done += finish(1, pairs - 2)
+    note(done)
+    note(finish(2, pairs - 1) + finish(3, pairs))
+
+
+def convolve_alone(sources, taps, mode, base=None, mask=None):
+    rows, _, cols = sources[0].shape
+    outputs = taps.shape[0] // 3
+    operands = [*sources, taps]
+    operands += [value for value in (base, mask) if value is not None]
+    return pl.pallas_call(
+        partial(main_kernel, len(sources), mode),
+        out_shape=[jax.ShapeDtypeStruct((rows, outputs, cols), BF16)]
+        + [jax.ShapeDtypeStruct((outputs, rows), F32)] * 2,
+        in_specs=[VM] * len(operands),
+        out_specs=[VM] * 3,
+        scratch_shapes=[
+            pltpu.VMEM((4, taps.shape[1], 2 * cols), BF16),
+            pltpu.VMEM((4, taps.shape[0], 2 * cols), F32),
+        ],
+        cost_estimate=lasting(rows * outputs * taps.shape[1] / 700000),
+        compiler_params=SMALL,
+    )(*operands)
+
+
+def edge_kernel(parts, mode, where, *refs):
+    refs = list(refs)
+    main, side_left, side_right = [refs.pop(0) for _ in range(3)]
+    sources = [refs.pop(0) for _ in range(2 * parts)]
+    ends, left, right, taps = [refs.pop(0) for _ in range(4)]
+    base = refs.pop(0) if mode in ("add", "masked") else None
+    mask = refs.pop(0) if mode == "masked" else None
+    gelu = mode in ("turned", "plain")
+    out = refs.pop(0)
+    edges = [refs.pop(0) for _ in range(4)] if gelu else None
+    stacked = refs.pop(0)
+    rows, outputs, cols = out.shape
+    spans = spans_of(sources[:parts])
+    channels = spans[-1][1]
+    lanes = iota((channels, cols), 1)
+    out_lanes = iota((outputs, cols), 1)
+    if stacked.shape[1] > 3 * channels:
+        spare = stacked.shape[1] - 3 * channels
+        stacked[:, 3 * channels :, :] = jnp.zeros((stacked.shape[0], spare, 2 * cols), BF16)
+
+    def place(slot, half, low, high, shifted):
+        for b, value in enumerate(shifted):
+            at = 3 * low + b * (high - low)
+            stacked[slot, at : at + high - low, half * cols : (half + 1) * cols] = value.astype(
+                BF16
+            )
+
+    def end(slot, half, which):
+        for low, high in spans:
+            row = ends[which, low:high, :]
+            place(slot, half, low, high, [row[:, b : b + cols] for b in range(3)])
+
+    def inner(slot, half, late, at):
+        for number, (low, high) in enumerate(spans):
+            row = sources[number + parts * late][at].astype(F32)
+            y = (rows - 2) * late + at
+            before = pltpu.roll(left[low:high, :], (cols - y) % cols, 1)
+            after = pltpu.roll(right[low:high, :], cols - 1 - y, 1)
+            shifts = (
+                jnp.where(lanes[low:high] == 0, before, pltpu.roll(row, 1, 1)),
+                row,
+                jnp.where(lanes[low:high] == cols - 1, after, pltpu.roll(row, cols - 1, 1)),
+            )
+            place(slot, half, low, high, shifts)
+
+    end(0, 0, 0)
+    inner(1, 0, 0, 0)
+    inner(2, 0, 0, 1)
+    inner(0, 1, 1, 0)
+    inner(1, 1, 1, 1)
+    end(2, 1, 1)
+    for a, distance in enumerate((1, 0, cols - 1)):
+        for low, high in spans:
+            zero = jnp.zeros((high - low, cols), F32)
+            before, after = left[low:high, :], right[low:high, :]
+            if distance:
+                before, after = pltpu.roll(before, distance, 1), pltpu.roll(after, distance, 1)
+            place(3 + a, 0, low, high, (before, zero, zero))
+            place(3 + a, 1, low, high, (zero, zero, after))
+
+    def product(slot):
+        a = slot % 3
+        return dot(taps[a * outputs : (a + 1) * outputs, :], stacked[slot])
+
+    ended = product(0) + product(1) + product(2)
+    sided = product(3) + product(4) + product(5)
+    top, bottom = ended[:, :cols], ended[:, cols:]
+    first = side_left[...] + sided[:, :cols]
+    last = side_right[...] + sided[:, cols:]
+    if gelu:
+        top, bottom, first, last = [
+            jax.nn.gelu(value, approximate=True).astype(BF16).astype(F32)
+            for value in (top, bottom, first, last)
+        ]
+
+    def complete(y, value):
+        if gelu:
+            return value
+        value = base[y].astype(F32) + value
+        return value * mask[y] if mode == "masked" else value
+
+    def step(y, _):
+        before = pltpu.roll(first, lax.rem(cols - y, cols), 1)
+        after = pltpu.roll(last, cols - 1 - y, 1)
+        side = complete(y, jnp.where(out_lanes == 0, before, after))
+        inside = (out_lanes > 0) & (out_lanes < cols - 1)
+        out[y] = jnp.where(inside, main[y].astype(F32), side).astype(BF16)
+        return 0
+
+    lax.fori_loop(0, rows, step, 0, unroll=8)
+    out[0] = complete(0, top).astype(BF16)
+    out[rows - 1] = complete(rows - 1, bottom).astype(BF16)
+    if gelu:
+
+        def ended_column(value, at):
+            value = jnp.where(out_lanes == 0, top[:, at : at + 1], value)
+            return jnp.where(out_lanes == rows - 1, bottom[:, at : at + 1], value)
+
+        found = (top, bottom, ended_column(first, 0), ended_column(last, cols - 1))
+        if mode == "turned":
+            found = turn_edges(where[0, 0], found, cols)
+        else:
+            found = paired(where, found)
+        for edge, value in zip(edges, found):
+            edge[...] = value.astype(BF16)
+
+
+def with_edges(where, main, sources, halo, taps, mode, base=None, mask=None):
+    rows, outputs, cols = main[0].shape
+    pairs = rows // 2
+
+    def pair_of(values, number):
+        return pl.BlockSpec((2, *values.shape[1:]), lambda i: (number, 0, 0))
+
+    operands = [*main, *sources, *sources, *halo, taps]
+    extra = [value for value in (base, mask) if value is not None]
+    specs = [VM] * 3
+    specs += [pair_of(value, 0) for value in sources]
+    specs += [pair_of(value, pairs - 1) for value in sources]
+    specs += [VM] * (len(halo) + 1 + len(extra))
+    shapes = [jax.ShapeDtypeStruct((rows, outputs, cols), BF16)]
+    if base is None:
+        shapes += [jax.ShapeDtypeStruct((outputs, cols), BF16)] * 4
+    result = pl.pallas_call(
+        partial(edge_kernel, len(sources), mode),
+        grid=(1,),
+        out_shape=shapes,
+        in_specs=[SM] + specs,
+        out_specs=[VM] * len(shapes),
+        scratch_shapes=[pltpu.VMEM((6, taps.shape[1], 2 * cols), BF16)],
+        cost_estimate=lasting(3),
+        compiler_params=SMALL,
+    )(where, *operands, *extra)
+    return (result[0], result[1:]) if base is None else result[0]
+
+
 def shifted(value, axis, distance):
     count = lax.axis_size(axis)
     return lax.ppermute(value, axis, [(i, (i + distance) % count) for i in range(count)])
@@ -649,7 +930,10 @@
         cost_estimate=lasting(3),
         compiler_params=SMALL,
     )(face_turns, incoming)
-    sea_halo = exchanged(sea_edges, place)
+    sea_rows = send_rows(sea_edges)
+    hidden_main = convolve_alone([state, sea], taps1, "gelu")
+    sea_rows, hidden_main = barrier((sea_rows, hidden_main))
+    sea_halo = send_sides(sides_of(place, sea_rows, sea_edges))
     forcing, *forcing_edges = pl.pallas_call(
         partial(force_kernel, capacity),
         out_shape=[jax.ShapeDtypeStruct((rows, CF, cols), F32), *edge_shapes(CF)],
@@ -661,9 +945,11 @@
     forcing_rows = send_rows(forcing_edges, swaps=True)
 
     state_span = (0, state_channels)
+    sea_halo, _ = barrier((sea_halo, forcing))
     halo = halo_of(face_turns, [state_span, (0, CS)], True, early_halo, sea_halo)
-    sea, _ = barrier((sea, forcing))
-    hidden, hidden_edges = convolve(face_turns, [state, sea], halo, taps1, "turned")
+    hidden, hidden_edges = with_edges(
+        face_turns, hidden_main, [state, sea], halo, taps1, "turned"
+    )
     forcing_rows, hidden_edges = barrier((forcing_rows, hidden_edges))
     forcing_sides = sides_of(place, forcing_rows, forcing_edges, swaps=True)
     forcing_halo = send_sides(forcing_sides)

time: 163 us -> 156 us (0.957); the launches traced: 161 us -> 155 us
  waiting for transfers between devices: 19.8 us -> 6.31 us
  Pallas kernels: 57.4 us -> 63.4 us
  local copies, waits for them, and re-layouts: 32.3 us -> 34 us
    pallas_call x0 -> x2, Pallas kernels: none -> 14.7 us  [the longest x1 10.4 us: convolve_alone(): pl.pallas_call(partial(main_kernel, len(sources), mode), out_shape=[jax.S...]
    pallas_call x4 -> x3, Pallas kernels: 38 us -> 25.5 us  [convolve(): pl.pallas_call(partial(conv_kernel, len(sources), mode), out_shape=shapes...]
    ppermute x16, waiting for transfers between devices: 13.7 us -> 4.79 us  [shifted(): lax.ppermute(value, axis, [(i, (i + distance) % count) for i in range(cou...]
    all_to_all x1, waiting for transfers between devices: 6.07 us -> 1.51 us  [on_device(): lax.all_to_all(answer, axes, split_axis=0, concat_axis=0, tiled=True)]
    pallas_call x1, Pallas kernels: 0.48 us -> 2.29 us  [on_device(): pl.pallas_call(return_kernel, grid=(1,), out_shape=jax.ShapeDtypeStruct((...]
    unnamed x72 -> x104, local copies, waits for them, and re-layouts: 32.1 us -> 33.8 us
  transfers between devices with their start and end apart: 23 -> 23, of which waited for: 8 -> 5; matrix products, arithmetic and copies ran while one was open for 5% -> 5% of each run, Pallas kernels for 26% -> 32%
where the time goes in v2:
time: 156 us; the launch traced here: 155 us
  Pallas kernels  63.4 us (41%)
  starting transfers between devices  48.5 us (31%)
  local copies, waits for them, and re-layouts  34 us (22%)
  waiting for transfers between devices  6.31 us (4%)
  between operations  1.92 us (1%)
    unnamed x104, local copies, waits for them, and re-layouts  33.8 us
    ppermute x16, starting transfers between devices, shifted(): lax.ppermute(value, axis, [(i, (i + distance) % count) for i in range(cou...  27.1 us
    pallas_call x3, Pallas kernels, convolve(): pl.pallas_call(partial(conv_kernel, len(sources), mode), out_shape=shapes...  25.5 us
    pallas_call x1, Pallas kernels, convolve_alone(): pl.pallas_call(partial(main_kernel, len(sources), mode), out_shape=[jax.S...  10.4 us
    all_to_all x1, starting transfers between devices, on_device(): lax.all_to_all(payload, axes, split_axis=0, concat_axis=0, tiled=True)  7.44 us
    ppermute x2, starting transfers between devices, send_rows(): lax.ppermute(bottom, axes, swap(0))  7.2 us
    pallas_call x1, Pallas kernels, on_device(): pl.pallas_call(early_kernel, out_shape=edge_shapes(state_channels + ocean...  5.38 us
    ppermute x16, waiting for transfers between devices, shifted(): lax.ppermute(value, axis, [(i, (i + distance) % count) for i in range(cou...  4.79 us
  transfers between devices with their start and end apart: 23, of which 5 were waited for; matrix products, arithmetic and copies ran while one was open for 5% of the time, Pallas kernels for 32%

profile of v2, /device:TPU:0, one launch (start us, length us, event | category | flops | bytes accessed | tf_op | source)
XLA Modules:
  0.0 155.5 jit_solution(3771555261492554844)
XLA Ops:
  0.6 1.6 %copy-done.8 = bf16[64,128,128]{2,1,0:T(8,128)(2,1)S(1)} copy-done((bf16[64,128,128]{2,1,0:T(8,128)(2,1)S(1)}, bf16[64,128,128]{2,1,0:T(8,128)(2,1)}, u32[]{:S(2)}) %copy-start.8) | copy-done | bytes 2097176
  2.2 0.7 copy-done.16
  4.9 1.5 shard_map.122
  6.4 7.4 %all-to-all-start = ((bf16[32,8,2176]{2,1,0:T(8,128)(2,1)}), bf16[32,8,2176]{2,1,0:T(8,128)(2,1)}, u32[]{:S(2)}, u32[]{:S(2)}) async-start(bf16[32,8,2176]{2,1,0:T(8,128)(2,1)} %bitcast.7), calls=%async_computation | async-start | bytes 2228224 | tf_op jit(solution)/shard_map/all_to_all | solution.py:863
  14.7 5.0 %copy.31 = bf16[128,128,128]{2,0,1:T(8,128)(2,1)S(1)} copy(bf16[128,128,128]{2,1,0:T(8,128)(2,1)} %surface.3) | data formatting | bytes 8388608 | tf_op args[0]
  19.7 1.3 fusion.ocean.refs_1_.refs_6_
  21.1 0.7 copy-done
  21.8 5.4 %shard_map.123 = (bf16[192,128]{1,0:T(8,128)(2,1)S(1)}, bf16[192,128]{1,0:T(8,128)(2,1)S(1)}, bf16[192,128]{1,0:T(8,128)(2,1)S(1)}, bf16[192,128]{1,0:T(8,128)(2,1)S(1)}) custom-call(s32[1,1]{1,0:T(1,128)S(6)} %copy.32.turn.where.refs_0_, bf16[128,128,128]{2,1,0:T(8,128)(2,1)S(1)} %bitcast.21, bf16[128,64,128]{2,1,0:T(8,128)(2,1)S(1)} %fusion.ocean.refs_1_.refs_6_), custom_call_target="tpu_custom_call" | custom-call | flops 6442450944 | tf_op jit(solution)/shard_map/pallas_call | solution.py:868
  27.1 1.8 %collective-permute-start = (bf16[192,128]{1,0:T(8,128)(2,1)S(1)}, bf16[192,128]{1,0:T(8,128)(2,1)S(1)}, u32[]{:S(2)}, u32[]{:S(2)}) collective-permute-start(bf16[192,128]{1,0:T(8,128)(2,1)S(1)} %get-tuple-element.104), channel_id=1, source_target_pairs={{0,8},{8,16},{16,24},{24,0},{1,9},{9,17},{17,25},{25,1},{2,10},{10... | collective-permute-start | bytes 147464 | tf_op jit(solution)/shard_map/ppermute | solution.py:739
  29.6 5.5 %collective-permute-start.1 = (bf16[192,128]{1,0:T(8,128)(2,1)S(1)}, bf16[192,128]{1,0:T(8,128)(2,1)S(1)}, u32[]{:S(2)}, u32[]{:S(2)}) collective-permute-start(bf16[192,128]{1,0:T(8,128)(2,1)S(1)} %get-tuple-element.105), channel_id=1, source_target_pairs={{0,24},{8,0},{16,8},{24,16},{1,25},{9,1},{17,9},{25,17},{2,26},{10... | collective-permute-start | bytes 147464 | tf_op jit(solution)/shard_map/ppermute | solution.py:739
  35.2 2.2 %copy-done.3 = bf16[128,128,128]{2,1,0:T(8,128)(2,1)S(1)} copy-done((bf16[128,128,128]{2,1,0:T(8,128)(2,1)S(1)}, bf16[128,128,128]{2,1,0:T(8,128)(2,1)}, u32[]{:S(2)}) %copy-start.3) | copy-done | bytes 4194328
  38.0 0.8 copy-done.10
  38.8 1.2 copy.23.refs_0_
  40.1 0.8 shard_map.124
  41.8 3.2 %collective-permute-start.4 = (bf16[192,256]{1,0:T(8,128)(2,1)S(1)}, bf16[192,256]{1,0:T(8,128)(2,1)S(1)}, u32[]{:S(2)}, u32[]{:S(2)}) collective-permute-start(bf16[192,256]{1,0:T(8,128)(2,1)S(1)} %get-tuple-element.111), channel_id=1, source_target_pairs={{0,7},{1,0},{2,1},{3,2},{4,3},{5,4},{6,5},{7,6},{8,15},{9,8},{10,9... | collective-permute-start | bytes 294920 | tf_op jit(solution)/shard_map/ppermute | solution.py:739
  45.2 0.7 copy-done.34
  47.4 0.7 copy-done.23
  48.1 1.0 copy-done.11
  49.1 2.3 %shard_map.127 = bf16[256,2048]{1,0:T(8,128)(2,1)} custom-call(bf16[256,2176]{1,0:T(8,128)(2,1)} %bitcast.8.meta.incoming, bf16[128,2048]{1,0:T(8,128)(2,1)S(1)} %copy-done.11), custom_call_target="tpu_custom_call" | custom-call | flops 1073741824 | tf_op jit(solution)/shard_map/pallas_call | solution.py:912
  51.4 4.6 %all-to-all-start.1 = ((bf16[32,8,2048]{2,1,0:T(8,128)(2,1)}), bf16[32,8,2048]{2,1,0:T(8,128)(2,1)}, u32[]{:S(2)}, u32[]{:S(2)}) async-start(bf16[32,8,2048]{2,1,0:T(8,128)(2,1)} %bitcast.12), calls=%async_computation.1 | async-start | bytes 2097152 | tf_op jit(solution)/shard_map/all_to_all | solution.py:924
  56.1 4.1 %shard_map.129 = (f32[128,16,128]{2,1,0:T(8,128)S(1)}, bf16[16,128]{1,0:T(8,128)(2,1)S(1)}, bf16[16,128]{1,0:T(8,128)(2,1)S(1)}, bf16[16,128]{1,0:T(8,128)(2,1)S(1)}, bf16[16,128]{1,0:T(8,128)(2,1)S(1)}) custom-call(s32[1,1]{1,0:T(1,128)S(6)} %copy.32.turn.where.refs_0_, bf16[256,2176]{1,0:T(8,128)(2,1)} %bitcast.8.meta.incoming), custom_call_target="tpu_custom_call" | custom-call | flops 3221225472 | tf_op jit(solution)/shard_map/pallas_call | solution.py:925
  60.2 1.5 collective-permute-start.7
  61.7 1.4 collective-permute-start.8
  63.1 10.4 %shard_map.130 = (bf16[128,128,128]{2,1,0:T(8,128)(2,1)S(1)}, f32[128,128]{1,0:T(8,128)S(1)}, f32[128,128]{1,0:T(8,128)S(1)}) custom-call(bf16[128,128,128]{2,1,0:T(8,128)(2,1)S(1)} %bitcast.22, f32[128,16,128]{2,1,0:T(8,128)S(1)} %get-tuple-element.127.refs_1_.refs_4_.refs_6_, bf16[384,512]{1,0:T(8,128)(2,1)S(1)} %get-tuple-element.128.refs_2_.refs_10_), custom_call_target="tpu_custom_call" | custom-call | flops 12867427328 | tf_op jit(solution)/shard_map/pallas_call | solution.py:586
  73.6 2.0 %copy-done.6 = bf16[128,128,128]{2,1,0:T(8,128)(2,1)} copy-done((bf16[128,128,128]{2,1,0:T(8,128)(2,1)}, bf16[128,128,128]{2,1,0:T(8,128)(2,1)S(1)}, u32[]{:S(2)}) %copy-start.6) | copy-done | bytes 4194328
  76.9 1.2 shard_map.131
  79.3 2.7 %collective-permute-start.10 = (bf16[16,256]{1,0:T(8,128)(2,1)}, bf16[16,256]{1,0:T(8,128)(2,1)S(1)}, u32[]{:S(2)}, u32[]{:S(2)}) collective-permute-start(bf16[16,256]{1,0:T(8,128)(2,1)} %get-tuple-element.146), channel_id=1, source_target_pairs={{0,7},{1,0},{2,1},{3,2},{4,3},{5,4},{6,5},{7,6},{8,15},{9,8},{10,9... | collective-permute-start | bytes 24584 | tf_op jit(solution)/shard_map/ppermute | solution.py:739
  82.0 1.5 all-to-all-done.1
  84.2 0.7 copy-done.30
  84.9 3.8 %shard_map.128 = (f32[128,16,128]{2,1,0:T(8,128)S(1)}, bf16[16,128]{1,0:T(8,128)(2,1)S(1)}, bf16[16,128]{1,0:T(8,128)(2,1)S(1)}, bf16[16,128]{1,0:T(8,128)(2,1)S(1)}, bf16[16,128]{1,0:T(8,128)(2,1)S(1)}) custom-call(s32[1,2]{1,0:T(1,128)S(1)} %copy-done.30, s32[1,128]{1,0:T(1,128)S(1)} %bitcast.32, bf16[256,2048]{1,0:T(8,128)(2,1)} %bitcast.13.returned), custom_call_target="tpu_custom_call" | custom-call | flops 3221225472 | tf_op jit(solution)/shard_map/pallas_call | solution.py:937
  89.4 3.3 %collective-permute-start.6 = (bf16[16,128]{1,0:T(8,128)(2,1)S(1)}, bf16[16,128]{1,0:T(8,128)(2,1)S(1)}, u32[]{:S(2)}, u32[]{:S(2)}) collective-permute-start(bf16[16,128]{1,0:T(8,128)(2,1)S(1)} %get-tuple-element.122), channel_id=1, source_target_pairs={{0,8},{1,9},{2,10},{3,11},{4,12},{5,13},{6,14},{7,15},{8,0},{9,1},... | collective-permute-start | bytes 12296 | tf_op jit(solution)/shard_map/ppermute | solution.py:759
  93.2 4.3 %shard_map.133 = (bf16[128,128,128]{2,1,0:T(8,128)(2,1)S(1)}, bf16[128,128]{1,0:T(8,128)(2,1)S(1)}, bf16[128,128]{1,0:T(8,128)(2,1)S(1)}, bf16[128,128]{1,0:T(8,128)(2,1)S(1)}, bf16[128,128]{1,0:T(8,128)(2,1)S(1)}) custom-call(s32[1,1]{1,0:T(1,128)S(6)} %copy.32.turn.where.refs_0_, bf16[128,128,128]{2,1,0:T(8,128)(2,1)S(1)} %copy-done.7, ...), custom_call_target="tpu_custom_call" | custom-call | flops 3221225472 | tf_op jit(solution)/shard_map/pallas_call | solution.py:724
  97.5 0.7 shard_map.135
  98.3 3.5 %collective-permute-start.14 = (bf16[16,256]{1,0:T(8,128)(2,1)S(1)}, bf16[16,256]{1,0:T(8,128)(2,1)S(1)}, u32[]{:S(2)}, u32[]{:S(2)}) collective-permute-start(bf16[16,256]{1,0:T(8,128)(2,1)S(1)} %get-tuple-element.171), channel_id=1, source_target_pairs={{0,7},{1,0},{2,1},{3,2},{4,3},{5,4},{6,5},{7,6},{8,15},{9,8},{10,9... | collective-permute-start | bytes 24584 | tf_op jit(solution)/shard_map/ppermute | solution.py:739
  101.9 2.9 %collective-permute-start.12 = (bf16[128,128]{1,0:T(8,128)(2,1)S(1)}, bf16[128,128]{1,0:T(8,128)(2,1)S(1)}, u32[]{:S(2)}, u32[]{:S(2)}) collective-permute-start(bf16[128,128]{1,0:T(8,128)(2,1)S(1)} %get-tuple-element.159), channel_id=1, source_target_pairs={{0,24},{8,0},{16,8},{24,16},{1,25},{9,1},{17,9},{25,17},{2,26},{10... | collective-permute-start | bytes 98312 | tf_op jit(solution)/shard_map/ppermute | solution.py:739
  104.9 1.7 %collective-permute-done.11.refs_0_ = bf16[128,128]{1,0:T(8,128)(2,1)S(1)} collective-permute-done((bf16[128,128]{1,0:T(8,128)(2,1)S(1)}, bf16[128,128]{1,0:T(8,128)(2,1)S(1)}, u32[]{:S(2)}, u32[]{:S(2)}) %collective-permute-start.11) | collective-permute-done | bytes 32800 | tf_op jit(solution)/shard_map/ppermute | solution.py:739
  106.6 1.0 collective-permute-done.12.refs_1_
  108.9 7.5 %shard_map.137 = (bf16[128,64,128]{2,1,0:T(8,128)(2,1)S(1)}, bf16[64,128]{1,0:T(8,128)(2,1)S(1)}, bf16[64,128]{1,0:T(8,128)(2,1)S(1)}, bf16[64,128]{1,0:T(8,128)(2,1)S(1)}, bf16[64,128]{1,0:T(8,128)(2,1)S(1)}) custom-call(s32[1,2]{1,0:T(1,128)S(1)} %copy-done.30, bf16[128,64,128]{2,1,0:T(8,128)(2,1)S(1)} %fusion.ocean.refs_1_.refs_6_, ...), custom_call_target="tpu_custom_call" | custom-call | flops 3216856832 | tf_op jit(solution)/shard_map/pallas_call | solution.py:444
  116.4 0.8 collective-permute-start.15
  117.2 3.9 %collective-permute-start.16 = (bf16[64,128]{1,0:T(8,128)(2,1)S(1)}, bf16[64,128]{1,0:T(8,128)(2,1)S(1)}, u32[]{:S(2)}, u32[]{:S(2)}) collective-permute-start(bf16[64,128]{1,0:T(8,128)(2,1)S(1)} %get-tuple-element.177), channel_id=1, source_target_pairs={{0,8},{1,9},{2,10},{3,11},{4,12},{5,13},{6,14},{7,15},{8,0},{9,1},... | collective-permute-start | bytes 49160 | tf_op jit(solution)/shard_map/ppermute | solution.py:759
  121.6 11.1 %shard_map.139 = bf16[128,128,128]{2,1,0:T(8,128)(2,1)S(1)} custom-call(s32[1,1]{1,0:T(1,128)S(6)} %copy.32.turn.where.refs_0_, bf16[128,128,128]{2,1,0:T(8,128)(2,1)S(1)} %get-tuple-element.180.refs_1_, f32[2,128,256]{2,1,0:T(8,128)S(1)} %get-tuple-element.184.refs_2_, f32[128,128]{1,0:T(8,128)S(1)} %get-tuple-element.185.refs_3_, ...), custom_call_target="tpu_custom_call" | custom-call | flops 9650570240 | tf_op jit(solution)/shard_map/pallas_call | solution.py:444
  132.7 2.0 %copy-done.4 = bf16[128,128,128]{2,1,0:T(8,128)(2,1)} copy-done((bf16[128,128,128]{2,1,0:T(8,128)(2,1)}, bf16[128,128,128]{2,1,0:T(8,128)(2,1)S(1)}, u32[]{:S(2)}) %copy-start.4) | copy-done | bytes 4194328
  134.7 0.8 shard_map.140
  135.6 3.5 %collective-permute-start.20 = (bf16[64,256]{1,0:T(8,128)(2,1)S(1)}, bf16[64,256]{1,0:T(8,128)(2,1)S(1)}, u32[]{:S(2)}, u32[]{:S(2)}) collective-permute-start(bf16[64,256]{1,0:T(8,128)(2,1)S(1)} %get-tuple-element.195), channel_id=1, source_target_pairs={{0,7},{1,0},{2,1},{3,2},{4,3},{5,4},{6,5},{7,6},{8,15},{9,8},{10,9... | collective-permute-start | bytes 98312 | tf_op jit(solution)/shard_map/ppermute | solution.py:739
  139.2 1.8 %collective-permute-done.19.refs_2_ = bf16[64,256]{1,0:T(8,128)(2,1)S(1)} collective-permute-done((bf16[64,256]{1,0:T(8,128)(2,1)S(1)}, bf16[64,256]{1,0:T(8,128)(2,1)S(1)}, u32[]{:S(2)}, u32[]{:S(2)}) %collective-permute-start.19) | collective-permute-done | bytes 32800 | tf_op jit(solution)/shard_map/ppermute | solution.py:739
  141.2 6.9 %shard_map.142 = bf16[128,64,128]{2,1,0:T(8,128)(2,1)S(1)} custom-call(s32[1,2]{1,0:T(1,128)S(1)} %copy-done.31, bf16[128,64,128]{2,1,0:T(8,128)(2,1)S(1)} %copy-done.33, f32[2,64,256]{2,1,0:T(8,128)S(1)} %get-tuple-element.202.refs_2_, f32[64,128]{1,0:T(8,128)S(1)} %get-tuple-element.203.refs_3_, f32[64,128]{1,0:T(8,128)S(1)} %get-tuple-element.204.refs_4_, ...), custom_call_target="tpu_custom_call" | custom-call | flops 3216856832 | tf_op jit(solution)/shard_map/pallas_call | solution.py:444
  148.1 2.7 %copy.26 = bf16[64,128,128]{2,1,0:T(8,128)(2,1)} copy(bf16[64,128,128]{2,0,1:T(8,128)(2,1)S(1)} %bitcast.27) | data formatting | bytes 4194304
  150.8 4.7 %copy.25 = bf16[128,128,128]{2,1,0:T(8,128)(2,1)} copy(bf16[128,128,128]{2,0,1:T(8,128)(2,1)S(1)} %bitcast.26) | data formatting | bytes 8388608
  (131 shorter events, 12.6 us)
Async XLA Ops:
  6.4 7.5 %copy-start.17 = (s32[128,4]{0,1:T(4,128)S(1)}, s32[128,4]{0,1:T(4,128)}, u32[]{:S(2)}) copy-start(s32[128,4]{0,1:T(4,128)} %param.13) | copy-start | bytes 6148
  6.4 41.7 %all-to-all-start = ((bf16[32,8,2176]{2,1,0:T(8,128)(2,1)}), bf16[32,8,2176]{2,1,0:T(8,128)(2,1)}, u32[]{:S(2)}, u32[]{:S(2)}) async-start(bf16[32,8,2176]{2,1,0:T(8,128)(2,1)} %bitcast.7), calls=%async_computation | async-start | bytes 2228224 | tf_op jit(solution)/shard_map/all_to_all | solution.py:863
  14.7 5.1 %copy-start.9 = (bf16[64,128,128]{2,1,0:T(8,128)(2,1)S(1)}, bf16[64,128,128]{2,1,0:T(8,128)(2,1)}, u32[]{:S(2)}) copy-start(bf16[64,128,128]{2,1,0:T(8,128)(2,1)} %surface.2) | copy-start | bytes 6291460
  27.1 12.9 %collective-permute-start = (bf16[192,128]{1,0:T(8,128)(2,1)S(1)}, bf16[192,128]{1,0:T(8,128)(2,1)S(1)}, u32[]{:S(2)}, u32[]{:S(2)}) collective-permute-start(bf16[192,128]{1,0:T(8,128)(2,1)S(1)} %get-tuple-element.104), channel_id=1, source_target_pairs={{0,8},{8,16},{16,24},{24,0},{1,9},{9,17},{17,25},{25,1},{2,10},{10... | collective-permute-start | bytes 147464 | tf_op jit(solution)/shard_map/ppermute | solution.py:739
  28.9 11.1 %collective-permute-start.2 = (bf16[64,128]{1,0:T(8,128)(2,1)S(1)}, bf16[64,128]{1,0:T(8,128)(2,1)S(1)}, u32[]{:S(2)}, u32[]{:S(2)}) collective-permute-start(bf16[64,128]{1,0:T(8,128)(2,1)S(1)} %slice.3), channel_id=1, source_target_pairs={{24,31},{25,30},{26,29},{27,28},{28,27},{29,26},{30,25},{31,24}} | collective-permute-start | bytes 49160 | tf_op jit(solution)/shard_map/ppermute | solution.py:762
  29.6 10.5 %collective-permute-start.1 = (bf16[192,128]{1,0:T(8,128)(2,1)S(1)}, bf16[192,128]{1,0:T(8,128)(2,1)S(1)}, u32[]{:S(2)}, u32[]{:S(2)}) collective-permute-start(bf16[192,128]{1,0:T(8,128)(2,1)S(1)} %get-tuple-element.105), channel_id=1, source_target_pairs={{0,24},{8,0},{16,8},{24,16},{1,25},{9,1},{17,9},{25,17},{2,26},{10... | collective-permute-start | bytes 147464 | tf_op jit(solution)/shard_map/ppermute | solution.py:739
  37.3 39.6 %copy-start.29 = (s32[1,2]{1,0:T(1,128)}, s32[1,2]{1,0:T(1,128)S(1)}, u32[]{:S(2)}) copy-start(s32[1,2]{1,0:T(1,128)S(1)} %add_bitcast_fusion.place.refs_0_) | copy-start | bytes 28
  40.0 5.0 %copy-start.18 = (bf16[9,128,128]{2,1,0:T(8,128)(2,1)S(1)}, bf16[9,128,128]{2,1,0:T(8,128)(2,1)}, u32[]{:S(2)}) copy-start(bf16[9,128,128]{2,1,0:T(8,128)(2,1)} %refs_1_.1) | copy-start | bytes 884740
  40.0 5.0 %copy-start.19 = (bf16[9,64,80]{2,1,0:T(8,128)(2,1)S(1)}, bf16[9,64,80]{2,1,0:T(8,128)(2,1)}, u32[]{:S(2)}) copy-start(bf16[9,64,80]{2,1,0:T(8,128)(2,1)} %refs_2_.1) | copy-start | bytes 276484
  40.0 5.0 %copy-start.20 = (bf16[9,64,64]{2,1,0:T(8,128)(2,1)S(1)}, bf16[9,64,64]{2,1,0:T(8,128)(2,1)}, u32[]{:S(2)}) copy-start(bf16[9,64,64]{2,1,0:T(8,128)(2,1)} %refs_3_.1) | copy-start | bytes 221188
  41.4 10.0 %copy-start.40 = (bf16[192,128]{1,0:T(8,128)(2,1)}, bf16[192,128]{1,0:T(8,128)(2,1)S(1)}, u32[]{:S(2)}) copy-start(bf16[192,128]{1,0:T(8,128)(2,1)S(1)} %get-tuple-element.135.refs_0_) | copy-start | bytes 147460
  41.4 6.0 %collective-permute-start.3 = (bf16[192,256]{1,0:T(8,128)(2,1)S(1)}, bf16[192,256]{1,0:T(8,128)(2,1)S(1)}, u32[]{:S(2)}, u32[]{:S(2)}) collective-permute-start(bf16[192,256]{1,0:T(8,128)(2,1)S(1)} %get-tuple-element.110), channel_id=1, source_target_pairs={{0,1},{1,2},{2,3},{3,4},{4,5},{5,6},{6,7},{7,0},{8,9},{9,10},{10,1... | collective-permute-start | bytes 294920 | tf_op jit(solution)/shard_map/ppermute | solution.py:739
  41.8 5.6 %collective-permute-start.4 = (bf16[192,256]{1,0:T(8,128)(2,1)S(1)}, bf16[192,256]{1,0:T(8,128)(2,1)S(1)}, u32[]{:S(2)}, u32[]{:S(2)}) collective-permute-start(bf16[192,256]{1,0:T(8,128)(2,1)S(1)} %get-tuple-element.111), channel_id=1, source_target_pairs={{0,7},{1,0},{2,1},{3,2},{4,3},{5,4},{6,5},{7,6},{8,15},{9,8},{10,9... | collective-permute-start | bytes 294920 | tf_op jit(solution)/shard_map/ppermute | solution.py:739
  47.4 4.0 %copy-start.21 = (bf16[192,256]{1,0:T(8,128)(2,1)}, bf16[192,256]{1,0:T(8,128)(2,1)S(1)}, u32[]{:S(2)}) copy-start(bf16[192,256]{1,0:T(8,128)(2,1)S(1)} %collective-permute-done.3.refs_2_) | copy-start | bytes 294916
  51.4 32.1 %all-to-all-start.1 = ((bf16[32,8,2048]{2,1,0:T(8,128)(2,1)}), bf16[32,8,2048]{2,1,0:T(8,128)(2,1)}, u32[]{:S(2)}, u32[]{:S(2)}) async-start(bf16[32,8,2048]{2,1,0:T(8,128)(2,1)} %bitcast.12), calls=%async_computation.1 | async-start | bytes 2097152 | tf_op jit(solution)/shard_map/all_to_all | solution.py:924
  56.1 7.1 %copy-start.1 = (bf16[128,128,128]{2,0,1:T(8,128)(2,1)S(1)}, bf16[128,128,128]{2,0,1:T(8,128)(2,1)}, u32[]{:S(2)}) copy-start(bf16[128,128,128]{2,0,1:T(8,128)(2,1)} %copy-done) | copy-start | bytes 12582916
  60.2 16.7 %collective-permute-start.7 = (bf16[16,128]{1,0:T(8,128)(2,1)S(1)}, bf16[16,128]{1,0:T(8,128)(2,1)S(1)}, u32[]{:S(2)}, u32[]{:S(2)}) collective-permute-start(bf16[16,128]{1,0:T(8,128)(2,1)S(1)} %get-tuple-element.124), channel_id=1, source_target_pairs={{0,8},{8,16},{16,24},{24,0},{1,9},{9,17},{17,25},{25,1},{2,10},{10... | collective-permute-start | bytes 12296 | tf_op jit(solution)/shard_map/ppermute | solution.py:739
  61.7 15.2 %collective-permute-start.8 = (bf16[16,128]{1,0:T(8,128)(2,1)S(1)}, bf16[16,128]{1,0:T(8,128)(2,1)S(1)}, u32[]{:S(2)}, u32[]{:S(2)}) collective-permute-start(bf16[16,128]{1,0:T(8,128)(2,1)S(1)} %get-tuple-element.125), channel_id=1, source_target_pairs={{0,24},{8,0},{16,8},{24,16},{1,25},{9,1},{17,9},{25,17},{2,26},{10... | collective-permute-start | bytes 12296 | tf_op jit(solution)/shard_map/ppermute | solution.py:739
  79.3 9.4 %collective-permute-start.10 = (bf16[16,256]{1,0:T(8,128)(2,1)}, bf16[16,256]{1,0:T(8,128)(2,1)S(1)}, u32[]{:S(2)}, u32[]{:S(2)}) collective-permute-start(bf16[16,256]{1,0:T(8,128)(2,1)} %get-tuple-element.146), channel_id=1, source_target_pairs={{0,7},{1,0},{2,1},{3,2},{4,3},{5,4},{6,5},{7,6},{8,15},{9,8},{10,9... | collective-permute-start | bytes 24584 | tf_op jit(solution)/shard_map/ppermute | solution.py:739
  82.0 6.7 %collective-permute-start.9 = (bf16[16,256]{1,0:T(8,128)(2,1)}, bf16[16,256]{1,0:T(8,128)(2,1)S(1)}, u32[]{:S(2)}, u32[]{:S(2)}) collective-permute-start(bf16[16,256]{1,0:T(8,128)(2,1)} %get-tuple-element.145), channel_id=1, source_target_pairs={{0,1},{1,2},{2,3},{3,4},{4,5},{5,6},{6,7},{7,0},{8,9},{9,10},{10,1... | collective-permute-start | bytes 24584 | tf_op jit(solution)/shard_map/ppermute | solution.py:739
  84.9 7.9 %copy-start.22 = (bf16[192,256]{1,0:T(8,128)(2,1)S(1)}, bf16[192,256]{1,0:T(8,128)(2,1)}, u32[]{:S(2)}) copy-start(bf16[192,256]{1,0:T(8,128)(2,1)} %copy-done.21) | copy-start | bytes 294916
  84.9 7.9 %copy-start.24 = (bf16[192,256]{1,0:T(8,128)(2,1)S(1)}, bf16[192,256]{1,0:T(8,128)(2,1)}, u32[]{:S(2)}) copy-start(bf16[192,256]{1,0:T(8,128)(2,1)} %copy-done.23) | copy-start | bytes 294916
  84.9 7.9 %copy-start.41 = (bf16[192,128]{1,0:T(8,128)(2,1)S(1)}, bf16[192,128]{1,0:T(8,128)(2,1)}, u32[]{:S(2)}) copy-start(bf16[192,128]{1,0:T(8,128)(2,1)} %copy-done.40) | copy-start | bytes 147460
  84.9 7.9 %copy-start.43 = (bf16[192,128]{1,0:T(8,128)(2,1)S(1)}, bf16[192,128]{1,0:T(8,128)(2,1)}, u32[]{:S(2)}) copy-start(bf16[192,128]{1,0:T(8,128)(2,1)} %copy-done.42) | copy-start | bytes 147460
  84.9 7.9 %copy-start.45 = (bf16[16,128]{1,0:T(8,128)(2,1)S(1)}, bf16[16,128]{1,0:T(8,128)(2,1)}, u32[]{:S(2)}) copy-start(bf16[16,128]{1,0:T(8,128)(2,1)} %copy-done.44) | copy-start | bytes 12292
  84.9 7.9 %copy-start.47 = (bf16[16,128]{1,0:T(8,128)(2,1)S(1)}, bf16[16,128]{1,0:T(8,128)(2,1)}, u32[]{:S(2)}) copy-start(bf16[16,128]{1,0:T(8,128)(2,1)} %copy-done.46) | copy-start | bytes 12292
  84.9 8.3 %copy-start.2 = (bf16[128,128,128]{2,0,1:T(8,128)(2,1)S(1)}, bf16[128,128,128]{2,0,1:T(8,128)(2,1)}, u32[]{:S(2)}) copy-start(bf16[128,128,128]{2,0,1:T(8,128)(2,1)} %copy-done) | copy-start | bytes 12582916
  84.9 8.3 %copy-start.7 = (bf16[128,128,128]{2,1,0:T(8,128)(2,1)S(1)}, bf16[128,128,128]{2,1,0:T(8,128)(2,1)}, u32[]{:S(2)}) copy-start(bf16[128,128,128]{2,1,0:T(8,128)(2,1)} %copy-done.6) | copy-start | bytes 12582916
  88.7 4.5 %copy-start.13 = (f32[128,128]{1,0:T(8,128)S(1)}, f32[128,128]{1,0:T(8,128)}, u32[]{:S(2)}) copy-start(f32[128,128]{1,0:T(8,128)} %copy-done.12) | copy-start | bytes 196612
  88.7 4.5 %copy-start.15 = (f32[128,128]{1,0:T(8,128)S(1)}, f32[128,128]{1,0:T(8,128)}, u32[]{:S(2)}) copy-start(f32[128,128]{1,0:T(8,128)} %copy-done.14) | copy-start | bytes 196612
  88.8 8.8 %collective-permute-start.5 = (bf16[16,128]{1,0:T(8,128)(2,1)S(1)}, bf16[16,128]{1,0:T(8,128)(2,1)S(1)}, u32[]{:S(2)}, u32[]{:S(2)}) collective-permute-start(bf16[16,128]{1,0:T(8,128)(2,1)S(1)} %get-tuple-element.121), channel_id=1, source_target_pairs={{8,16},{9,17},{10,18},{11,19},{12,20},{13,21},{14,22},{15,23},{16,... | collective-permute-start | bytes 12296 | tf_op jit(solution)/shard_map/ppermute | solution.py:759
  89.4 8.1 %collective-permute-start.6 = (bf16[16,128]{1,0:T(8,128)(2,1)S(1)}, bf16[16,128]{1,0:T(8,128)(2,1)S(1)}, u32[]{:S(2)}, u32[]{:S(2)}) collective-permute-start(bf16[16,128]{1,0:T(8,128)(2,1)S(1)} %get-tuple-element.122), channel_id=1, source_target_pairs={{0,8},{1,9},{2,10},{3,11},{4,12},{5,13},{6,14},{7,15},{8,0},{9,1},... | collective-permute-start | bytes 12296 | tf_op jit(solution)/shard_map/ppermute | solution.py:759
  98.3 6.5 %collective-permute-start.13 = (bf16[16,256]{1,0:T(8,128)(2,1)S(1)}, bf16[16,256]{1,0:T(8,128)(2,1)S(1)}, u32[]{:S(2)}, u32[]{:S(2)}) collective-permute-start(bf16[16,256]{1,0:T(8,128)(2,1)S(1)} %get-tuple-element.170), channel_id=1, source_target_pairs={{0,1},{1,2},{2,3},{3,4},{4,5},{5,6},{6,7},{7,0},{8,9},{9,10},{10,1... | collective-permute-start | bytes 24584 | tf_op jit(solution)/shard_map/ppermute | solution.py:739
  98.3 6.5 %collective-permute-start.14 = (bf16[16,256]{1,0:T(8,128)(2,1)S(1)}, bf16[16,256]{1,0:T(8,128)(2,1)S(1)}, u32[]{:S(2)}, u32[]{:S(2)}) collective-permute-start(bf16[16,256]{1,0:T(8,128)(2,1)S(1)} %get-tuple-element.171), channel_id=1, source_target_pairs={{0,7},{1,0},{2,1},{3,2},{4,3},{5,4},{6,5},{7,6},{8,15},{9,8},{10,9... | collective-permute-start | bytes 24584 | tf_op jit(solution)/shard_map/ppermute | solution.py:739
  101.8 4.8 %collective-permute-start.11 = (bf16[128,128]{1,0:T(8,128)(2,1)S(1)}, bf16[128,128]{1,0:T(8,128)(2,1)S(1)}, u32[]{:S(2)}, u32[]{:S(2)}) collective-permute-start(bf16[128,128]{1,0:T(8,128)(2,1)S(1)} %get-tuple-element.158), channel_id=1, source_target_pairs={{0,8},{8,16},{16,24},{24,0},{1,9},{9,17},{17,25},{25,1},{2,10},{10... | collective-permute-start | bytes 98312 | tf_op jit(solution)/shard_map/ppermute | solution.py:739
  101.9 5.8 %collective-permute-start.12 = (bf16[128,128]{1,0:T(8,128)(2,1)S(1)}, bf16[128,128]{1,0:T(8,128)(2,1)S(1)}, u32[]{:S(2)}, u32[]{:S(2)}) collective-permute-start(bf16[128,128]{1,0:T(8,128)(2,1)S(1)} %get-tuple-element.159), channel_id=1, source_target_pairs={{0,24},{8,0},{16,8},{24,16},{1,25},{9,1},{17,9},{25,17},{2,26},{10... | collective-permute-start | bytes 98312 | tf_op jit(solution)/shard_map/ppermute | solution.py:739
  104.9 4.0 %copy-start.39 = (bf16[192,256]{1,0:T(8,128)(2,1)S(1)}, bf16[192,256]{1,0:T(8,128)(2,1)}, u32[]{:S(2)}) copy-start(bf16[192,256]{1,0:T(8,128)(2,1)} %copy-done.38) | copy-start | bytes 294916
  108.3 12.8 %collective-permute-start.18 = (bf16[128,256]{1,0:T(8,128)(2,1)S(1)}, bf16[128,256]{1,0:T(8,128)(2,1)S(1)}, u32[]{:S(2)}, u32[]{:S(2)}) collective-permute-start(bf16[128,256]{1,0:T(8,128)(2,1)S(1)} %get-tuple-element.162), channel_id=1, source_target_pairs={{0,7},{1,0},{2,1},{3,2},{4,3},{5,4},{6,5},{7,6},{8,15},{9,8},{10,9... | collective-permute-start | bytes 196616 | tf_op jit(solution)/shard_map/ppermute | solution.py:739
  108.4 12.7 %collective-permute-start.17 = (bf16[128,256]{1,0:T(8,128)(2,1)S(1)}, bf16[128,256]{1,0:T(8,128)(2,1)S(1)}, u32[]{:S(2)}, u32[]{:S(2)}) collective-permute-start(bf16[128,256]{1,0:T(8,128)(2,1)S(1)} %get-tuple-element.183), channel_id=1, source_target_pairs={{0,1},{1,2},{2,3},{3,4},{4,5},{5,6},{6,7},{7,0},{8,9},{9,10},{10,1... | collective-permute-start | bytes 196616 | tf_op jit(solution)/shard_map/ppermute | solution.py:739
  116.4 5.2 %copy-start.32 = (bf16[128,64,128]{2,1,0:T(8,128)(2,1)}, bf16[128,64,128]{2,1,0:T(8,128)(2,1)S(1)}, u32[]{:S(2)}) copy-start(bf16[128,64,128]{2,1,0:T(8,128)(2,1)S(1)} %get-tuple-element.179.refs_1_) | copy-start | bytes 6291460
  116.4 5.2 %copy-start.35 = (bf16[384,384]{1,0:T(8,128)(2,1)S(1)}, bf16[384,384]{1,0:T(8,128)(2,1)}, u32[]{:S(2)}) copy-start(bf16[384,384]{1,0:T(8,128)(2,1)} %copy-done.34) | copy-start | bytes 884740
  116.4 18.3 %collective-permute-start.15 = (bf16[64,128]{1,0:T(8,128)(2,1)S(1)}, bf16[64,128]{1,0:T(8,128)(2,1)S(1)}, u32[]{:S(2)}, u32[]{:S(2)}) collective-permute-start(bf16[64,128]{1,0:T(8,128)(2,1)S(1)} %get-tuple-element.176), channel_id=1, source_target_pairs={{8,16},{9,17},{10,18},{11,19},{12,20},{13,21},{14,22},{15,23},{16,... | collective-permute-start | bytes 49160 | tf_op jit(solution)/shard_map/ppermute | solution.py:759
  117.2 17.5 %collective-permute-start.16 = (bf16[64,128]{1,0:T(8,128)(2,1)S(1)}, bf16[64,128]{1,0:T(8,128)(2,1)S(1)}, u32[]{:S(2)}, u32[]{:S(2)}) collective-permute-start(bf16[64,128]{1,0:T(8,128)(2,1)S(1)} %get-tuple-element.177), channel_id=1, source_target_pairs={{0,8},{1,9},{2,10},{3,11},{4,12},{5,13},{6,14},{7,15},{8,0},{9,1},... | collective-permute-start | bytes 49160 | tf_op jit(solution)/shard_map/ppermute | solution.py:759
  121.6 13.2 %copy-start.31 = (s32[1,2]{1,0:T(1,128)S(1)}, s32[1,2]{1,0:T(1,128)}, u32[]{:S(2)}) copy-start(s32[1,2]{1,0:T(1,128)} %copy-done.29) | copy-start | bytes 28
  134.7 4.4 %copy-start.49 = (bf16[128,4]{0,1:T(4,128)(2,1)S(1)}, bf16[128,4]{0,1:T(4,128)(2,1)}, u32[]{:S(2)}) copy-start(bf16[128,4]{0,1:T(4,128)(2,1)} %copy-done.48) | copy-start | bytes 3076
  135.5 5.7 %copy-start.37 = (bf16[192,256]{1,0:T(8,128)(2,1)S(1)}, bf16[192,256]{1,0:T(8,128)(2,1)}, u32[]{:S(2)}) copy-start(bf16[192,256]{1,0:T(8,128)(2,1)} %copy-done.36) | copy-start | bytes 294916
  135.5 5.5 %collective-permute-start.19 = (bf16[64,256]{1,0:T(8,128)(2,1)S(1)}, bf16[64,256]{1,0:T(8,128)(2,1)S(1)}, u32[]{:S(2)}, u32[]{:S(2)}) collective-permute-start(bf16[64,256]{1,0:T(8,128)(2,1)S(1)} %get-tuple-element.194), channel_id=1, source_target_pairs={{0,1},{1,2},{2,3},{3,4},{4,5},{5,6},{6,7},{7,0},{8,9},{9,10},{10,1... | collective-permute-start | bytes 98312 | tf_op jit(solution)/shard_map/ppermute | solution.py:739
  135.6 5.5 %collective-permute-start.20 = (bf16[64,256]{1,0:T(8,128)(2,1)S(1)}, bf16[64,256]{1,0:T(8,128)(2,1)S(1)}, u32[]{:S(2)}, u32[]{:S(2)}) collective-permute-start(bf16[64,256]{1,0:T(8,128)(2,1)S(1)} %get-tuple-element.195), channel_id=1, source_target_pairs={{0,7},{1,0},{2,1},{3,2},{4,3},{5,4},{6,5},{7,6},{8,15},{9,8},{10,9... | collective-permute-start | bytes 98312 | tf_op jit(solution)/shard_map/ppermute | solution.py:739
  (25 other events, 26.7 us)

commit v3 on v2

--- a/solution.py
+++ b/solution.py
@@ -4,6 +4,7 @@
 import jax.numpy as jnp
 from jax import lax
 from jax.experimental import pallas as pl
+from jax.experimental.layout import Layout, with_layout_constraint
 from jax.experimental.pallas import tpu as pltpu
 from jax.sharding import PartitionSpec as P
 
@@ -967,7 +968,8 @@
     atmos_out = convolve(face_turns, [hidden], halo, taps2, "add", base=state)
     ocean_sent, atmos_out = barrier((ocean_sent, atmos_out))
     ocean_halo = send_sides(sides_of(place, ocean_sent, ocean_edges, swaps=True))
-    ocean_halo, atmos_out = barrier((ocean_halo, atmos_out.transpose(1, 0, 2)))
+    atmos_out = with_layout_constraint(atmos_out.transpose(1, 0, 2), Layout((0, 1, 2)))
+    ocean_halo, atmos_out = barrier((ocean_halo, atmos_out))
     halo = halo_of(face_turns, [(0, ocean_channels)], False, ocean_halo)
     ocean_out = convolve(
         place,

time: 156 us -> 158 us (1.013)
  local copies, waits for them, and re-layouts: 34 us -> 37.6 us
  waiting for transfers between devices: 6.31 us -> 4.51 us
    optimization_barrier x0 -> x1, local copies, waits for them, and re-layouts: none -> 6.91 us  [on_device(): ocean_sent, atmos_out = barrier((ocean_sent, atmos_out))]
    unnamed x104 -> x101, local copies, waits for them, and re-layouts: 33.8 us -> 30.5 us
    ppermute x16, waiting for transfers between devices: 4.79 us -> 2.97 us  [shifted(): lax.ppermute(value, axis, [(i, (i + distance) % count) for i in range(cou...]
  transfers between devices with their start and end apart: 23 -> 23, of which waited for: 5 -> 4; matrix products, arithmetic and copies ran while one was open for 5% -> 9% of each run, Pallas kernels for 32% -> 32%
where the time goes in v3:
time: 158 us; the launch traced here: 157 us
  Pallas kernels  63.1 us (40%)
  starting transfers between devices  48.7 us (31%)
  local copies, waits for them, and re-layouts  37.6 us (24%)
  waiting for transfers between devices  4.51 us (3%)
  between operations  1.89 us (1%)
    unnamed x101, local copies, waits for them, and re-layouts  30.5 us
    ppermute x16, starting transfers between devices, shifted(): lax.ppermute(value, axis, [(i, (i + distance) % count) for i in range(cou...  27.3 us
    pallas_call x3, Pallas kernels, convolve(): pl.pallas_call(partial(conv_kernel, len(sources), mode), out_shape=shapes...  25.4 us
    pallas_call x1, Pallas kernels, convolve_alone(): pl.pallas_call(partial(main_kernel, len(sources), mode), out_shape=[jax.S...  10.4 us
    all_to_all x1, starting transfers between devices, on_device(): lax.all_to_all(payload, axes, split_axis=0, concat_axis=0, tiled=True)  7.44 us
    ppermute x2, starting transfers between devices, send_rows(): lax.ppermute(bottom, axes, swap(0))  7.2 us
    optimization_barrier x1, local copies, waits for them, and re-layouts, on_device(): ocean_sent, atmos_out = barrier((ocean_sent, atmos_out))  6.91 us
    pallas_call x1, Pallas kernels, on_device(): pl.pallas_call(early_kernel, out_shape=edge_shapes(state_channels + ocean...  5.38 us
  transfers between devices with their start and end apart: 23, of which 4 were waited for; matrix products, arithmetic and copies ran while one was open for 9% of the time, Pallas kernels for 32%

profile of v3, /device:TPU:0, one launch (start us, length us, event | category | flops | bytes accessed | tf_op | source)
XLA Modules:
  0.0 157.2 jit_solution(3904568149452941671)
XLA Ops:
  0.6 1.6 %copy-done.7 = bf16[64,128,128]{2,1,0:T(8,128)(2,1)S(1)} copy-done((bf16[64,128,128]{2,1,0:T(8,128)(2,1)S(1)}, bf16[64,128,128]{2,1,0:T(8,128)(2,1)}, u32[]{:S(2)}) %copy-start.7) | copy-done | bytes 2097176
  2.2 0.7 copy-done.15
  4.9 1.5 shard_map.122
  6.4 7.4 %all-to-all-start = ((bf16[32,8,2176]{2,1,0:T(8,128)(2,1)}), bf16[32,8,2176]{2,1,0:T(8,128)(2,1)}, u32[]{:S(2)}, u32[]{:S(2)}) async-start(bf16[32,8,2176]{2,1,0:T(8,128)(2,1)} %bitcast.7), calls=%async_computation | async-start | bytes 2228224 | tf_op jit(solution)/shard_map/all_to_all | solution.py:864
  14.7 5.0 %copy.33 = bf16[128,128,128]{2,0,1:T(8,128)(2,1)S(1)} copy(bf16[128,128,128]{2,1,0:T(8,128)(2,1)} %surface.3) | data formatting | bytes 8388608 | tf_op args[0]
  19.7 1.3 fusion.ocean.refs_1_.refs_6_
  21.1 0.7 copy-done
  21.8 5.4 %shard_map.123 = (bf16[192,128]{1,0:T(8,128)(2,1)S(1)}, bf16[192,128]{1,0:T(8,128)(2,1)S(1)}, bf16[192,128]{1,0:T(8,128)(2,1)S(1)}, bf16[192,128]{1,0:T(8,128)(2,1)S(1)}) custom-call(s32[1,1]{1,0:T(1,128)S(6)} %copy.34.turn.where.refs_0_, bf16[128,128,128]{2,1,0:T(8,128)(2,1)S(1)} %bitcast.23, bf16[128,64,128]{2,1,0:T(8,128)(2,1)S(1)} %fusion.ocean.refs_1_.refs_6_), custom_call_target="tpu_custom_call" | custom-call | flops 6442450944 | tf_op jit(solution)/shard_map/pallas_call | solution.py:869
  27.1 1.8 %collective-permute-start = (bf16[192,128]{1,0:T(8,128)(2,1)S(1)}, bf16[192,128]{1,0:T(8,128)(2,1)S(1)}, u32[]{:S(2)}, u32[]{:S(2)}) collective-permute-start(bf16[192,128]{1,0:T(8,128)(2,1)S(1)} %get-tuple-element.104), channel_id=1, source_target_pairs={{0,8},{8,16},{16,24},{24,0},{1,9},{9,17},{17,25},{25,1},{2,10},{10... | collective-permute-start | bytes 147464 | tf_op jit(solution)/shard_map/ppermute | solution.py:740
  29.6 5.5 %collective-permute-start.1 = (bf16[192,128]{1,0:T(8,128)(2,1)S(1)}, bf16[192,128]{1,0:T(8,128)(2,1)S(1)}, u32[]{:S(2)}, u32[]{:S(2)}) collective-permute-start(bf16[192,128]{1,0:T(8,128)(2,1)S(1)} %get-tuple-element.105), channel_id=1, source_target_pairs={{0,24},{8,0},{16,8},{24,16},{1,25},{9,1},{17,9},{25,17},{2,26},{10... | collective-permute-start | bytes 147464 | tf_op jit(solution)/shard_map/ppermute | solution.py:740
  35.2 2.2 %copy-done.3 = bf16[128,128,128]{2,1,0:T(8,128)(2,1)S(1)} copy-done((bf16[128,128,128]{2,1,0:T(8,128)(2,1)S(1)}, bf16[128,128,128]{2,1,0:T(8,128)(2,1)}, u32[]{:S(2)}) %copy-start.3) | copy-done | bytes 4194328
  38.0 0.8 copy-done.9
  38.8 1.2 copy.23.refs_0_
  40.1 0.8 shard_map.124
  41.8 3.2 %collective-permute-start.4 = (bf16[192,256]{1,0:T(8,128)(2,1)S(1)}, bf16[192,256]{1,0:T(8,128)(2,1)S(1)}, u32[]{:S(2)}, u32[]{:S(2)}) collective-permute-start(bf16[192,256]{1,0:T(8,128)(2,1)S(1)} %get-tuple-element.111), channel_id=1, source_target_pairs={{0,7},{1,0},{2,1},{3,2},{4,3},{5,4},{6,5},{7,6},{8,15},{9,8},{10,9... | collective-permute-start | bytes 294920 | tf_op jit(solution)/shard_map/ppermute | solution.py:740
  45.2 0.7 copy-done.33
  47.4 0.7 copy-done.22
  48.1 1.0 copy-done.10
  49.1 2.3 %shard_map.127 = bf16[256,2048]{1,0:T(8,128)(2,1)} custom-call(bf16[256,2176]{1,0:T(8,128)(2,1)} %bitcast.8.meta.incoming, bf16[128,2048]{1,0:T(8,128)(2,1)S(1)} %copy-done.10), custom_call_target="tpu_custom_call" | custom-call | flops 1073741824 | tf_op jit(solution)/shard_map/pallas_call | solution.py:913
  51.4 4.6 %all-to-all-start.1 = ((bf16[32,8,2048]{2,1,0:T(8,128)(2,1)}), bf16[32,8,2048]{2,1,0:T(8,128)(2,1)}, u32[]{:S(2)}, u32[]{:S(2)}) async-start(bf16[32,8,2048]{2,1,0:T(8,128)(2,1)} %bitcast.12), calls=%async_computation.1 | async-start | bytes 2097152 | tf_op jit(solution)/shard_map/all_to_all | solution.py:925
  56.1 3.9 %shard_map.129 = (f32[128,16,128]{2,1,0:T(8,128)S(1)}, bf16[16,128]{1,0:T(8,128)(2,1)S(1)}, bf16[16,128]{1,0:T(8,128)(2,1)S(1)}, bf16[16,128]{1,0:T(8,128)(2,1)S(1)}, bf16[16,128]{1,0:T(8,128)(2,1)S(1)}) custom-call(s32[1,1]{1,0:T(1,128)S(6)} %copy.34.turn.where.refs_0_, bf16[256,2176]{1,0:T(8,128)(2,1)} %bitcast.8.meta.incoming), custom_call_target="tpu_custom_call" | custom-call | flops 3221225472 | tf_op jit(solution)/shard_map/pallas_call | solution.py:926
  60.0 1.9 %collective-permute-start.7 = (bf16[16,128]{1,0:T(8,128)(2,1)S(1)}, bf16[16,128]{1,0:T(8,128)(2,1)S(1)}, u32[]{:S(2)}, u32[]{:S(2)}) collective-permute-start(bf16[16,128]{1,0:T(8,128)(2,1)S(1)} %get-tuple-element.124), channel_id=1, source_target_pairs={{0,8},{8,16},{16,24},{24,0},{1,9},{9,17},{17,25},{25,1},{2,10},{10... | collective-permute-start | bytes 12296 | tf_op jit(solution)/shard_map/ppermute | solution.py:740
  61.9 1.1 collective-permute-start.8
  63.0 10.4 %shard_map.130 = (bf16[128,128,128]{2,1,0:T(8,128)(2,1)S(1)}, f32[128,128]{1,0:T(8,128)S(1)}, f32[128,128]{1,0:T(8,128)S(1)}) custom-call(bf16[128,128,128]{2,1,0:T(8,128)(2,1)S(1)} %bitcast.24, f32[128,16,128]{2,1,0:T(8,128)S(1)} %get-tuple-element.127.refs_1_.refs_4_.refs_6_, bf16[384,512]{1,0:T(8,128)(2,1)S(1)} %get-tuple-element.128.refs_2_.refs_10_), custom_call_target="tpu_custom_call" | custom-call | flops 12867427328 | tf_op jit(solution)/shard_map/pallas_call | solution.py:587
  73.5 2.0 %copy-done.5 = bf16[128,128,128]{2,1,0:T(8,128)(2,1)} copy-done((bf16[128,128,128]{2,1,0:T(8,128)(2,1)}, bf16[128,128,128]{2,1,0:T(8,128)(2,1)S(1)}, u32[]{:S(2)}) %copy-start.5) | copy-done | bytes 4194328
  76.8 1.2 shard_map.131
  79.2 2.8 %collective-permute-start.10 = (bf16[16,256]{1,0:T(8,128)(2,1)}, bf16[16,256]{1,0:T(8,128)(2,1)S(1)}, u32[]{:S(2)}, u32[]{:S(2)}) collective-permute-start(bf16[16,256]{1,0:T(8,128)(2,1)} %get-tuple-element.146), channel_id=1, source_target_pairs={{0,7},{1,0},{2,1},{3,2},{4,3},{5,4},{6,5},{7,6},{8,15},{9,8},{10,9... | collective-permute-start | bytes 24584 | tf_op jit(solution)/shard_map/ppermute | solution.py:740
  82.0 1.5 all-to-all-done.1
  84.9 3.8 %shard_map.128 = (f32[128,16,128]{2,1,0:T(8,128)S(1)}, bf16[16,128]{1,0:T(8,128)(2,1)S(1)}, bf16[16,128]{1,0:T(8,128)(2,1)S(1)}, bf16[16,128]{1,0:T(8,128)(2,1)S(1)}, bf16[16,128]{1,0:T(8,128)(2,1)S(1)}) custom-call(s32[1,2]{1,0:T(1,128)S(1)} %copy-done.29, s32[1,128]{1,0:T(1,128)S(1)} %bitcast.33, bf16[256,2048]{1,0:T(8,128)(2,1)} %bitcast.13.returned), custom_call_target="tpu_custom_call" | custom-call | flops 3221225472 | tf_op jit(solution)/shard_map/pallas_call | solution.py:938
  88.7 0.7 collective-permute-start.5
  89.4 3.3 %collective-permute-start.6 = (bf16[16,128]{1,0:T(8,128)(2,1)S(1)}, bf16[16,128]{1,0:T(8,128)(2,1)S(1)}, u32[]{:S(2)}, u32[]{:S(2)}) collective-permute-start(bf16[16,128]{1,0:T(8,128)(2,1)S(1)} %get-tuple-element.122), channel_id=1, source_target_pairs={{0,8},{1,9},{2,10},{3,11},{4,12},{5,13},{6,14},{7,15},{8,0},{9,1},... | collective-permute-start | bytes 12296 | tf_op jit(solution)/shard_map/ppermute | solution.py:760
  93.2 4.3 %shard_map.133 = (bf16[128,128,128]{2,1,0:T(8,128)(2,1)S(1)}, bf16[128,128]{1,0:T(8,128)(2,1)S(1)}, bf16[128,128]{1,0:T(8,128)(2,1)S(1)}, bf16[128,128]{1,0:T(8,128)(2,1)S(1)}, bf16[128,128]{1,0:T(8,128)(2,1)S(1)}) custom-call(s32[1,1]{1,0:T(1,128)S(6)} %copy.34.turn.where.refs_0_, bf16[128,128,128]{2,1,0:T(8,128)(2,1)S(1)} %copy-done.6, ...), custom_call_target="tpu_custom_call" | custom-call | flops 3221225472 | tf_op jit(solution)/shard_map/pallas_call | solution.py:725
  97.5 0.7 shard_map.135
  98.3 3.5 %collective-permute-start.14 = (bf16[16,256]{1,0:T(8,128)(2,1)S(1)}, bf16[16,256]{1,0:T(8,128)(2,1)S(1)}, u32[]{:S(2)}, u32[]{:S(2)}) collective-permute-start(bf16[16,256]{1,0:T(8,128)(2,1)S(1)} %get-tuple-element.171), channel_id=1, source_target_pairs={{0,7},{1,0},{2,1},{3,2},{4,3},{5,4},{6,5},{7,6},{8,15},{9,8},{10,9... | collective-permute-start | bytes 24584 | tf_op jit(solution)/shard_map/ppermute | solution.py:740
  101.9 2.9 %collective-permute-start.12 = (bf16[128,128]{1,0:T(8,128)(2,1)S(1)}, bf16[128,128]{1,0:T(8,128)(2,1)S(1)}, u32[]{:S(2)}, u32[]{:S(2)}) collective-permute-start(bf16[128,128]{1,0:T(8,128)(2,1)S(1)} %get-tuple-element.159), channel_id=1, source_target_pairs={{0,24},{8,0},{16,8},{24,16},{1,25},{9,1},{17,9},{25,17},{2,26},{10... | collective-permute-start | bytes 98312 | tf_op jit(solution)/shard_map/ppermute | solution.py:740
  104.9 1.7 %collective-permute-done.11.refs_0_ = bf16[128,128]{1,0:T(8,128)(2,1)S(1)} collective-permute-done((bf16[128,128]{1,0:T(8,128)(2,1)S(1)}, bf16[128,128]{1,0:T(8,128)(2,1)S(1)}, u32[]{:S(2)}, u32[]{:S(2)}) %collective-permute-start.11) | collective-permute-done | bytes 32800 | tf_op jit(solution)/shard_map/ppermute | solution.py:740
  106.6 1.0 collective-permute-done.12.refs_1_
  108.9 7.5 %shard_map.137 = (bf16[128,64,128]{2,1,0:T(8,128)(2,1)S(1)}, bf16[64,128]{1,0:T(8,128)(2,1)S(1)}, bf16[64,128]{1,0:T(8,128)(2,1)S(1)}, bf16[64,128]{1,0:T(8,128)(2,1)S(1)}, bf16[64,128]{1,0:T(8,128)(2,1)S(1)}) custom-call(s32[1,2]{1,0:T(1,128)S(1)} %copy-done.29, bf16[128,64,128]{2,1,0:T(8,128)(2,1)S(1)} %fusion.ocean.refs_1_.refs_6_, ...), custom_call_target="tpu_custom_call" | custom-call | flops 3216856832 | tf_op jit(solution)/shard_map/pallas_call | solution.py:445
  116.4 0.8 collective-permute-start.15
  117.2 3.9 %collective-permute-start.16 = (bf16[64,128]{1,0:T(8,128)(2,1)S(1)}, bf16[64,128]{1,0:T(8,128)(2,1)S(1)}, u32[]{:S(2)}, u32[]{:S(2)}) collective-permute-start(bf16[64,128]{1,0:T(8,128)(2,1)S(1)} %get-tuple-element.177), channel_id=1, source_target_pairs={{0,8},{1,9},{2,10},{3,11},{4,12},{5,13},{6,14},{7,15},{8,0},{9,1},... | collective-permute-start | bytes 49160 | tf_op jit(solution)/shard_map/ppermute | solution.py:760
  121.5 11.1 %shard_map.139 = bf16[128,128,128]{2,1,0:T(8,128)(2,1)S(1)} custom-call(s32[1,1]{1,0:T(1,128)S(6)} %copy.34.turn.where.refs_0_, bf16[128,128,128]{2,1,0:T(8,128)(2,1)S(1)} %get-tuple-element.180.refs_1_, f32[2,128,256]{2,1,0:T(8,128)S(1)} %get-tuple-element.184.refs_2_, f32[128,128]{1,0:T(8,128)S(1)} %get-tuple-element.185.refs_3_, ...), custom_call_target="tpu_custom_call" | custom-call | flops 9650570240 | tf_op jit(solution)/shard_map/pallas_call | solution.py:445
  132.7 2.0 %copy-done.4 = bf16[128,128,128]{2,1,0:T(8,128)(2,1)} copy-done((bf16[128,128,128]{2,1,0:T(8,128)(2,1)}, bf16[128,128,128]{2,1,0:T(8,128)(2,1)S(1)}, u32[]{:S(2)}) %copy-start.4) | copy-done | bytes 4194328
  134.7 0.8 shard_map.140
  135.6 3.5 %collective-permute-start.20 = (bf16[64,256]{1,0:T(8,128)(2,1)S(1)}, bf16[64,256]{1,0:T(8,128)(2,1)S(1)}, u32[]{:S(2)}, u32[]{:S(2)}) collective-permute-start(bf16[64,256]{1,0:T(8,128)(2,1)S(1)} %get-tuple-element.195), channel_id=1, source_target_pairs={{0,7},{1,0},{2,1},{3,2},{4,3},{5,4},{6,5},{7,6},{8,15},{9,8},{10,9... | collective-permute-start | bytes 98312 | tf_op jit(solution)/shard_map/ppermute | solution.py:740
  139.2 6.9 %copy.32 = bf16[128,128,128]{2,0,1:T(8,128)(2,1)} copy(bf16[128,128,128]{2,1,0:T(8,128)(2,1)} %copy-done.4) | data formatting | bytes 8388608 | tf_op jit(solution)/shard_map/optimization_barrier | solution.py:969
  146.2 1.5 copy-done.32
  147.7 6.8 %shard_map.142 = bf16[128,64,128]{2,1,0:T(8,128)(2,1)S(1)} custom-call(s32[1,2]{1,0:T(1,128)S(1)} %copy-done.30, bf16[128,64,128]{2,1,0:T(8,128)(2,1)S(1)} %copy-done.32, f32[2,64,256]{2,1,0:T(8,128)S(1)} %get-tuple-element.202.refs_2_, f32[64,128]{1,0:T(8,128)S(1)} %get-tuple-element.203.refs_3_, f32[64,128]{1,0:T(8,128)S(1)} %get-tuple-element.204.refs_4_, ...), custom_call_target="tpu_custom_call" | custom-call | flops 3216856832 | tf_op jit(solution)/shard_map/pallas_call | solution.py:445
  154.5 2.7 %copy.26 = bf16[64,128,128]{2,1,0:T(8,128)(2,1)} copy(bf16[64,128,128]{2,0,1:T(8,128)(2,1)S(1)} %bitcast.28) | data formatting | bytes 4194304
  (129 shorter events, 12.5 us)
Async XLA Ops:
  6.4 7.5 %copy-start.16 = (s32[128,4]{0,1:T(4,128)S(1)}, s32[128,4]{0,1:T(4,128)}, u32[]{:S(2)}) copy-start(s32[128,4]{0,1:T(4,128)} %param.13) | copy-start | bytes 6148
  6.4 41.7 %all-to-all-start = ((bf16[32,8,2176]{2,1,0:T(8,128)(2,1)}), bf16[32,8,2176]{2,1,0:T(8,128)(2,1)}, u32[]{:S(2)}, u32[]{:S(2)}) async-start(bf16[32,8,2176]{2,1,0:T(8,128)(2,1)} %bitcast.7), calls=%async_computation | async-start | bytes 2228224 | tf_op jit(solution)/shard_map/all_to_all | solution.py:864
  14.7 5.1 %copy-start.8 = (bf16[64,128,128]{2,1,0:T(8,128)(2,1)S(1)}, bf16[64,128,128]{2,1,0:T(8,128)(2,1)}, u32[]{:S(2)}) copy-start(bf16[64,128,128]{2,1,0:T(8,128)(2,1)} %surface.2) | copy-start | bytes 6291460
  27.1 12.9 %collective-permute-start = (bf16[192,128]{1,0:T(8,128)(2,1)S(1)}, bf16[192,128]{1,0:T(8,128)(2,1)S(1)}, u32[]{:S(2)}, u32[]{:S(2)}) collective-permute-start(bf16[192,128]{1,0:T(8,128)(2,1)S(1)} %get-tuple-element.104), channel_id=1, source_target_pairs={{0,8},{8,16},{16,24},{24,0},{1,9},{9,17},{17,25},{25,1},{2,10},{10... | collective-permute-start | bytes 147464 | tf_op jit(solution)/shard_map/ppermute | solution.py:740
  28.9 11.1 %collective-permute-start.2 = (bf16[64,128]{1,0:T(8,128)(2,1)S(1)}, bf16[64,128]{1,0:T(8,128)(2,1)S(1)}, u32[]{:S(2)}, u32[]{:S(2)}) collective-permute-start(bf16[64,128]{1,0:T(8,128)(2,1)S(1)} %slice.3), channel_id=1, source_target_pairs={{24,31},{25,30},{26,29},{27,28},{28,27},{29,26},{30,25},{31,24}} | collective-permute-start | bytes 49160 | tf_op jit(solution)/shard_map/ppermute | solution.py:763
  29.6 10.5 %collective-permute-start.1 = (bf16[192,128]{1,0:T(8,128)(2,1)S(1)}, bf16[192,128]{1,0:T(8,128)(2,1)S(1)}, u32[]{:S(2)}, u32[]{:S(2)}) collective-permute-start(bf16[192,128]{1,0:T(8,128)(2,1)S(1)} %get-tuple-element.105), channel_id=1, source_target_pairs={{0,24},{8,0},{16,8},{24,16},{1,25},{9,1},{17,9},{25,17},{2,26},{10... | collective-permute-start | bytes 147464 | tf_op jit(solution)/shard_map/ppermute | solution.py:740
  35.2 2.2 %copy-start.3 = (bf16[128,128,128]{2,1,0:T(8,128)(2,1)S(1)}, bf16[128,128,128]{2,1,0:T(8,128)(2,1)}, u32[]{:S(2)}) copy-start(bf16[128,128,128]{2,1,0:T(8,128)(2,1)} %surface.3) | copy-start | bytes 12582916
  37.3 39.4 %copy-start.28 = (s32[1,2]{1,0:T(1,128)}, s32[1,2]{1,0:T(1,128)S(1)}, u32[]{:S(2)}) copy-start(s32[1,2]{1,0:T(1,128)S(1)} %add_bitcast_fusion.place.refs_0_) | copy-start | bytes 28
  40.0 5.0 %copy-start.17 = (bf16[9,128,128]{2,1,0:T(8,128)(2,1)S(1)}, bf16[9,128,128]{2,1,0:T(8,128)(2,1)}, u32[]{:S(2)}) copy-start(bf16[9,128,128]{2,1,0:T(8,128)(2,1)} %refs_1_.1) | copy-start | bytes 884740
  40.0 5.0 %copy-start.18 = (bf16[9,64,80]{2,1,0:T(8,128)(2,1)S(1)}, bf16[9,64,80]{2,1,0:T(8,128)(2,1)}, u32[]{:S(2)}) copy-start(bf16[9,64,80]{2,1,0:T(8,128)(2,1)} %refs_2_.1) | copy-start | bytes 276484
  40.0 5.0 %copy-start.19 = (bf16[9,64,64]{2,1,0:T(8,128)(2,1)S(1)}, bf16[9,64,64]{2,1,0:T(8,128)(2,1)}, u32[]{:S(2)}) copy-start(bf16[9,64,64]{2,1,0:T(8,128)(2,1)} %refs_3_.1) | copy-start | bytes 221188
  41.4 10.0 %copy-start.39 = (bf16[192,128]{1,0:T(8,128)(2,1)}, bf16[192,128]{1,0:T(8,128)(2,1)S(1)}, u32[]{:S(2)}) copy-start(bf16[192,128]{1,0:T(8,128)(2,1)S(1)} %get-tuple-element.135.refs_0_) | copy-start | bytes 147460
  41.4 6.0 %collective-permute-start.3 = (bf16[192,256]{1,0:T(8,128)(2,1)S(1)}, bf16[192,256]{1,0:T(8,128)(2,1)S(1)}, u32[]{:S(2)}, u32[]{:S(2)}) collective-permute-start(bf16[192,256]{1,0:T(8,128)(2,1)S(1)} %get-tuple-element.110), channel_id=1, source_target_pairs={{0,1},{1,2},{2,3},{3,4},{4,5},{5,6},{6,7},{7,0},{8,9},{9,10},{10,1... | collective-permute-start | bytes 294920 | tf_op jit(solution)/shard_map/ppermute | solution.py:740
  41.8 5.6 %collective-permute-start.4 = (bf16[192,256]{1,0:T(8,128)(2,1)S(1)}, bf16[192,256]{1,0:T(8,128)(2,1)S(1)}, u32[]{:S(2)}, u32[]{:S(2)}) collective-permute-start(bf16[192,256]{1,0:T(8,128)(2,1)S(1)} %get-tuple-element.111), channel_id=1, source_target_pairs={{0,7},{1,0},{2,1},{3,2},{4,3},{5,4},{6,5},{7,6},{8,15},{9,8},{10,9... | collective-permute-start | bytes 294920 | tf_op jit(solution)/shard_map/ppermute | solution.py:740
  47.4 4.0 %copy-start.20 = (bf16[192,256]{1,0:T(8,128)(2,1)}, bf16[192,256]{1,0:T(8,128)(2,1)S(1)}, u32[]{:S(2)}) copy-start(bf16[192,256]{1,0:T(8,128)(2,1)S(1)} %collective-permute-done.3.refs_2_) | copy-start | bytes 294916
  51.4 32.1 %all-to-all-start.1 = ((bf16[32,8,2048]{2,1,0:T(8,128)(2,1)}), bf16[32,8,2048]{2,1,0:T(8,128)(2,1)}, u32[]{:S(2)}, u32[]{:S(2)}) async-start(bf16[32,8,2048]{2,1,0:T(8,128)(2,1)} %bitcast.12), calls=%async_computation.1 | async-start | bytes 2097152 | tf_op jit(solution)/shard_map/all_to_all | solution.py:925
  56.1 7.0 %copy-start.1 = (bf16[128,128,128]{2,0,1:T(8,128)(2,1)S(1)}, bf16[128,128,128]{2,0,1:T(8,128)(2,1)}, u32[]{:S(2)}) copy-start(bf16[128,128,128]{2,0,1:T(8,128)(2,1)} %copy-done) | copy-start | bytes 12582916
  60.0 16.7 %collective-permute-start.7 = (bf16[16,128]{1,0:T(8,128)(2,1)S(1)}, bf16[16,128]{1,0:T(8,128)(2,1)S(1)}, u32[]{:S(2)}, u32[]{:S(2)}) collective-permute-start(bf16[16,128]{1,0:T(8,128)(2,1)S(1)} %get-tuple-element.124), channel_id=1, source_target_pairs={{0,8},{8,16},{16,24},{24,0},{1,9},{9,17},{17,25},{25,1},{2,10},{10... | collective-permute-start | bytes 12296 | tf_op jit(solution)/shard_map/ppermute | solution.py:740
  61.9 14.9 %collective-permute-start.8 = (bf16[16,128]{1,0:T(8,128)(2,1)S(1)}, bf16[16,128]{1,0:T(8,128)(2,1)S(1)}, u32[]{:S(2)}, u32[]{:S(2)}) collective-permute-start(bf16[16,128]{1,0:T(8,128)(2,1)S(1)} %get-tuple-element.125), channel_id=1, source_target_pairs={{0,24},{8,0},{16,8},{24,16},{1,25},{9,1},{17,9},{25,17},{2,26},{10... | collective-permute-start | bytes 12296 | tf_op jit(solution)/shard_map/ppermute | solution.py:740
  79.2 9.6 %collective-permute-start.10 = (bf16[16,256]{1,0:T(8,128)(2,1)}, bf16[16,256]{1,0:T(8,128)(2,1)S(1)}, u32[]{:S(2)}, u32[]{:S(2)}) collective-permute-start(bf16[16,256]{1,0:T(8,128)(2,1)} %get-tuple-element.146), channel_id=1, source_target_pairs={{0,7},{1,0},{2,1},{3,2},{4,3},{5,4},{6,5},{7,6},{8,15},{9,8},{10,9... | collective-permute-start | bytes 24584 | tf_op jit(solution)/shard_map/ppermute | solution.py:740
  82.0 6.8 %collective-permute-start.9 = (bf16[16,256]{1,0:T(8,128)(2,1)}, bf16[16,256]{1,0:T(8,128)(2,1)S(1)}, u32[]{:S(2)}, u32[]{:S(2)}) collective-permute-start(bf16[16,256]{1,0:T(8,128)(2,1)} %get-tuple-element.145), channel_id=1, source_target_pairs={{0,1},{1,2},{2,3},{3,4},{4,5},{5,6},{6,7},{7,0},{8,9},{9,10},{10,1... | collective-permute-start | bytes 24584 | tf_op jit(solution)/shard_map/ppermute | solution.py:740
  84.8 7.9 %copy-start.21 = (bf16[192,256]{1,0:T(8,128)(2,1)S(1)}, bf16[192,256]{1,0:T(8,128)(2,1)}, u32[]{:S(2)}) copy-start(bf16[192,256]{1,0:T(8,128)(2,1)} %copy-done.20) | copy-start | bytes 294916
  84.8 7.9 %copy-start.23 = (bf16[192,256]{1,0:T(8,128)(2,1)S(1)}, bf16[192,256]{1,0:T(8,128)(2,1)}, u32[]{:S(2)}) copy-start(bf16[192,256]{1,0:T(8,128)(2,1)} %copy-done.22) | copy-start | bytes 294916
  84.8 7.9 %copy-start.40 = (bf16[192,128]{1,0:T(8,128)(2,1)S(1)}, bf16[192,128]{1,0:T(8,128)(2,1)}, u32[]{:S(2)}) copy-start(bf16[192,128]{1,0:T(8,128)(2,1)} %copy-done.39) | copy-start | bytes 147460
  84.8 7.9 %copy-start.42 = (bf16[192,128]{1,0:T(8,128)(2,1)S(1)}, bf16[192,128]{1,0:T(8,128)(2,1)}, u32[]{:S(2)}) copy-start(bf16[192,128]{1,0:T(8,128)(2,1)} %copy-done.41) | copy-start | bytes 147460
  84.8 7.9 %copy-start.44 = (bf16[16,128]{1,0:T(8,128)(2,1)S(1)}, bf16[16,128]{1,0:T(8,128)(2,1)}, u32[]{:S(2)}) copy-start(bf16[16,128]{1,0:T(8,128)(2,1)} %copy-done.43) | copy-start | bytes 12292
  84.8 7.9 %copy-start.46 = (bf16[16,128]{1,0:T(8,128)(2,1)S(1)}, bf16[16,128]{1,0:T(8,128)(2,1)}, u32[]{:S(2)}) copy-start(bf16[16,128]{1,0:T(8,128)(2,1)} %copy-done.45) | copy-start | bytes 12292
  84.9 8.3 %copy-start.2 = (bf16[128,128,128]{2,0,1:T(8,128)(2,1)S(1)}, bf16[128,128,128]{2,0,1:T(8,128)(2,1)}, u32[]{:S(2)}) copy-start(bf16[128,128,128]{2,0,1:T(8,128)(2,1)} %copy-done) | copy-start | bytes 12582916
  84.9 8.3 %copy-start.6 = (bf16[128,128,128]{2,1,0:T(8,128)(2,1)S(1)}, bf16[128,128,128]{2,1,0:T(8,128)(2,1)}, u32[]{:S(2)}) copy-start(bf16[128,128,128]{2,1,0:T(8,128)(2,1)} %copy-done.5) | copy-start | bytes 12582916
  88.7 4.5 %copy-start.12 = (f32[128,128]{1,0:T(8,128)S(1)}, f32[128,128]{1,0:T(8,128)}, u32[]{:S(2)}) copy-start(f32[128,128]{1,0:T(8,128)} %copy-done.11) | copy-start | bytes 196612
  88.7 4.5 %copy-start.14 = (f32[128,128]{1,0:T(8,128)S(1)}, f32[128,128]{1,0:T(8,128)}, u32[]{:S(2)}) copy-start(f32[128,128]{1,0:T(8,128)} %copy-done.13) | copy-start | bytes 196612
  88.7 8.8 %collective-permute-start.5 = (bf16[16,128]{1,0:T(8,128)(2,1)S(1)}, bf16[16,128]{1,0:T(8,128)(2,1)S(1)}, u32[]{:S(2)}, u32[]{:S(2)}) collective-permute-start(bf16[16,128]{1,0:T(8,128)(2,1)S(1)} %get-tuple-element.121), channel_id=1, source_target_pairs={{8,16},{9,17},{10,18},{11,19},{12,20},{13,21},{14,22},{15,23},{16,... | collective-permute-start | bytes 12296 | tf_op jit(solution)/shard_map/ppermute | solution.py:760
  89.4 8.1 %collective-permute-start.6 = (bf16[16,128]{1,0:T(8,128)(2,1)S(1)}, bf16[16,128]{1,0:T(8,128)(2,1)S(1)}, u32[]{:S(2)}, u32[]{:S(2)}) collective-permute-start(bf16[16,128]{1,0:T(8,128)(2,1)S(1)} %get-tuple-element.122), channel_id=1, source_target_pairs={{0,8},{1,9},{2,10},{3,11},{4,12},{5,13},{6,14},{7,15},{8,0},{9,1},... | collective-permute-start | bytes 12296 | tf_op jit(solution)/shard_map/ppermute | solution.py:760
  98.3 6.5 %collective-permute-start.13 = (bf16[16,256]{1,0:T(8,128)(2,1)S(1)}, bf16[16,256]{1,0:T(8,128)(2,1)S(1)}, u32[]{:S(2)}, u32[]{:S(2)}) collective-permute-start(bf16[16,256]{1,0:T(8,128)(2,1)S(1)} %get-tuple-element.170), channel_id=1, source_target_pairs={{0,1},{1,2},{2,3},{3,4},{4,5},{5,6},{6,7},{7,0},{8,9},{9,10},{10,1... | collective-permute-start | bytes 24584 | tf_op jit(solution)/shard_map/ppermute | solution.py:740
  98.3 6.5 %collective-permute-start.14 = (bf16[16,256]{1,0:T(8,128)(2,1)S(1)}, bf16[16,256]{1,0:T(8,128)(2,1)S(1)}, u32[]{:S(2)}, u32[]{:S(2)}) collective-permute-start(bf16[16,256]{1,0:T(8,128)(2,1)S(1)} %get-tuple-element.171), channel_id=1, source_target_pairs={{0,7},{1,0},{2,1},{3,2},{4,3},{5,4},{6,5},{7,6},{8,15},{9,8},{10,9... | collective-permute-start | bytes 24584 | tf_op jit(solution)/shard_map/ppermute | solution.py:740
  101.8 4.8 %collective-permute-start.11 = (bf16[128,128]{1,0:T(8,128)(2,1)S(1)}, bf16[128,128]{1,0:T(8,128)(2,1)S(1)}, u32[]{:S(2)}, u32[]{:S(2)}) collective-permute-start(bf16[128,128]{1,0:T(8,128)(2,1)S(1)} %get-tuple-element.158), channel_id=1, source_target_pairs={{0,8},{8,16},{16,24},{24,0},{1,9},{9,17},{17,25},{25,1},{2,10},{10... | collective-permute-start | bytes 98312 | tf_op jit(solution)/shard_map/ppermute | solution.py:740
  101.9 5.8 %collective-permute-start.12 = (bf16[128,128]{1,0:T(8,128)(2,1)S(1)}, bf16[128,128]{1,0:T(8,128)(2,1)S(1)}, u32[]{:S(2)}, u32[]{:S(2)}) collective-permute-start(bf16[128,128]{1,0:T(8,128)(2,1)S(1)} %get-tuple-element.159), channel_id=1, source_target_pairs={{0,24},{8,0},{16,8},{24,16},{1,25},{9,1},{17,9},{25,17},{2,26},{10... | collective-permute-start | bytes 98312 | tf_op jit(solution)/shard_map/ppermute | solution.py:740
  104.9 4.0 %copy-start.38 = (bf16[192,256]{1,0:T(8,128)(2,1)S(1)}, bf16[192,256]{1,0:T(8,128)(2,1)}, u32[]{:S(2)}) copy-start(bf16[192,256]{1,0:T(8,128)(2,1)} %copy-done.37) | copy-start | bytes 294916
  108.3 12.8 %collective-permute-start.18 = (bf16[128,256]{1,0:T(8,128)(2,1)S(1)}, bf16[128,256]{1,0:T(8,128)(2,1)S(1)}, u32[]{:S(2)}, u32[]{:S(2)}) collective-permute-start(bf16[128,256]{1,0:T(8,128)(2,1)S(1)} %get-tuple-element.162), channel_id=1, source_target_pairs={{0,7},{1,0},{2,1},{3,2},{4,3},{5,4},{6,5},{7,6},{8,15},{9,8},{10,9... | collective-permute-start | bytes 196616 | tf_op jit(solution)/shard_map/ppermute | solution.py:740
  108.4 12.7 %collective-permute-start.17 = (bf16[128,256]{1,0:T(8,128)(2,1)S(1)}, bf16[128,256]{1,0:T(8,128)(2,1)S(1)}, u32[]{:S(2)}, u32[]{:S(2)}) collective-permute-start(bf16[128,256]{1,0:T(8,128)(2,1)S(1)} %get-tuple-element.183), channel_id=1, source_target_pairs={{0,1},{1,2},{2,3},{3,4},{4,5},{5,6},{6,7},{7,0},{8,9},{9,10},{10,1... | collective-permute-start | bytes 196616 | tf_op jit(solution)/shard_map/ppermute | solution.py:740
  116.3 5.2 %copy-start.31 = (bf16[128,64,128]{2,1,0:T(8,128)(2,1)}, bf16[128,64,128]{2,1,0:T(8,128)(2,1)S(1)}, u32[]{:S(2)}) copy-start(bf16[128,64,128]{2,1,0:T(8,128)(2,1)S(1)} %get-tuple-element.179.refs_1_) | copy-start | bytes 6291460
  116.3 5.2 %copy-start.34 = (bf16[384,384]{1,0:T(8,128)(2,1)S(1)}, bf16[384,384]{1,0:T(8,128)(2,1)}, u32[]{:S(2)}) copy-start(bf16[384,384]{1,0:T(8,128)(2,1)} %copy-done.33) | copy-start | bytes 884740
  116.4 18.3 %collective-permute-start.15 = (bf16[64,128]{1,0:T(8,128)(2,1)S(1)}, bf16[64,128]{1,0:T(8,128)(2,1)S(1)}, u32[]{:S(2)}, u32[]{:S(2)}) collective-permute-start(bf16[64,128]{1,0:T(8,128)(2,1)S(1)} %get-tuple-element.176), channel_id=1, source_target_pairs={{8,16},{9,17},{10,18},{11,19},{12,20},{13,21},{14,22},{15,23},{16,... | collective-permute-start | bytes 49160 | tf_op jit(solution)/shard_map/ppermute | solution.py:760
  117.2 17.6 %collective-permute-start.16 = (bf16[64,128]{1,0:T(8,128)(2,1)S(1)}, bf16[64,128]{1,0:T(8,128)(2,1)S(1)}, u32[]{:S(2)}, u32[]{:S(2)}) collective-permute-start(bf16[64,128]{1,0:T(8,128)(2,1)S(1)} %get-tuple-element.177), channel_id=1, source_target_pairs={{0,8},{1,9},{2,10},{3,11},{4,12},{5,13},{6,14},{7,15},{8,0},{9,1},... | collective-permute-start | bytes 49160 | tf_op jit(solution)/shard_map/ppermute | solution.py:760
  121.5 13.2 %copy-start.30 = (s32[1,2]{1,0:T(1,128)S(1)}, s32[1,2]{1,0:T(1,128)}, u32[]{:S(2)}) copy-start(s32[1,2]{1,0:T(1,128)} %copy-done.28) | copy-start | bytes 28
  134.7 4.4 %copy-start.48 = (bf16[128,4]{0,1:T(4,128)(2,1)S(1)}, bf16[128,4]{0,1:T(4,128)(2,1)}, u32[]{:S(2)}) copy-start(bf16[128,4]{0,1:T(4,128)(2,1)} %copy-done.47) | copy-start | bytes 3076
  135.5 10.6 %collective-permute-start.19 = (bf16[64,256]{1,0:T(8,128)(2,1)S(1)}, bf16[64,256]{1,0:T(8,128)(2,1)S(1)}, u32[]{:S(2)}, u32[]{:S(2)}) collective-permute-start(bf16[64,256]{1,0:T(8,128)(2,1)S(1)} %get-tuple-element.194), channel_id=1, source_target_pairs={{0,1},{1,2},{2,3},{3,4},{4,5},{5,6},{6,7},{7,0},{8,9},{9,10},{10,1... | collective-permute-start | bytes 98312 | tf_op jit(solution)/shard_map/ppermute | solution.py:740
  135.6 10.6 %collective-permute-start.20 = (bf16[64,256]{1,0:T(8,128)(2,1)S(1)}, bf16[64,256]{1,0:T(8,128)(2,1)S(1)}, u32[]{:S(2)}, u32[]{:S(2)}) collective-permute-start(bf16[64,256]{1,0:T(8,128)(2,1)S(1)} %get-tuple-element.195), channel_id=1, source_target_pairs={{0,7},{1,0},{2,1},{3,2},{4,3},{5,4},{6,5},{7,6},{8,15},{9,8},{10,9... | collective-permute-start | bytes 98312 | tf_op jit(solution)/shard_map/ppermute | solution.py:740
  (24 other events, 23.0 us)
